TPU v7x, 32 devices: a whole 2x2x4 slice. The times are simulated.
32 devices in a mesh: fsdp: 8 (over z, x), ctx: 2 (over core), tp: 2 (over y).
Axes of the slice: x: 2, y: 2, z: 4, core: 2. Of those that a mesh axis runs over, the one named last changes fastest.
Arguments:
- hidden_in: bfloat16 [2048, 2048], P(('fsdp', 'ctx')), may hold values from -6 to 6
- segment_ids: int32 [2048], P(('fsdp', 'ctx')), may hold values from 0 to 15, never falling along the last dimension, each value on 1 to 256 neighbouring positions
- routes: int32 [2048, 8], P(('fsdp', 'ctx')), may hold values from 0 to 31, all different within a row; in each aligned block of 128 rows (0 to 127, 128 to 255, ...) at most 64 rows name the same one
- attn_gain: bfloat16 [2048], P('fsdp'), may hold values from 0.5 to 1.5
- qk_gains: bfloat16 [256], P('fsdp'), may hold values from 0.6 to 1.6
- w_query: bfloat16 [2048, 4096], P('fsdp', 'tp')
- key_projection: bfloat16 [2048, 512], P('fsdp', 'tp')
- value_projection: bfloat16 [2048, 512], P('fsdp', 'tp'), may hold values from -0.125 to 0.125
- w_out: bfloat16 [4096, 2048], P('tp', 'fsdp'), may hold values from -0.5 to 0.5
- ffn_gain: bfloat16 [2048], P('fsdp'), may hold values from 0.5 to 1.5
- w_router: bfloat16 [2048, 32], P('fsdp')
- w_gate: bfloat16 [32, 2048, 768], P(('fsdp', 'ctx'), None, 'tp'), may hold values from -0.125 to 0.125
- w_up: bfloat16 [32, 2048, 768], P(('fsdp', 'ctx'), None, 'tp'), may hold values from -0.125 to 0.125
- w_down: bfloat16 [32, 768, 2048], P(('fsdp', 'ctx'), 'tp'), may hold values from -0.625 to 0.625
- grad_out: bfloat16 [2048, 2048], P(('fsdp', 'ctx')), may hold values from -6 to 6
Outputs:
- block_out: bfloat16 [2048, 2048], P(('fsdp', 'ctx'))
- grad_in: float32 [2048, 2048], P(('fsdp', 'ctx'))
- grad_attn_gain: float32 [2048], P('fsdp')
- grad_qk_gains: float32 [256], P('fsdp')
- grad_query: float32 [2048, 4096], P('fsdp', 'tp')
- grad_key: float32 [2048, 512], P('fsdp', 'tp')
- grad_value: float32 [2048, 512], P('fsdp', 'tp')
- grad_out_proj: float32 [4096, 2048], P('tp', 'fsdp')
- grad_ffn_gain: float32 [2048], P('fsdp')
- grad_router: float32 [2048, 32], P('fsdp')
- grad_gate: float32 [32, 2048, 768], P(('fsdp', 'ctx'), None, 'tp')
- grad_up: float32 [32, 2048, 768], P(('fsdp', 'ctx'), None, 'tp')
- grad_down: float32 [32, 768, 2048], P(('fsdp', 'ctx'), 'tp')
Inputs may be any that keep to these rules, and one draw needn't show every extreme that they name: `routes`: each row names 8 different experts. Within the 128 rows of one device no expert is named by more than 64 rows, and in some device one expert is named by exactly 64 rows. `segment_ids`: segment ids never fall along the tokens; a segment holds 1 to 256 tokens, and one holds exactly 256.
All inputs are finite; a program needn't handle non-finite values.
Results may differ from a plain program's by a relative error of at most 0.028.
Values may be sent and summed in bfloat16 or wider, within the bound.
A program may use at most 256 MiB of HBM per device.

v0:
```python
import jax
import jax.numpy as jnp
from jax import lax
from jax.sharding import PartitionSpec as P

QUERY_HEADS = 32
KEY_VALUE_HEADS = 4
HEAD_SIZE = 128
TOPK = 8


eps_norm = 1e-06
rope_base = 1000000.0


def norm_forward(values, gain_row):
    inverse = lax.rsqrt(jnp.mean(values * values, axis=-1, keepdims=True) + eps_norm)
    normed = values * inverse
    return (normed * gain_row, normed, inverse)


def rms_norm_gradient(grad_scaled, normed, inverse, gain_row):
    grad_normed = grad_scaled * gain_row
    inner_mean = jnp.mean(grad_normed * normed, axis=-1, keepdims=True)
    return inverse * (grad_normed - normed * inner_mean)


def rope_tables(positions):
    half_dim = HEAD_SIZE // 2
    frequencies = rope_base ** (-(jnp.arange(half_dim, dtype=jnp.float32) * 2.0) / HEAD_SIZE)
    angles = positions.astype(jnp.float32)[:, None] * frequencies[None, :]
    return (jnp.cos(angles)[:, None, :], jnp.sin(angles)[:, None, :])


def rotate(values, cosine_table, sine_values):
    half_dim = values.shape[-1] // 2
    first_half = values[..., :half_dim]
    second_half = values[..., half_dim:]
    return jnp.concatenate(
        [
            first_half * cosine_table - second_half * sine_values,
            second_half * cosine_table + first_half * sine_values,
        ],
        axis=-1,
    )


def inverse_rotation(grad_in_rot, cosine_table, sine_values):
    half_dim = grad_in_rot.shape[-1] // 2
    first_half = grad_in_rot[..., :half_dim]
    second_half = grad_in_rot[..., half_dim:]
    return jnp.concatenate(
        [
            first_half * cosine_table + second_half * sine_values,
            second_half * cosine_table - first_half * sine_values,
        ],
        axis=-1,
    )


def masked_scores(query_rotated, key_rotated, allowed):
    scores = jnp.einsum(
        "qkgd,skd->kgqs", query_rotated, key_rotated, preferred_element_type=jnp.float32
    ) * HEAD_SIZE ** (-0.5)
    return jnp.where(allowed[None, None], scores, -jnp.inf)


def slot_index(route_rows, experts, capacity, devices, per_device):
    flat_routes = route_rows.reshape(-1)
    onehot = (flat_routes[:, None] == jnp.arange(experts, dtype=jnp.int32)[None, :]).astype(
        jnp.int32
    )
    rank_rows = jnp.cumsum(onehot, axis=0) - onehot
    slot_rows = jnp.sum(rank_rows * onehot, axis=1)
    local_expert = flat_routes % per_device
    device_of = flat_routes // per_device
    return (local_expert * devices + device_of) * capacity + slot_rows


def collect_weights(shards):
    return (
        lax.all_gather(shards[0], "fsdp", axis=0, tiled=True),
        lax.all_gather(shards[1], "fsdp", axis=0, tiled=True),
        lax.all_gather(shards[2], "fsdp", axis=0, tiled=True),
        lax.all_gather(shards[3], "fsdp", axis=0, tiled=True),
        lax.all_gather(shards[4], "fsdp", axis=0, tiled=True),
        lax.all_gather(shards[5], "fsdp", axis=0, tiled=True),
        lax.all_gather(shards[6], "fsdp", axis=0, tiled=True),
        lax.all_gather(shards[7], "fsdp", axis=1, tiled=True),
    )


def reduce_grads(local_grads):
    pieces = (
        lax.psum_scatter(
            local_grads[0].astype(jnp.bfloat16), "fsdp", scatter_dimension=0, tiled=True
        ).astype(jnp.float32),
        lax.psum_scatter(
            local_grads[1].astype(jnp.bfloat16), "fsdp", scatter_dimension=0, tiled=True
        ).astype(jnp.float32),
        lax.psum_scatter(
            local_grads[2].astype(jnp.bfloat16), "fsdp", scatter_dimension=0, tiled=True
        ).astype(jnp.float32),
        lax.psum_scatter(
            local_grads[3].astype(jnp.bfloat16), "fsdp", scatter_dimension=0, tiled=True
        ).astype(jnp.float32),
        lax.psum_scatter(
            local_grads[4].astype(jnp.bfloat16), "fsdp", scatter_dimension=0, tiled=True
        ).astype(jnp.float32),
        lax.psum_scatter(
            local_grads[5].astype(jnp.bfloat16), "fsdp", scatter_dimension=0, tiled=True
        ).astype(jnp.float32),
        lax.psum_scatter(
            local_grads[6].astype(jnp.bfloat16), "fsdp", scatter_dimension=0, tiled=True
        ).astype(jnp.float32),
        lax.psum_scatter(
            local_grads[7].astype(jnp.bfloat16), "fsdp", scatter_dimension=1, tiled=True
        ).astype(jnp.float32),
    )
    return (
        lax.psum(pieces[0].astype(jnp.bfloat16), "ctx").astype(jnp.float32),
        lax.psum(pieces[1].astype(jnp.bfloat16), "ctx").astype(jnp.float32),
        lax.psum(pieces[2].astype(jnp.bfloat16), "ctx").astype(jnp.float32),
        lax.psum(pieces[3].astype(jnp.bfloat16), "ctx").astype(jnp.float32),
        lax.psum(pieces[4].astype(jnp.bfloat16), "ctx").astype(jnp.float32),
        lax.psum(pieces[5].astype(jnp.bfloat16), "ctx").astype(jnp.float32),
        lax.psum(pieces[6].astype(jnp.bfloat16), "ctx").astype(jnp.float32),
        lax.psum(pieces[7].astype(jnp.bfloat16), "ctx").astype(jnp.float32),
    )


def on_device(
    hidden_in,
    segment_ids,
    routes,
    attn_gain,
    qk_gains,
    w_query,
    key_projection,
    value_projection,
    w_out,
    ffn_gain,
    w_router,
    w_gate,
    w_up,
    w_down,
    grad_out,
):
    tokens_dev = hidden_in.shape[0]
    width_dim = hidden_in.shape[1]
    devices = lax.axis_size(("fsdp", "ctx"))
    local_experts = w_gate.shape[0]
    experts = local_experts * devices
    capacity = max(2, 2 * tokens_dev * TOPK // experts)
    hidden_local = w_gate.shape[2]
    query_group_width = QUERY_HEADS // KEY_VALUE_HEADS
    shards = (
        attn_gain,
        ffn_gain,
        qk_gains,
        w_query,
        key_projection,
        value_projection,
        w_router,
        w_out,
    )
    gathered = collect_weights(shards)
    (
        gain_attn,
        gain_ffn,
        gain_qk,
        query_weight,
        key_weight,
        value_weight,
        router_weight,
        out_weight,
    ) = gathered
    kv_local = key_weight.shape[1] // HEAD_SIZE
    head_local = query_weight.shape[1] // HEAD_SIZE
    resid = hidden_in.astype(jnp.float32)
    scaled_one, normed_one, inverse_one = norm_forward(resid, gain_attn.astype(jnp.float32))
    hidden_first = scaled_one.astype(jnp.bfloat16)
    query_raw = jnp.dot(hidden_first, query_weight, preferred_element_type=jnp.float32).reshape(
        tokens_dev, head_local, HEAD_SIZE
    )
    key_projected = jnp.dot(hidden_first, key_weight, preferred_element_type=jnp.float32).reshape(
        tokens_dev, kv_local, HEAD_SIZE
    )
    value_matrix_rows = (
        jnp.dot(hidden_first, value_weight, preferred_element_type=jnp.float32)
        .astype(jnp.bfloat16)
        .reshape(tokens_dev, kv_local, HEAD_SIZE)
    )
    query_normed, query_hat, query_inverse = norm_forward(
        query_raw, gain_qk[:HEAD_SIZE].astype(jnp.float32)
    )
    key_normed, key_unit_rows, key_inverse_norm = norm_forward(
        key_projected, gain_qk[HEAD_SIZE:].astype(jnp.float32)
    )
    offset = lax.axis_index("ctx") * tokens_dev
    own_positions = offset + jnp.arange(tokens_dev, dtype=jnp.int32)
    cosine_table, sine_values = rope_tables(own_positions)
    query_rotated = (
        rotate(query_normed, cosine_table, sine_values)
        .astype(jnp.bfloat16)
        .reshape(tokens_dev, kv_local, query_group_width, HEAD_SIZE)
    )
    key_rotated = rotate(key_normed, cosine_table, sine_values).astype(jnp.bfloat16)
    own_segments = segment_ids.astype(jnp.bfloat16)
    key_all, value_all, segment_all = (
        lax.all_gather(key_rotated, "ctx", axis=0, tiled=True),
        lax.all_gather(value_matrix_rows, "ctx", axis=0, tiled=True),
        lax.all_gather(own_segments, "ctx", axis=0, tiled=True),
    )
    key_positions = jnp.arange(key_all.shape[0], dtype=jnp.int32)
    allowed = (key_positions[None, :] <= own_positions[:, None]) & (
        segment_all[None, :] == own_segments[:, None]
    )
    scores = masked_scores(query_rotated, key_all, allowed)
    top_score = jnp.max(scores, axis=-1, keepdims=True)
    log_total = top_score + jnp.log(jnp.sum(jnp.exp(scores - top_score), axis=-1, keepdims=True))
    weights_att = jnp.exp(scores - log_total).astype(jnp.bfloat16)
    attended = jnp.einsum(
        "kgqs,skd->qkgd", weights_att, value_all, preferred_element_type=jnp.float32
    )
    attended = attended.astype(jnp.bfloat16).reshape(tokens_dev, head_local * HEAD_SIZE)
    out_partial = jnp.dot(attended, out_weight, preferred_element_type=jnp.float32)
    resid_mid = resid + lax.psum(out_partial.astype(jnp.bfloat16), "tp").astype(jnp.float32)
    scaled_two, normed_two, inverse_two = norm_forward(resid_mid, gain_ffn.astype(jnp.float32))
    hidden_two = scaled_two.astype(jnp.bfloat16)
    logits = jnp.dot(hidden_two, router_weight, preferred_element_type=jnp.float32)
    chosen = jnp.take_along_axis(logits, routes, axis=1)
    raised = jnp.exp(chosen - jnp.max(chosen, axis=1, keepdims=True))
    route_probs = raised / jnp.sum(raised, axis=1, keepdims=True)
    assign_count = tokens_dev * TOPK
    targets = slot_index(routes, experts, capacity, devices, local_experts)
    owners = (
        jnp.full((experts * capacity,), assign_count, jnp.int32)
        .at[targets]
        .set(jnp.arange(assign_count, dtype=jnp.int32))
    )
    padded_rows = jnp.concatenate([hidden_two, jnp.zeros((1, width_dim), jnp.bfloat16)], axis=0)
    send_rows = padded_rows[owners // TOPK].reshape(local_experts, devices, capacity, width_dim)
    received = lax.all_to_all(send_rows, ("fsdp", "ctx"), split_axis=1, concat_axis=1, tiled=True)
    slot_count = received.shape[2]
    row_block = received.reshape(local_experts, devices * slot_count, width_dim)
    gate_pre = jnp.einsum("jrd,jdf->jrf", row_block, w_gate, preferred_element_type=jnp.float32)
    up_pre = jnp.einsum("jrd,jdf->jrf", row_block, w_up, preferred_element_type=jnp.float32)
    activated = (jax.nn.silu(gate_pre) * up_pre).astype(jnp.bfloat16)
    produced = jnp.einsum(
        "jrf,jfd->jrd", activated, w_down, preferred_element_type=jnp.float32
    ).astype(jnp.bfloat16)

    def back_shape(tensor):
        return tensor.reshape(local_experts, devices, slot_count, tensor.shape[-1])

    produced, gate_kept, up_kept, act_kept, rows_kept = (
        back_shape(produced),
        back_shape(gate_pre),
        back_shape(up_pre),
        back_shape(activated),
        received,
    )
    returned = lax.all_to_all(
        produced, ("fsdp", "ctx"), split_axis=1, concat_axis=1, tiled=True
    ).reshape(experts * capacity, width_dim)
    expert_vals = returned[targets].reshape(tokens_dev, TOPK, width_dim).astype(jnp.float32)
    moe_partial = jnp.sum(route_probs[:, :, None] * expert_vals, axis=1)
    moe_total = lax.psum(moe_partial.astype(jnp.bfloat16), "tp").astype(jnp.float32)
    block_out = (resid_mid + moe_total).astype(jnp.bfloat16)
    weights_back = collect_weights(shards)
    (
        gain_attn_b,
        gain_ffn_b,
        gain_qk_b,
        query_weight_b,
        key_weight_b,
        value_weight_b,
        router_weight_b,
        out_weight_b,
    ) = weights_back
    gain_query_b = gain_qk_b[:HEAD_SIZE].astype(jnp.float32)
    gain_key_b = gain_qk_b[HEAD_SIZE:].astype(jnp.float32)
    grad_rows = grad_out.astype(jnp.float32)
    grad_prob_partial = jnp.sum(grad_rows[:, None, :] * expert_vals, axis=2)
    grad_expert = (
        (route_probs[:, :, None] * grad_rows[:, None, :])
        .astype(jnp.bfloat16)
        .reshape(assign_count, width_dim)
    )
    padded_grad = jnp.concatenate([grad_expert, jnp.zeros((1, width_dim), jnp.bfloat16)], axis=0)
    send_grads = padded_grad[owners].reshape(local_experts, devices, capacity, width_dim)
    recv_grads = lax.all_to_all(
        send_grads, ("fsdp", "ctx"), split_axis=1, concat_axis=1, tiled=True
    ).reshape(local_experts, devices * capacity, width_dim)
    gate_flat = gate_kept.reshape(local_experts, devices * capacity, hidden_local)
    up_flat = up_kept.reshape(local_experts, devices * capacity, hidden_local)
    act_flat = act_kept.reshape(local_experts, devices * capacity, hidden_local)
    rows_flat = rows_kept.reshape(local_experts, devices * capacity, width_dim)
    sigmoid_gate = jax.nn.sigmoid(gate_flat)
    silu_gate = jax.nn.silu(gate_flat)
    grad_act = jnp.einsum("jrd,jfd->jrf", recv_grads, w_down, preferred_element_type=jnp.float32)
    grad_down = jnp.einsum("jrf,jrd->jfd", act_flat, recv_grads, preferred_element_type=jnp.float32)
    grad_gate_pre = (
        grad_act * up_flat * (sigmoid_gate * (1.0 + gate_flat * (1.0 - sigmoid_gate)))
    ).astype(jnp.bfloat16)
    grad_up_pre = (grad_act * silu_gate).astype(jnp.bfloat16)
    grad_gate = jnp.einsum(
        "jrd,jrf->jdf", rows_flat, grad_gate_pre, preferred_element_type=jnp.float32
    )
    grad_up = jnp.einsum("jrd,jrf->jdf", rows_flat, grad_up_pre, preferred_element_type=jnp.float32)
    grad_slots = jnp.einsum(
        "jrf,jdf->jrd", grad_gate_pre, w_gate, preferred_element_type=jnp.float32
    )
    grad_slots = (
        grad_slots
        + jnp.einsum("jrf,jdf->jrd", grad_up_pre, w_up, preferred_element_type=jnp.float32)
    ).astype(jnp.bfloat16)
    grad_slots = grad_slots.reshape(local_experts, devices, capacity, width_dim)
    grad_back = lax.all_to_all(grad_slots, ("fsdp", "ctx"), split_axis=1, concat_axis=1, tiled=True)
    grad_back = grad_back.reshape(experts * capacity, width_dim)
    grad_hidden_partial = jnp.sum(
        grad_back[targets].reshape(tokens_dev, TOPK, width_dim).astype(jnp.float32), axis=1
    )
    grad_hidden_moe, grad_prob = (
        lax.psum(grad_hidden_partial.astype(jnp.bfloat16), "tp").astype(jnp.float32),
        lax.psum(grad_prob_partial.astype(jnp.bfloat16), "tp").astype(jnp.float32),
    )
    grad_chosen = route_probs * (
        grad_prob - jnp.sum(route_probs * grad_prob, axis=1, keepdims=True)
    )
    route_hits = (routes[:, :, None] == jnp.arange(experts, dtype=jnp.int32)[None, None, :]).astype(
        jnp.float32
    )
    grad_logits = jnp.sum(route_hits * grad_chosen[:, :, None], axis=1).astype(jnp.bfloat16)
    grad_router_local = jnp.einsum(
        "td,te->de", hidden_two, grad_logits, preferred_element_type=jnp.float32
    )
    grad_hidden_two = grad_hidden_moe + jnp.einsum(
        "te,de->td", grad_logits, router_weight_b, preferred_element_type=jnp.float32
    )
    gain_two_wide = gain_ffn_b.astype(jnp.float32)
    grad_ffn_local = jnp.sum(grad_hidden_two * normed_two, axis=0)
    grad_mid = grad_rows + rms_norm_gradient(
        grad_hidden_two, normed_two, inverse_two, gain_two_wide
    )
    grad_proj = grad_mid.astype(jnp.bfloat16)
    grad_outproj_local = jnp.einsum(
        "tq,td->qd", attended, grad_proj, preferred_element_type=jnp.float32
    )
    attended_gradient = jnp.einsum(
        "td,qd->tq", grad_proj, out_weight_b, preferred_element_type=jnp.float32
    ).astype(jnp.bfloat16)
    attended_gradient = attended_gradient.reshape(
        tokens_dev, kv_local, query_group_width, HEAD_SIZE
    )
    scores_again = masked_scores(query_rotated, key_all, allowed)
    probs_att = jnp.exp(scores_again - log_total)
    weights_back_att = probs_att.astype(jnp.bfloat16)
    grad_value_all = jnp.einsum(
        "kgqs,qkgd->skd", weights_back_att, attended_gradient, preferred_element_type=jnp.float32
    )
    grad_probs = jnp.einsum(
        "qkgd,skd->kgqs", attended_gradient, value_all, preferred_element_type=jnp.float32
    )
    delta_row = jnp.sum(probs_att * grad_probs, axis=-1, keepdims=True)
    grad_scores = (probs_att * (grad_probs - delta_row) * HEAD_SIZE ** (-0.5)).astype(jnp.bfloat16)
    grad_query_rot = jnp.einsum(
        "kgqs,skd->qkgd", grad_scores, key_all, preferred_element_type=jnp.float32
    ).reshape(tokens_dev, head_local, HEAD_SIZE)
    grad_key_all = jnp.einsum(
        "kgqs,qkgd->skd", grad_scores, query_rotated, preferred_element_type=jnp.float32
    )
    key_rotated_gradient, grad_value_own = (
        lax.psum_scatter(
            grad_key_all.astype(jnp.bfloat16), "ctx", scatter_dimension=0, tiled=True
        ).astype(jnp.float32),
        lax.psum_scatter(
            grad_value_all.astype(jnp.bfloat16), "ctx", scatter_dimension=0, tiled=True
        ).astype(jnp.float32),
    )
    grad_query_norm = inverse_rotation(grad_query_rot, cosine_table, sine_values)
    key_normed_gradient = inverse_rotation(key_rotated_gradient, cosine_table, sine_values)
    grad_qk_local = jnp.concatenate(
        [
            jnp.sum(grad_query_norm * query_hat, axis=(0, 1)),
            jnp.sum(key_normed_gradient * key_unit_rows, axis=(0, 1)),
        ]
    )
    grad_query_raw = (
        rms_norm_gradient(grad_query_norm, query_hat, query_inverse, gain_query_b)
        .astype(jnp.bfloat16)
        .reshape(tokens_dev, head_local * HEAD_SIZE)
    )
    key_projected_gradient = (
        rms_norm_gradient(key_normed_gradient, key_unit_rows, key_inverse_norm, gain_key_b)
        .astype(jnp.bfloat16)
        .reshape(tokens_dev, kv_local * HEAD_SIZE)
    )
    value_projected_gradient = grad_value_own.astype(jnp.bfloat16).reshape(
        tokens_dev, kv_local * HEAD_SIZE
    )
    grad_query_local = jnp.einsum(
        "td,tq->dq", hidden_first, grad_query_raw, preferred_element_type=jnp.float32
    )
    grad_key_local = jnp.einsum(
        "td,tq->dq", hidden_first, key_projected_gradient, preferred_element_type=jnp.float32
    )
    grad_value_local = jnp.einsum(
        "td,tq->dq", hidden_first, value_projected_gradient, preferred_element_type=jnp.float32
    )
    grad_hidden_part = jnp.einsum(
        "tq,dq->td", grad_query_raw, query_weight_b, preferred_element_type=jnp.float32
    )
    grad_hidden_part = grad_hidden_part + jnp.einsum(
        "tq,dq->td", key_projected_gradient, key_weight_b, preferred_element_type=jnp.float32
    )
    grad_hidden_part = grad_hidden_part + jnp.einsum(
        "tq,dq->td", value_projected_gradient, value_weight_b, preferred_element_type=jnp.float32
    )
    grad_hidden_one, grad_qk_summed = (
        lax.psum(grad_hidden_part.astype(jnp.bfloat16), "tp").astype(jnp.float32),
        lax.psum(grad_qk_local.astype(jnp.bfloat16), "tp").astype(jnp.float32),
    )
    gain_one_wide = gain_attn_b.astype(jnp.float32)
    grad_attn_local = jnp.sum(grad_hidden_one * normed_one, axis=0)
    grad_in = grad_mid + rms_norm_gradient(grad_hidden_one, normed_one, inverse_one, gain_one_wide)
    reduced = reduce_grads(
        (
            grad_attn_local,
            grad_ffn_local,
            grad_qk_summed,
            grad_query_local,
            grad_key_local,
            grad_value_local,
            grad_router_local,
            grad_outproj_local,
        )
    )
    return (
        block_out,
        grad_in,
        reduced[0],
        reduced[2],
        reduced[3],
        reduced[4],
        reduced[5],
        reduced[7],
        reduced[1],
        reduced[6],
        grad_gate,
        grad_up,
        grad_down,
    )


def solution(mesh):
    return jax.shard_map(
        on_device,
        mesh=mesh,
        in_specs=(
            P(("fsdp", "ctx"), None),
            P(("fsdp", "ctx")),
            P(("fsdp", "ctx"), None),
            P("fsdp"),
            P("fsdp"),
            P("fsdp", "tp"),
            P("fsdp", "tp"),
            P("fsdp", "tp"),
            P("tp", "fsdp"),
            P("fsdp"),
            P("fsdp", None),
            P(("fsdp", "ctx"), None, "tp"),
            P(("fsdp", "ctx"), None, "tp"),
            P(("fsdp", "ctx"), "tp", None),
            P(("fsdp", "ctx"), None),
        ),
        out_specs=(
            P(("fsdp", "ctx"), None),
            P(("fsdp", "ctx"), None),
            P("fsdp"),
            P("fsdp"),
            P("fsdp", "tp"),
            P("fsdp", "tp"),
            P("fsdp", "tp"),
            P("tp", "fsdp"),
            P("fsdp"),
            P("fsdp", None),
            P(("fsdp", "ctx"), None, "tp"),
            P(("fsdp", "ctx"), None, "tp"),
            P(("fsdp", "ctx"), "tp", None),
        ),
        check_vma=False,
    )
```

profile of v0, /device:TPU:0, one launch (start us, length us, event | category | flops | bytes accessed | tf_op | source)
XLA Modules:
  0.0 1923.7 jit_solution(16529751070191121559)
XLA Ops:
  13.7 22.3 %all-gather.2 = bf16[8,1,256]{2,1,0:T(2,128)(2,1)S(1)} all-gather(bf16[1,1,256]{2,1,0:T(2,128)(2,1)S(1)} %reshape.539), channel_id=1, replica_groups=mesh['fsdp'=8,'ctx'=2,'tp'=2] {'fsdp'}, dimensions={0}, use_global_device_ids=true | all-gather | bytes 4608 | tf_op jit(solution)/shard_map/all_gather | solution.py:83
  36.0 16.4 all-gather
  52.4 9.0 reduce-window.6
  65.2 19.2 all-reduce.2
  104.5 115.4 %all-gather.12.cloned.1.call-done = bf16[2048,2048]{1,0:T(8,128)(2,1)} async-done(((bf16[256,2048]{1,0:T(8,128)(2,1)}), bf16[2048,2048]{1,0:T(8,128)(2,1)}) %all-gather.12.cloned.1.call-update) | async-done | bytes 8388624 | tf_op jit(solution)/shard_map/all_gather | solution.py:85
  232.6 112.3 %all-gather.14.cloned.1.call-done = bf16[2048,2048]{1,0:T(8,128)(2,1)} async-done(((bf16[2048,256]{1,0:T(8,128)(2,1)}), bf16[2048,2048]{1,0:T(8,128)(2,1)}) %all-gather.14.cloned.1.call-update) | async-done | bytes 8388624 | tf_op jit(solution)/shard_map/all_gather | solution.py:89
  355.6 22.0 %all-reduce.15.cloned.1.call-done = bf16[128,2048]{1,0:T(8,128)(2,1)} async-done(((bf16[128,2048]{1,0:T(8,128)(2,1)}), bf16[128,2048]{1,0:T(8,128)(2,1)}) %all-reduce.15.cloned.1.call-update) | async-done | bytes 524304 | tf_op jit(solution)/shard_map/psum | solution.py:228
  382.2 17.5 gather_fusion
  416.1 201.6 %all_gather.51 = bf16[2048,32]{0,1:T(8,128)(2,1)S(1)} all-gather(bf16[256,32]{0,1:T(8,128)(2,1)S(1)} %copy-done.56), channel_id=1, replica_groups=mesh['fsdp'=8,'ctx'=2,'tp'=2] {'fsdp'}, dimensions={0}, use_global_device_ids=true | all-gather | bytes 147456 | tf_op jit(solution)/shard_map/all_gather | solution.py:88
  631.4 19.1 gather_fusion.2
  687.0 127.2 %all-to-all-done.2 = bf16[2,16,64,2048]{3,2,0,1:T(8,128)(2,1)} async-done(((bf16[2,16,64,2048]{3,2,0,1:T(8,128)(2,1)}), bf16[2,16,64,2048]{3,2,0,1:T(8,128)(2,1)}, u32[]{:S(2)}, u32[]{:S(2)}) %all-to-all-start.2) | async-done | bytes 8388640 | tf_op jit(solution)/shard_map/all_to_all | solution.py:293
  822.6 11.4 multiply_convert_fusion
  849.1 36.5 %all-to-all-start.1 = ((bf16[2,16,64,2048]{3,2,0,1:T(8,128)(2,1)}), bf16[2,16,64,2048]{3,2,0,1:T(8,128)(2,1)}, u32[]{:S(2)}, u32[]{:S(2)}) async-start(bf16[2,16,64,2048]{3,2,0,1:T(8,128)(2,1)} %copy.265), calls=%async_computation.1 | async-start | bytes 16777216 | tf_op jit(solution)/shard_map/all_to_all | solution.py:264
  885.7 12.8 fusion.95
  898.5 10.7 add_convert_fusion
  917.4 118.8 %all-to-all-done.1 = bf16[2,16,64,2048]{3,2,0,1:T(8,128)(2,1)} async-done(((bf16[2,16,64,2048]{3,2,0,1:T(8,128)(2,1)}), bf16[2,16,64,2048]{3,2,0,1:T(8,128)(2,1)}, u32[]{:S(2)}, u32[]{:S(2)}) %all-to-all-start.1) | async-done | bytes 8388640 | tf_op jit(solution)/shard_map/all_to_all | solution.py:264
  1036.2 36.5 %all-to-all-start.3 = ((bf16[2,16,64,2048]{3,2,0,1:T(8,128)(2,1)}), bf16[2,16,64,2048]{3,2,0,1:T(8,128)(2,1)}, u32[]{:S(2)}, u32[]{:S(2)}) async-start(bf16[2,16,64,2048]{3,2,0,1:T(8,128)(2,1)} %copy.270), calls=%async_computation.3 | async-start | bytes 16777216 | tf_op jit(solution)/shard_map/all_to_all | solution.py:320
  1083.2 13.3 gather_fusion.1
  1096.5 126.9 %all-to-all-done.3 = bf16[2,16,64,2048]{3,2,0,1:T(8,128)(2,1)} async-done(((bf16[2,16,64,2048]{3,2,0,1:T(8,128)(2,1)}), bf16[2,16,64,2048]{3,2,0,1:T(8,128)(2,1)}, u32[]{:S(2)}, u32[]{:S(2)}) %all-to-all-start.3) | async-done | bytes 8388640 | tf_op jit(solution)/shard_map/all_to_all | solution.py:320
  1231.6 13.3 gather_fusion.3
  1262.0 48.7 %all-reduce.17.cloned.1.call-done = bf16[128,2048]{1,0:T(8,128)(2,1)} async-done(((bf16[128,2048]{1,0:T(8,128)(2,1)}), bf16[128,2048]{1,0:T(8,128)(2,1)}) %all-reduce.17.cloned.1.call-update) | async-done | bytes 524304 | tf_op jit(solution)/shard_map/psum | solution.py:326
  1384.5 10.1 fusion.99
  1394.5 14.9 reduce-scatter.16.cloned.1.call-done
  1409.4 67.0 %reduce-scatter.14.cloned.1.call-done = bf16[256,256]{1,0:T(8,128)(2,1)} async-done(((bf16[2048,256]{1,0:T(8,128)(2,1)}), bf16[256,256]{1,0:T(8,128)(2,1)}) %reduce-scatter.14.cloned.1.call-update) | async-done | bytes 131088 | tf_op jit(solution)/shard_map/reduce_scatter | solution.py:107
  1476.5 150.5 %reduce-scatter.18.cloned.1.call-done = bf16[2048,256]{1,0:T(8,128)(2,1)} async-done(((bf16[2048,2048]{1,0:T(8,128)(2,1)}), bf16[2048,256]{1,0:T(8,128)(2,1)}) %reduce-scatter.18.cloned.1.call-update) | async-done | bytes 1048592 | tf_op jit(solution)/shard_map/reduce_scatter | solution.py:116
  1627.0 150.1 %reduce-scatter.12.cloned.1.call-done = bf16[256,2048]{1,0:T(8,128)(2,1)} async-done(((bf16[2048,2048]{1,0:T(8,128)(2,1)}), bf16[256,2048]{1,0:T(8,128)(2,1)}) %reduce-scatter.12.cloned.1.call-update) | async-done | bytes 1048592 | tf_op jit(solution)/shard_map/reduce_scatter | solution.py:104
  1777.1 11.2 fusion.98
  1788.3 11.5 fusion.97
  1799.8 19.4 %all-reduce.19.cloned.1.call-done = (bf16[128,2048]{1,0:T(8,128)(2,1)}, bf16[128,2048]{1,0:T(8,128)(2,1)}) async-done(((bf16[128,2048]{1,0:T(8,128)(2,1)}, bf16[128,2048]{1,0:T(8,128)(2,1)}), (bf16[128,2048]{1,0:T(8,128)(2,1)}, bf16[128,2048]{1,0:T(8,128)(2,1)})) %all-reduce.19.cloned.1.call-update) | async-done | bytes 1048592 | tf_op jit(solution)/shard_map/psum | solution.py:269
  1820.7 22.0 %all-reduce.6 = (bf16[2048]{0:T(1024)(128)(2,1)S(1)}, bf16[256]{0:T(256)(128)(2,1)S(1)}, bf16[2048]{0:T(1024)(128)(2,1)S(1)}) all-reduce(bf16[2048]{0:T(1024)(128)(2,1)S(1)} %get-tuple-element.17, bf16[256]{0:T(256)(128)(2,1)S(1)} %pad_maximum_fusion.6, ...), channel_id=4, replica_groups=mesh['fsdp'=8,'ctx'=2,'tp'=2] {'fsdp'}, use_global_device_ids=true, to_apply=%region_30.31.clone | all-reduce | flops 4352 | bytes 17408
  1847.9 37.5 %reduce-scatter.20.cloned.1.call-done = bf16[256,32]{0,1:T(8,128)(2,1)} async-done(((bf16[2048,32]{0,1:T(8,128)(2,1)}), bf16[256,32]{0,1:T(8,128)(2,1)}) %reduce-scatter.20.cloned.1.call-update) | async-done | bytes 16400 | tf_op jit(solution)/shard_map/reduce_scatter | solution.py:113
  1894.6 14.3 all-reduce.21.cloned.1.call-done
  (333 shorter events, 286.9 us)
Async XLA Ops:
  7.2 815.4 %copy-start = (bf16[2,384,2048]{2,1,0:T(8,128)(2,1)S(1)}, bf16[2,384,2048]{2,1,0:T(8,128)(2,1)}, u32[]{:S(2)}) copy-start(bf16[2,384,2048]{2,1,0:T(8,128)(2,1)} %param.28) | copy-start | bytes 9437188
  7.2 80.7 %all-gather.8.cloned.1.call-start = ((), (), s32[]{:S(2)}) async-start(), calls=%async_computation.11 | async-start | bytes 1179648 | tf_op jit(solution)/shard_map/all_gather | solution.py:87
  8.0 86.5 %all-gather.10.cloned.1.call-start = ((), (), s32[]{:S(2)}) async-start(), calls=%async_computation.12 | async-start | bytes 1179648 | tf_op jit(solution)/shard_map/all_gather | solution.py:86
  8.7 211.1 %all-gather.12.cloned.1.call-start = ((), (), s32[]{:S(2)}) async-start(), calls=%async_computation.13 | async-start | bytes 9437184 | tf_op jit(solution)/shard_map/all_gather | solution.py:85
  9.4 335.5 %all-gather.14.cloned.1.call-start = ((), (), s32[]{:S(2)}) async-start(), calls=%async_computation.14 | async-start | bytes 9437184 | tf_op jit(solution)/shard_map/all_gather | solution.py:89
  10.0 367.6 %all-reduce.15.cloned.1.call-start = ((), (), s32[]{:S(2)}) async-start(), calls=%async_computation.15 | async-start | bytes 1048576 | tf_op jit(solution)/shard_map/psum | solution.py:228
  35.9 343.1 %copy-start.47 = (f32[8,1,256]{2,1,0:T(1,128)}, f32[8,1,256]{2,1,0:T(1,128)S(1)}, u32[]{:S(2)}) copy-start(f32[8,1,256]{2,1,0:T(1,128)S(1)} %convert_element_type.286) | copy-start | bytes 24580
  52.4 167.4 %copy-start.40 = (f32[8,1,256]{2,1,0:T(1,128)}, f32[8,1,256]{2,1,0:T(1,128)S(1)}, u32[]{:S(2)}) copy-start(f32[8,1,256]{2,1,0:T(1,128)S(1)} %convert_element_type.285) | copy-start | bytes 24580
  87.2 139.3 %copy-start.26 = (f32[128,64]{1,0:T(8,128)}, f32[128,64]{1,0:T(8,128)S(1)}, u32[]{:S(2)}) copy-start(f32[128,64]{1,0:T(8,128)S(1)} %get-tuple-element.57) | copy-start | bytes 98308
  87.2 139.3 %copy-start.28 = (f32[128,64]{1,0:T(8,128)}, f32[128,64]{1,0:T(8,128)S(1)}, u32[]{:S(2)}) copy-start(f32[128,64]{1,0:T(8,128)S(1)} %get-tuple-element.58) | copy-start | bytes 98308
  96.3 128.5 %copy-start.24 = (f32[128,256]{1,0:T(8,128)}, f32[128,256]{1,0:T(8,128)S(1)}, u32[]{:S(2)}) copy-start(f32[128,256]{1,0:T(8,128)S(1)} %fusion.86) | copy-start | bytes 393220
  100.8 129.4 %copy-start.33 = (bf16[256,2,128]{0,2,1:T(8,128)(2,1)}, bf16[256,2,128]{0,2,1:T(8,128)(2,1)S(1)}, u32[]{:S(2)}) copy-start(bf16[256,2,128]{0,2,1:T(8,128)(2,1)S(1)} %all_gather.43) | copy-start | bytes 393220
  407.9 250.8 %all-to-all-start = ((bf16[2,16,64,2048]{3,2,0,1:T(8,128)(2,1)}), bf16[2,16,64,2048]{3,2,0,1:T(8,128)(2,1)}, u32[]{:S(2)}, u32[]{:S(2)}) async-start(bf16[2,16,64,2048]{3,2,0,1:T(8,128)(2,1)} %copy.263), calls=%async_computation | async-start | bytes 16777216 | tf_op jit(solution)/shard_map/all_to_all | solution.py:244
  658.7 155.5 %all-to-all-start.2 = ((bf16[2,16,64,2048]{3,2,0,1:T(8,128)(2,1)}), bf16[2,16,64,2048]{3,2,0,1:T(8,128)(2,1)}, u32[]{:S(2)}, u32[]{:S(2)}) async-start(bf16[2,16,64,2048]{3,2,0,1:T(8,128)(2,1)} %copy.268), calls=%async_computation.2 | async-start | bytes 16777216 | tf_op jit(solution)/shard_map/all_to_all | solution.py:293
  849.1 187.1 %all-to-all-start.1 = ((bf16[2,16,64,2048]{3,2,0,1:T(8,128)(2,1)}), bf16[2,16,64,2048]{3,2,0,1:T(8,128)(2,1)}, u32[]{:S(2)}, u32[]{:S(2)}) async-start(bf16[2,16,64,2048]{3,2,0,1:T(8,128)(2,1)} %copy.265), calls=%async_computation.1 | async-start | bytes 16777216 | tf_op jit(solution)/shard_map/all_to_all | solution.py:264
  917.4 155.4 %copy-start.60 = (s32[1024,1]{0,1:T(1,128)S(1)}, s32[1024,1]{0,1:T(1,128)}, u32[]{:S(2)}) copy-start(s32[1024,1]{0,1:T(1,128)} %copy-done.59) | copy-start | bytes 12292
  917.4 155.4 %copy-start.9 = (bf16[2,8,128,256]{2,3,1,0:T(8,128)(2,1)S(1)}, bf16[2,8,128,256]{2,3,1,0:T(8,128)(2,1)}, u32[]{:S(2)}) copy-start(bf16[2,8,128,256]{2,3,1,0:T(8,128)(2,1)} %copy-done.8) | copy-start | bytes 3145732
  1036.2 187.1 %all-to-all-start.3 = ((bf16[2,16,64,2048]{3,2,0,1:T(8,128)(2,1)}), bf16[2,16,64,2048]{3,2,0,1:T(8,128)(2,1)}, u32[]{:S(2)}, u32[]{:S(2)}) async-start(bf16[2,16,64,2048]{3,2,0,1:T(8,128)(2,1)} %copy.270), calls=%async_computation.3 | async-start | bytes 16777216 | tf_op jit(solution)/shard_map/all_to_all | solution.py:320
  1072.8 237.9 %all-reduce.17.cloned.1.call-start = ((), (), s32[]{:S(2)}) async-start(), calls=%async_computation.16 | async-start | bytes 1048576 | tf_op jit(solution)/shard_map/psum | solution.py:326
  1250.8 59.8 %copy-start.6 = (bf16[128,2048]{1,0:T(8,128)(2,1)S(1)}, bf16[128,2048]{1,0:T(8,128)(2,1)}, u32[]{:S(2)}) copy-start(bf16[128,2048]{1,0:T(8,128)(2,1)} %all-reduce.15.cloned.1.call-done) | copy-start | bytes 1572868
  1250.8 59.8 %copy-start.32 = (bf16[2048,32]{0,1:T(8,128)(2,1)S(1)}, bf16[2048,32]{0,1:T(8,128)(2,1)}, u32[]{:S(2)}) copy-start(bf16[2048,32]{0,1:T(8,128)(2,1)} %copy-done.31) | copy-start | bytes 393220
  1250.8 59.8 %copy-start.48 = (f32[8,1,256]{2,1,0:T(1,128)S(1)}, f32[8,1,256]{2,1,0:T(1,128)}, u32[]{:S(2)}) copy-start(f32[8,1,256]{2,1,0:T(1,128)} %copy-done.47) | copy-start | bytes 24580
  1250.8 59.9 %copy-start.64 = (f32[128]{0:T(128)S(1)}, f32[128]{0:T(128)}, u32[]{:S(2)}) copy-start(f32[128]{0:T(128)} %copy-done.63) | copy-start | bytes 1540
  1250.9 78.4 %reduce-scatter.22.cloned.1.call-start = ((), (), s32[]{:S(2)}) async-start(), calls=%async_computation.23 | async-start | bytes 196608 | tf_op jit(solution)/shard_map/reshape | solution.py:400
  1321.5 19.2 %reduce-scatter.10.cloned.1.call-start = ((), (), s32[]{:S(2)}) async-start(), calls=%async_computation.17 | async-start | bytes 196608 | tf_op jit(solution)/shard_map/reduce_scatter | solution.py:375
  1328.9 80.5 %reduce-scatter.16.cloned.1.call-start = ((), (), s32[]{:S(2)}) async-start(), calls=%async_computation.20 | async-start | bytes 1179648 | tf_op jit(solution)/shard_map/reduce_scatter | solution.py:110
  1331.7 144.8 %reduce-scatter.14.cloned.1.call-start = ((), (), s32[]{:S(2)}) async-start(), calls=%async_computation.19 | async-start | bytes 1179648 | tf_op jit(solution)/shard_map/reduce_scatter | solution.py:107
  1344.1 282.9 %reduce-scatter.18.cloned.1.call-start = ((), (), s32[]{:S(2)}) async-start(), calls=%async_computation.21 | async-start | bytes 9437184 | tf_op jit(solution)/shard_map/reduce_scatter | solution.py:116
  1349.7 427.3 %reduce-scatter.12.cloned.1.call-start = ((), (), s32[]{:S(2)}) async-start(), calls=%async_computation.18 | async-start | bytes 9437184 | tf_op jit(solution)/shard_map/reduce_scatter | solution.py:104
  1372.9 446.4 %all-reduce.19.cloned.1.call-start = ((), (), s32[]{:S(2)}) async-start(), calls=%async_computation.24 | async-start | bytes 2097152 | tf_op jit(solution)/shard_map/psum | solution.py:269
  1381.9 503.5 %reduce-scatter.20.cloned.1.call-start = ((), (), s32[]{:S(2)}) async-start(), calls=%async_computation.22 | async-start | bytes 147456 | tf_op jit(solution)/shard_map/reduce_scatter | solution.py:113
  1384.2 524.8 %all-reduce.21.cloned.1.call-start = ((), (), s32[]{:S(2)}) async-start(), calls=%async_computation.25 | async-start | bytes 4718592 | tf_op jit(solution)/shard_map/psum | solution.py:124
  (57 other events, 569.3 us)
Sparse Core Ops, SparseCore 0:
  10.2 43.0 all-gather.7
  55.4 39.1 all-gather.9
  96.6 123.1 all-gather.11
  221.8 123.1 all-gather.13
  350.7 26.8 all-reduce.14
  1251.0 59.6 all-reduce.16
  1321.7 7.5 reduce-scatter.21
  1332.1 8.6 reduce-scatter.9
  1344.2 65.1 reduce-scatter.15
  1413.2 63.1 reduce-scatter.13
  1480.1 146.8 reduce-scatter.17
  1630.5 146.5 reduce-scatter.11
  1780.0 39.2 all-reduce.18
  1823.0 62.2 reduce-scatter.19
  1887.8 21.1 all-reduce.20
where the time goes:
time: 1930 us; the launch traced here: 1920 us
  waiting for transfers between devices  1140 us (59%)
  blocking collectives  301 us (16%)
  local copies, waits for them, and re-layouts  170 us (9%)
  matrix products  152 us (8%)
  starting transfers between devices  84.9 us (4%)
  other arithmetic  57.5 us (3%)
    all_gather x1, blocking collectives, collect_weights(): lax.all_gather(shards[6], 'fsdp', axis=0, tiled=True)  202 us
    reduce_scatter x1, waiting for transfers between devices, reduce_grads(): lax.psum_scatter(local_grads[7].astype(jnp.bfloat16), 'fsdp', scatter_dim...  151 us
    reduce_scatter x1, waiting for transfers between devices, reduce_grads(): lax.psum_scatter(local_grads[3].astype(jnp.bfloat16), 'fsdp', scatter_dim...  150 us
    all_to_all x1, waiting for transfers between devices, on_device(): lax.all_to_all(send_grads, ('fsdp', 'ctx'), split_axis=1, concat_axis=1,...  127 us
    all_to_all x1, waiting for transfers between devices, on_device(): lax.all_to_all(grad_slots, ('fsdp', 'ctx'), split_axis=1, concat_axis=1,...  127 us
    all_to_all x1, waiting for transfers between devices, on_device(): lax.all_to_all(produced, ('fsdp', 'ctx'), split_axis=1, concat_axis=1, ti...  119 us
    all_gather x1, waiting for transfers between devices, collect_weights(): lax.all_gather(shards[3], 'fsdp', axis=0, tiled=True)  115 us
    all_gather x1, waiting for transfers between devices, collect_weights(): lax.all_gather(shards[7], 'fsdp', axis=1, tiled=True)  112 us
  transfers between devices with their start and end apart: 19, of which 17 were waited for; matrix products, arithmetic and copies ran while one was open for 13% of the time, Pallas kernels for 0%

commit v1 on v0

v1 whole, which is shorter than its diff:
```python
import functools

import jax
import jax.numpy as jnp
from jax import lax
from jax.experimental import pallas as pl
from jax.experimental.pallas import tpu as pltpu
from jax.sharding import PartitionSpec as P

QUERY_HEADS = 32
KEY_VALUE_HEADS = 4
HEAD_SIZE = 128
TOPK = 8
MESH = pl.DeviceIdType.MESH

eps_norm = 1e-06
rope_base = 1000000.0

UP, DOWN, ACROSS, PARTNER, SIDE = range(5)


class Gather:
    def __init__(self, array, nf, form="row", half=False, rep=False, chunks=2):
        if nf > 8:
            chunks = 2 if rep else 1
        self.array, self.form, self.half, self.rep, self.chunks = array, form, half, rep, chunks
        self.shape = array.shape
        self.rows = array.shape[0] // 2 if half else array.shape[0]
        self.step = (self.rows // nf if form == "a2a" else self.rows) // chunks

    def out_shape(self, nf):
        rows, cols = self.rows, self.shape[1]
        if self.form == "col":
            return (2 * rows, nf * cols)
        if self.form == "a2a":
            return (2 * rows, cols)
        return (2 * nf * rows, cols)


def gather_kernel(nf, specs, *refs):
    n = len(specs)
    ins, outs, scratch = refs[:n], refs[n : 2 * n], refs[2 * n :]
    stage = scratch[:n]
    recv, send, local = scratch[n:]
    nz = nf // 2
    f, c, t = lax.axis_index("fsdp"), lax.axis_index("ctx"), lax.axis_index("tp")
    z, x = f // 2, lax.rem(f, 2)
    has_up, has_down = z + 1 < nz, z > 0
    device = {
        UP: (f + 2, c, t),
        DOWN: (f - 2, c, t),
        ACROSS: (z * 2 + 1 - x, c, t),
        PARTNER: (f, 1 - c, t),
        SIDE: (f, c, 1 - t),
    }
    any_a2a = any(s.form == "a2a" for s in specs)
    any_rep = any(s.rep for s in specs)
    barrier = pltpu.get_barrier_semaphore()

    def greet(dev):
        pl.semaphore_signal(barrier, 1, device_id=dev, device_id_type=MESH)

    greeted = 1
    greet(device[PARTNER])
    if any_rep:
        greet(device[SIDE])
        greeted += 1
    if any_a2a:

        def greet_far(d, carry):
            greet((lax.rem(f + d, nf), c, t))
            return carry

        lax.fori_loop(1, nf, greet_far, 0)
        pl.semaphore_wait(barrier, greeted + nf - 1)
    else:
        greet(device[ACROSS])

        @pl.when(has_up)
        def _():
            greet(device[UP])

        @pl.when(has_down)
        def _():
            greet(device[DOWN])

        pl.semaphore_wait(
            barrier, greeted + 1 + has_up.astype(jnp.int32) + has_down.astype(jnp.int32)
        )

    first = [sum(s.chunks for s in specs[:a]) for a in range(n)]

    def src(a, q, dest_f=None):
        s = specs[a]
        lo = q * s.step
        if s.half:
            lo = c * s.rows + lo
        if s.form == "a2a":
            lo = dest_f * (s.rows // nf) + lo
        return ins[a].at[pl.ds(lo, s.step)]

    def dst(a, q, bf, bc):
        s = specs[a]
        if s.form == "col":
            width = s.shape[1]
            return outs[a].at[
                pl.ds(bc * s.rows + q * s.step, s.step),
                pl.ds(pl.multiple_of(bf * width, width), width),
            ]
        rows = s.rows // nf if s.form == "a2a" else s.rows
        return outs[a].at[pl.ds((bf * 2 + bc) * rows + q * s.step, s.step)]

    def copy(a, q, bf, bc, source, kind, dev=None, slot=None):
        block = bf * 2 + bc if slot is None else slot
        return pltpu.make_async_remote_copy(
            src_ref=source,
            dst_ref=dst(a, q, bf, bc),
            send_sem=send.at[kind, block, first[a] + q],
            recv_sem=recv.at[bf * 2 + bc, first[a] + q],
            device_id=device[kind] if dev is None else dev,
            device_id_type=MESH,
        )

    def in_half(a, q):
        return (q * 2) // specs[a].chunks == t

    def both(*conds):
        conds = [k for k in conds if k is not None]
        if not conds:
            return None
        return functools.reduce(lambda u, v: u & v, conds)

    def when(cond, fn):
        if cond is None:
            fn()
        else:
            pl.when(cond)(fn)

    def go_up(a, q, dist):
        far = (dist + 1 < nz - 1) | in_half(a, q) if specs[a].rep else None
        return both(has_up, far)

    def go_down(a, q, dist):
        far = (dist + 1 < nz - 1) | in_half(a, q) if specs[a].rep else None
        return both(has_down, far)

    def go_across(a, q):
        return in_half(a, q) if specs[a].rep else None

    relays = [(a, q) for a in range(n) if specs[a].form != "a2a" for q in range(specs[a].chunks)]
    direct = [(a, q) for a in range(n) if specs[a].form == "a2a" for q in range(specs[a].chunks)]

    for a, q in relays:
        source = src(a, q)
        when(go_up(a, q, 0), lambda: copy(a, q, f, c, source, UP).start())
        when(go_down(a, q, 0), lambda: copy(a, q, f, c, source, DOWN).start())
        when(go_across(a, q), lambda: copy(a, q, f, c, source, ACROSS).start())
        copy(a, q, f, c, source, PARTNER).start()
    for a, q in direct:
        copy(a, q, f, c, src(a, q, f), PARTNER).start()

        def far_send(d, carry):
            there = lax.rem(f + d, nf)
            copy(a, q, f, c, src(a, q, there), UP, dev=(there, c, t), slot=there).start()
            return carry

        lax.fori_loop(1, nf, far_send, 0)

    def own_in(a):
        s = specs[a]
        if s.form == "a2a":
            view = ins[a].at[pl.ds(f * s.step, s.step)]
        elif s.half:
            view = ins[a].at[pl.ds(c * s.rows, s.rows)]
        else:
            view = ins[a]
        return pltpu.make_async_copy(view, stage[a], local.at[0, a])

    def own_out(a):
        s = specs[a]
        if s.form == "col":
            width = s.shape[1]
            view = outs[a].at[
                pl.ds(c * s.rows, s.rows), pl.ds(pl.multiple_of(f * width, width), width)
            ]
        else:
            rows = s.rows // nf if s.form == "a2a" else s.rows
            view = outs[a].at[pl.ds((f * 2 + c) * rows, rows)]
        return pltpu.make_async_copy(stage[a], view, local.at[1, a])

    for a in range(n):
        own_in(a).start()
    for a in range(n):
        own_in(a).wait()
        own_out(a).start()

    def arrived(a, q, bf, bc):
        copy(a, q, bf, bc, dst(a, q, bf, bc), PARTNER).wait_recv()

    def pass_on(a, q, bf, kind, cond=None):
        when(cond, lambda: copy(a, q, bf, c, dst(a, q, bf, c), kind).start())

    def column(k):
        for a, q in relays:
            rep = specs[a].rep
            came = ((k < nz - 1) | in_half(a, q)) if rep else None
            aside = (k == nz - 1) if rep else None

            def below():
                bf = (z - k) * 2 + x
                arrived(a, q, bf, c)
                pass_on(a, q, bf, UP, go_up(a, q, k))
                pass_on(a, q, bf, ACROSS, go_across(a, q))
                pass_on(a, q, bf, PARTNER)
                if rep:
                    pass_on(a, q, bf, SIDE, aside)

            def above():
                bf = (z + k) * 2 + x
                arrived(a, q, bf, c)
                pass_on(a, q, bf, DOWN, go_down(a, q, k))
                pass_on(a, q, bf, ACROSS, go_across(a, q))
                pass_on(a, q, bf, PARTNER)
                if rep:
                    pass_on(a, q, bf, SIDE, aside)

            when(both(z - k >= 0, came), below)
            when(both(z + k < nz, came), above)

    def across(k):
        for a, q in relays:
            rep = specs[a].rep

            def take(zz):
                bf = zz * 2 + 1 - x
                arrived(a, q, bf, c)
                pass_on(a, q, bf, PARTNER)
                if rep:
                    pass_on(a, q, bf, SIDE)

            mine = in_half(a, q) if rep else None
            when(both(z - k >= 0, mine), lambda: take(z - k))
            when(both(z + k < nz, k > 0, mine), lambda: take(z + k))

    def aside(k):
        for a, q in relays:
            if not specs[a].rep:
                continue
            other = jnp.logical_not(in_half(a, q))

            def take(bf):
                arrived(a, q, bf, c)
                pass_on(a, q, bf, PARTNER)

            when((z - k >= 0) & other, lambda: take((z - k) * 2 + 1 - x))
            when((z + k < nz) & (k > 0) & other, lambda: take((z + k) * 2 + 1 - x))
            when((z - k >= 0) & (k == nz - 1) & other, lambda: take((z - k) * 2 + x))
            when((z + k < nz) & (k == nz - 1) & other, lambda: take((z + k) * 2 + x))

    def step(k, carry):
        column(k)
        across(k - 1)

        @pl.when(k > 1)
        def _():
            aside(k - 2)

        return carry

    lax.fori_loop(1, nz, step, 0)
    across(nz - 1)
    if any_rep:
        aside(nz - 2)
        aside(nz - 1)

    for a, q in direct:

        def far_take(d, carry):
            there = lax.rem(f + nf - d, nf)
            arrived(a, q, there, c)
            pass_on(a, q, there, PARTNER)
            return carry

        lax.fori_loop(1, nf, far_take, 0)

    def finish(bf, carry):
        zz, xx = bf // 2, lax.rem(bf, 2)
        dist = jnp.abs(zz - z)
        here = xx == x
        for a, q in relays:
            rep = specs[a].rep
            arrived(a, q, bf, 1 - c)
            view = dst(a, q, bf, c)

            def sent(kind, cond):
                when(cond, lambda: copy(a, q, bf, c, view, kind).wait_send())

            half = in_half(a, q) if rep else None
            by_z = ((dist < nz - 1) | half) if rep else None
            sent(PARTNER, None)
            sent(UP, both(here, zz <= z, by_z, go_up(a, q, dist)))
            sent(DOWN, both(here, zz >= z, by_z, go_down(a, q, dist)))
            sent(ACROSS, both(here, by_z, go_across(a, q)))
            if rep:
                sent(SIDE, half & (jnp.logical_not(here) | (dist == nz - 1)))
        for a, q in direct:
            arrived(a, q, bf, 1 - c)
            view = dst(a, q, bf, c)
            copy(a, q, bf, c, view, PARTNER).wait_send()

            @pl.when(bf != f)
            def _():
                copy(a, q, bf, c, view, UP, slot=bf).wait_send()

        return carry

    lax.fori_loop(0, nf, finish, 0)
    for a in range(n):
        own_out(a).wait()


def plane_gather(specs, collective_id, nf):
    n = len(specs)
    total = sum(s.chunks for s in specs)

    def stage_of(s):
        rows = s.rows // nf if s.form == "a2a" else s.rows
        return pltpu.VMEM((rows, s.shape[1]), s.array.dtype)

    return pl.pallas_call(
        functools.partial(gather_kernel, nf, tuple(specs)),
        out_shape=tuple(jax.ShapeDtypeStruct(s.out_shape(nf), s.array.dtype) for s in specs),
        in_specs=[pl.BlockSpec(memory_space=pl.ANY)] * n,
        out_specs=tuple(pl.BlockSpec(memory_space=pl.ANY) for _ in specs),
        scratch_shapes=[stage_of(s) for s in specs]
        + [
            pltpu.SemaphoreType.DMA((2 * nf, total)),
            pltpu.SemaphoreType.DMA((5, 2 * nf, total)),
            pltpu.SemaphoreType.DMA((2, n)),
        ],
        compiler_params=pltpu.CompilerParams(
            collective_id=collective_id, has_side_effects=True
        ),
    )(*[s.array for s in specs])


def norm_forward(values, gain_row):
    inverse = lax.rsqrt(jnp.mean(values * values, axis=-1, keepdims=True) + eps_norm)
    normed = values * inverse
    return (normed * gain_row, normed, inverse)


def rms_norm_gradient(grad_scaled, normed, inverse, gain_row):
    grad_normed = grad_scaled * gain_row
    inner_mean = jnp.mean(grad_normed * normed, axis=-1, keepdims=True)
    return inverse * (grad_normed - normed * inner_mean)


def rope_tables(positions):
    half_dim = HEAD_SIZE // 2
    frequencies = rope_base ** (-(jnp.arange(half_dim, dtype=jnp.float32) * 2.0) / HEAD_SIZE)
    angles = positions.astype(jnp.float32)[:, None] * frequencies[None, :]
    return (jnp.cos(angles)[:, None, :], jnp.sin(angles)[:, None, :])


def rotate(values, cosine_table, sine_values):
    half_dim = values.shape[-1] // 2
    first_half = values[..., :half_dim]
    second_half = values[..., half_dim:]
    return jnp.concatenate(
        [
            first_half * cosine_table - second_half * sine_values,
            second_half * cosine_table + first_half * sine_values,
        ],
        axis=-1,
    )


def inverse_rotation(grad_in_rot, cosine_table, sine_values):
    half_dim = grad_in_rot.shape[-1] // 2
    first_half = grad_in_rot[..., :half_dim]
    second_half = grad_in_rot[..., half_dim:]
    return jnp.concatenate(
        [
            first_half * cosine_table + second_half * sine_values,
            second_half * cosine_table - first_half * sine_values,
        ],
        axis=-1,
    )


def masked_scores(query_rotated, key_rotated, allowed):
    scores = jnp.einsum(
        "qkgd,skd->kgqs", query_rotated, key_rotated, preferred_element_type=jnp.float32
    ) * HEAD_SIZE ** (-0.5)
    return jnp.where(allowed[None, None], scores, -jnp.inf)


def swap(value, axis_name):
    return lax.ppermute(value, axis_name, [(0, 1), (1, 0)])


def sum_over_tp(value):
    mine = value.astype(jnp.bfloat16)
    return mine.astype(jnp.float32) + swap(mine, "tp").astype(jnp.float32)


def block_sum(partial, nf):
    return lax.psum_scatter(partial, ("fsdp", "ctx"), scatter_dimension=0, tiled=True)


def by_shard(rows, nf):
    count, width = rows.shape
    return rows.reshape(count, nf, width // nf).transpose(1, 0, 2).reshape(nf * count, width // nf)


def on_device(
    hidden_in,
    segment_ids,
    routes,
    attn_gain,
    qk_gains,
    w_query,
    key_projection,
    value_projection,
    w_out,
    ffn_gain,
    w_router,
    w_gate,
    w_up,
    w_down,
    grad_out,
):
    tokens_dev, width_dim = hidden_in.shape
    nf = lax.axis_size("fsdp")
    devices = nf * lax.axis_size("ctx")
    local_experts = w_gate.shape[0]
    experts = local_experts * devices
    capacity = max(2, 2 * tokens_dev * TOPK // experts)
    query_group_width = QUERY_HEADS // KEY_VALUE_HEADS
    shard_width = attn_gain.shape[0]
    f_index, c_index = lax.axis_index("fsdp"), lax.axis_index("ctx")
    bf16 = jnp.bfloat16
    f32 = jnp.float32

    pieces = [w_router.reshape(-1), attn_gain, ffn_gain, qk_gains]
    flat = jnp.concatenate(pieces)
    small_rows = -(-flat.shape[0] // 2048) * 16
    small = jnp.pad(flat, (0, small_rows * 128 - flat.shape[0])).reshape(small_rows, 128)
    out_form = "row" if shard_width % 128 else "col"
    small_all, query_weight, key_weight, value_weight, out_weight, grad_all = plane_gather(
        [
            Gather(small, nf, chunks=1),
            Gather(w_query, nf, half=True, chunks=2),
            Gather(key_projection, nf, half=True, chunks=1),
            Gather(value_projection, nf, half=True, chunks=1),
            Gather(w_out, nf, form=out_form, half=True, chunks=2),
            Gather(grad_out, nf, rep=True, chunks=4),
        ],
        1,
        nf,
    )
    if out_form == "row":
        out_weight = out_weight.reshape(nf, -1, shard_width).transpose(1, 0, 2)
        out_weight = out_weight.reshape(-1, width_dim)
    small_all = small_all.reshape(nf, 2, small_rows * 128)[:, 0]
    ends = [0]
    for piece in pieces:
        ends.append(ends[-1] + piece.shape[0])
    router_weight = small_all[:, ends[0] : ends[1]].reshape(width_dim, experts)
    gain_one = small_all[:, ends[1] : ends[2]].reshape(-1).astype(f32)
    gain_two = small_all[:, ends[2] : ends[3]].reshape(-1).astype(f32)
    gain_qk = small_all[:, ends[3] : ends[4]].reshape(-1).astype(f32)
    gain_query, gain_key = gain_qk[:HEAD_SIZE], gain_qk[HEAD_SIZE:]

    kv_local = key_weight.shape[1] // HEAD_SIZE
    head_local = query_weight.shape[1] // HEAD_SIZE
    resid = hidden_in.astype(f32)
    scaled_one, normed_one, inverse_one = norm_forward(resid, gain_one)
    hidden_first = scaled_one.astype(bf16)
    query_raw = jnp.dot(hidden_first, query_weight, preferred_element_type=f32).reshape(
        tokens_dev, head_local, HEAD_SIZE
    )
    key_projected = jnp.dot(hidden_first, key_weight, preferred_element_type=f32).reshape(
        tokens_dev, kv_local, HEAD_SIZE
    )
    value_rows = jnp.dot(hidden_first, value_weight, preferred_element_type=f32).astype(bf16)
    query_normed, query_hat, query_inverse = norm_forward(query_raw, gain_query)
    key_normed, key_unit_rows, key_inverse_norm = norm_forward(key_projected, gain_key)
    own_positions = c_index * tokens_dev + jnp.arange(tokens_dev, dtype=jnp.int32)
    cosine_table, sine_values = rope_tables(own_positions)
    query_rotated = (
        rotate(query_normed, cosine_table, sine_values)
        .astype(bf16)
        .reshape(tokens_dev, kv_local, query_group_width, HEAD_SIZE)
    )
    key_rotated = rotate(key_normed, cosine_table, sine_values).astype(bf16)
    own_segments = segment_ids.astype(bf16)
    packed_kv = jnp.concatenate(
        [
            key_rotated.reshape(tokens_dev, -1),
            value_rows,
            jnp.broadcast_to(own_segments[:, None], (tokens_dev, 128)),
        ],
        axis=1,
    )
    kv_all = lax.all_gather(packed_kv, "ctx", axis=0, tiled=True)
    kv_width = kv_local * HEAD_SIZE
    key_all = kv_all[:, :kv_width].reshape(-1, kv_local, HEAD_SIZE)
    value_all = kv_all[:, kv_width : 2 * kv_width].reshape(-1, kv_local, HEAD_SIZE)
    segment_all = kv_all[:, 2 * kv_width]
    key_positions = jnp.arange(key_all.shape[0], dtype=jnp.int32)
    allowed = (key_positions[None, :] <= own_positions[:, None]) & (
        segment_all[None, :] == own_segments[:, None]
    )
    scores = masked_scores(query_rotated, key_all, allowed)
    top_score = jnp.max(scores, axis=-1, keepdims=True)
    log_total = top_score + jnp.log(jnp.sum(jnp.exp(scores - top_score), axis=-1, keepdims=True))
    weights_att = jnp.exp(scores - log_total).astype(bf16)
    attended = jnp.einsum("kgqs,skd->qkgd", weights_att, value_all, preferred_element_type=f32)
    attended = attended.astype(bf16).reshape(tokens_dev, head_local * HEAD_SIZE)
    out_partial = jnp.dot(attended, out_weight, preferred_element_type=f32)
    resid_mid = resid + sum_over_tp(out_partial)
    scaled_two, normed_two, inverse_two = norm_forward(resid_mid, gain_two)
    hidden_two = scaled_two.astype(bf16)
    logits = jnp.dot(hidden_two, router_weight, preferred_element_type=f32)
    expert_ids = jnp.arange(experts, dtype=jnp.int32)
    hits = routes[:, :, None] == expert_ids[None, None, :]
    routed = jnp.any(hits, axis=1)
    masked_logits = jnp.where(routed, logits, -jnp.inf)
    raised = jnp.where(
        routed, jnp.exp(masked_logits - jnp.max(masked_logits, axis=1, keepdims=True)), 0.0
    )
    probs = raised / jnp.sum(raised, axis=1, keepdims=True)
    marks = jnp.where(routed, probs, -1.0).T

    hidden_all, marks_all, hidden_first_slice = plane_gather(
        [
            Gather(hidden_two, nf, rep=True, chunks=4),
            Gather(marks, nf, chunks=1),
            Gather(by_shard(hidden_first, nf), nf, form="a2a", chunks=1),
        ],
        2,
        nf,
    )
    first_expert = (f_index * 2 + c_index) * local_experts
    marks_here = lax.dynamic_slice_in_dim(
        marks_all.reshape(devices, experts, tokens_dev), first_expert, local_experts, axis=1
    )
    taken = marks_here >= 0.0
    ranks = jnp.cumsum(taken.astype(jnp.int32), axis=2) - 1
    slots = jnp.arange(capacity, dtype=jnp.int32)
    chosen = taken[:, :, None, :] & (ranks[:, :, None, :] == slots[None, None, :, None])
    pick = chosen.astype(bf16)
    weight_slot = jnp.sum(jnp.where(chosen, marks_here[:, :, None, :], 0.0), axis=3)
    weight_slot = weight_slot.transpose(1, 0, 2).reshape(local_experts, devices * capacity)

    def select(rows):
        blocks = rows.reshape(devices, tokens_dev, width_dim)
        out = jnp.einsum("bjst,btd->jbsd", pick, blocks, preferred_element_type=f32)
        return out.astype(bf16).reshape(local_experts, devices * capacity, width_dim)

    def spread(rows):
        blocks = rows.reshape(local_experts, devices, capacity, width_dim)
        out = jnp.einsum("bjst,jbsd->btd", pick, blocks, preferred_element_type=f32)
        return out.astype(bf16).reshape(devices * tokens_dev, width_dim)

    rows_in = select(hidden_all)
    grad_rows_in = select(grad_all)
    gate_pre = jnp.einsum("jrd,jdf->jrf", rows_in, w_gate, preferred_element_type=f32)
    up_pre = jnp.einsum("jrd,jdf->jrf", rows_in, w_up, preferred_element_type=f32)
    sigmoid_gate = jax.nn.sigmoid(gate_pre)
    silu_gate = gate_pre * sigmoid_gate
    activated = (silu_gate * up_pre).astype(bf16)
    produced = jnp.einsum("jrf,jfd->jrd", activated, w_down, preferred_element_type=f32).astype(
        bf16
    )
    wide = produced.astype(f32)
    grad_prob_slot = jnp.sum(wide * grad_rows_in.astype(f32), axis=2)
    grad_prob_part = jnp.sum(
        jnp.where(
            chosen,
            grad_prob_slot.reshape(local_experts, devices, capacity).transpose(1, 0, 2)[..., None],
            0.0,
        ),
        axis=2,
    )
    moe_partial = spread((weight_slot[:, :, None] * wide).astype(bf16))
    grad_prod = (weight_slot[:, :, None] * grad_rows_in.astype(f32)).astype(bf16)
    grad_act = jnp.einsum("jrd,jfd->jrf", grad_prod, w_down, preferred_element_type=f32)
    grad_gate_pre = (
        grad_act * up_pre * (sigmoid_gate * (1.0 + gate_pre * (1.0 - sigmoid_gate)))
    ).astype(bf16)
    grad_up_pre = (grad_act * silu_gate).astype(bf16)
    grad_slots = jnp.einsum("jrf,jdf->jrd", grad_gate_pre, w_gate, preferred_element_type=f32)
    grad_slots = (
        grad_slots + jnp.einsum("jrf,jdf->jrd", grad_up_pre, w_up, preferred_element_type=f32)
    ).astype(bf16)
    hidden_grad_partial = spread(grad_slots)
    grad_down = jnp.einsum("jrf,jrd->jfd", activated, grad_prod, preferred_element_type=f32)
    grad_gate = jnp.einsum("jrd,jrf->jdf", rows_in, grad_gate_pre, preferred_element_type=f32)
    grad_up = jnp.einsum("jrd,jrf->jdf", rows_in, grad_up_pre, preferred_element_type=f32)

    grad_hidden_moe = sum_over_tp(block_sum(hidden_grad_partial, nf))
    grad_prob = lax.all_to_all(
        grad_prob_part, ("fsdp", "ctx"), split_axis=0, concat_axis=0, tiled=True
    ).reshape(experts, tokens_dev)
    grad_prob = grad_prob + swap(grad_prob, "tp")
    grad_prob = grad_prob.T
    block_out = (resid_mid + sum_over_tp(block_sum(moe_partial, nf))).astype(bf16)

    grad_rows = grad_out.astype(f32)
    grad_logits = (
        probs * (grad_prob - jnp.sum(probs * grad_prob, axis=1, keepdims=True))
    ).astype(bf16)
    grad_hidden_two = grad_hidden_moe + jnp.einsum(
        "te,de->td", grad_logits, router_weight, preferred_element_type=f32
    )
    grad_ffn_local = jnp.sum(grad_hidden_two * normed_two, axis=0)
    grad_mid = grad_rows + rms_norm_gradient(grad_hidden_two, normed_two, inverse_two, gain_two)
    grad_proj = grad_mid.astype(bf16)
    attended_gradient = jnp.einsum(
        "td,qd->tq", grad_proj, out_weight, preferred_element_type=f32
    ).astype(bf16)
    attended_gradient = attended_gradient.reshape(
        tokens_dev, kv_local, query_group_width, HEAD_SIZE
    )
    probs_att = jnp.exp(scores - log_total)
    grad_value_all = jnp.einsum(
        "kgqs,qkgd->skd", weights_att, attended_gradient, preferred_element_type=f32
    )
    grad_probs = jnp.einsum(
        "qkgd,skd->kgqs", attended_gradient, value_all, preferred_element_type=f32
    )
    delta_row = jnp.sum(probs_att * grad_probs, axis=-1, keepdims=True)
    grad_scores = (probs_att * (grad_probs - delta_row) * HEAD_SIZE ** (-0.5)).astype(bf16)
    grad_query_rot = jnp.einsum(
        "kgqs,skd->qkgd", grad_scores, key_all, preferred_element_type=f32
    ).reshape(tokens_dev, head_local, HEAD_SIZE)
    grad_key_all = jnp.einsum(
        "kgqs,qkgd->skd", grad_scores, query_rotated, preferred_element_type=f32
    )
    grad_kv_all = jnp.concatenate(
        [grad_key_all.reshape(-1, kv_width), grad_value_all.reshape(-1, kv_width)], axis=1
    )
    theirs = lax.dynamic_slice_in_dim(grad_kv_all, (1 - c_index) * tokens_dev, tokens_dev, axis=0)
    mine = lax.dynamic_slice_in_dim(grad_kv_all, c_index * tokens_dev, tokens_dev, axis=0)
    grad_kv = mine + swap(theirs.astype(bf16), "ctx").astype(f32)
    key_rotated_gradient = grad_kv[:, :kv_width].reshape(tokens_dev, kv_local, HEAD_SIZE)
    grad_query_norm = inverse_rotation(grad_query_rot, cosine_table, sine_values)
    key_normed_gradient = inverse_rotation(key_rotated_gradient, cosine_table, sine_values)
    grad_qk_local = jnp.concatenate(
        [
            jnp.sum(grad_query_norm * query_hat, axis=(0, 1)),
            jnp.sum(key_normed_gradient * key_unit_rows, axis=(0, 1)),
        ]
    )
    grad_query_raw = (
        rms_norm_gradient(grad_query_norm, query_hat, query_inverse, gain_query)
        .astype(bf16)
        .reshape(tokens_dev, head_local * HEAD_SIZE)
    )
    key_projected_gradient = (
        rms_norm_gradient(key_normed_gradient, key_unit_rows, key_inverse_norm, gain_key)
        .astype(bf16)
        .reshape(tokens_dev, kv_width)
    )
    value_projected_gradient = grad_kv[:, kv_width:].astype(bf16)
    grad_hidden_part = jnp.einsum(
        "tq,dq->td", grad_query_raw, query_weight, preferred_element_type=f32
    )
    grad_hidden_part = grad_hidden_part + jnp.einsum(
        "tq,dq->td", key_projected_gradient, key_weight, preferred_element_type=f32
    )
    grad_hidden_part = grad_hidden_part + jnp.einsum(
        "tq,dq->td", value_projected_gradient, value_weight, preferred_element_type=f32
    )
    grad_hidden_one = sum_over_tp(grad_hidden_part)
    grad_in = grad_mid + rms_norm_gradient(grad_hidden_one, normed_one, inverse_one, gain_one)
    grad_attn_local = jnp.sum(grad_hidden_one * normed_one, axis=0)
    grad_qk_local = grad_qk_local + swap(grad_qk_local, "tp")
    tail = jnp.concatenate([grad_attn_local, grad_ffn_local, grad_qk_local])
    tail = jnp.pad(tail, (0, -tail.shape[0] % 1024)).reshape(-1, 128)
    tail_rows = tail.shape[0]
    logit_pad = jnp.pad(grad_logits, ((0, 0), (0, -experts % 128)))

    dq_all, dk_all, dv_all, attended_all, proj_slice, logits_all, tail_all = plane_gather(
        [
            Gather(grad_query_raw, nf, chunks=2),
            Gather(key_projected_gradient, nf, chunks=1),
            Gather(value_projected_gradient, nf, chunks=1),
            Gather(attended, nf, chunks=2),
            Gather(by_shard(grad_proj, nf), nf, form="a2a", chunks=1),
            Gather(logit_pad, nf, chunks=1),
            Gather(tail, nf, chunks=1),
        ],
        3,
        nf,
    )
    over_tokens = functools.partial(
        jnp.einsum, "td,tq->dq", preferred_element_type=f32
    )
    grad_query = over_tokens(hidden_first_slice, dq_all)
    grad_key = over_tokens(hidden_first_slice, dk_all)
    grad_value = over_tokens(hidden_first_slice, dv_all)
    grad_out_proj = over_tokens(attended_all, proj_slice)
    hidden_slice = lax.dynamic_slice_in_dim(hidden_all, f_index * shard_width, shard_width, axis=1)
    grad_router = over_tokens(hidden_slice, logits_all)[:, :experts]
    tail_sum = jnp.sum(tail_all.reshape(devices, tail_rows * 128), axis=0)
    grad_attn = lax.dynamic_slice_in_dim(tail_sum, f_index * shard_width, shard_width)
    grad_ffn = lax.dynamic_slice_in_dim(tail_sum, width_dim + f_index * shard_width, shard_width)
    qk_width = qk_gains.shape[0]
    grad_qk = lax.dynamic_slice_in_dim(tail_sum, 2 * width_dim + f_index * qk_width, qk_width)
    return (
        block_out,
        grad_in,
        grad_attn,
        grad_qk,
        grad_query,
        grad_key,
        grad_value,
        grad_out_proj,
        grad_ffn,
        grad_router,
        grad_gate,
        grad_up,
        grad_down,
    )


def solution(mesh):
    return jax.shard_map(
        on_device,
        mesh=mesh,
        in_specs=(
            P(("fsdp", "ctx"), None),
            P(("fsdp", "ctx")),
            P(("fsdp", "ctx"), None),
            P("fsdp"),
            P("fsdp"),
            P("fsdp", "tp"),
            P("fsdp", "tp"),
            P("fsdp", "tp"),
            P("tp", "fsdp"),
            P("fsdp"),
            P("fsdp", None),
            P(("fsdp", "ctx"), None, "tp"),
            P(("fsdp", "ctx"), None, "tp"),
            P(("fsdp", "ctx"), "tp", None),
            P(("fsdp", "ctx"), None),
        ),
        out_specs=(
            P(("fsdp", "ctx"), None),
            P(("fsdp", "ctx"), None),
            P("fsdp"),
            P("fsdp"),
            P("fsdp", "tp"),
            P("fsdp", "tp"),
            P("fsdp", "tp"),
            P("tp", "fsdp"),
            P("fsdp"),
            P("fsdp", None),
            P(("fsdp", "ctx"), None, "tp"),
            P(("fsdp", "ctx"), None, "tp"),
            P(("fsdp", "ctx"), "tp", None),
        ),
        check_vma=False,
    )
```

time: 1930 us -> 865 us (0.45)
  waiting for transfers between devices: 1140 us -> 181 us
  Pallas kernels: 0 us -> 341 us
  blocking collectives: 301 us -> 2.51 us
  local copies, waits for them, and re-layouts: 170 us -> 65.6 us
  starting transfers between devices: 84.9 us -> 11.1 us
  matrix products: 152 us -> 193 us
    all_to_all x4 -> x1, waiting for transfers between devices: 373 us -> 0.01 us  [on_device(): lax.all_to_all(grad_prob_part, ('fsdp', 'ctx'), split_axis=0, concat_axis...]
    pallas_call x0 -> x3, Pallas kernels: none -> 341 us  [plane_gather(): pl.pallas_call(functools.partial(gather_kernel, nf, tuple(specs)), out_sh...]
    reduce_scatter x6 -> x2, waiting for transfers between devices: 429 us -> 162 us  [block_sum(): lax.psum_scatter(partial, ('fsdp', 'ctx'), scatter_dimension=0, tiled=True)]
    all_gather x6 -> x1, blocking collectives: 246 us -> 2.51 us  [on_device(): kv_all = lax.all_gather(packed_kv, 'ctx', axis=0, tiled=True)]
    all_gather x4 -> x0, waiting for transfers between devices: 232 us -> none  [the longest x1 115 us: collect_weights(): lax.all_gather(shards[3], 'fsdp', axis=0, tiled=True)]
    psum x4 -> x0, waiting for transfers between devices: 104 us -> none  [the longest x1 48.7 us: on_device(): lax.psum(grad_hidden_partial.astype(jnp.bfloat16), 'tp').astype(jnp.float32)]
    all_to_all x4 -> x1, starting transfers between devices: 83.8 us -> 4.39 us  [on_device(): lax.all_to_all(grad_prob_part, ('fsdp', 'ctx'), split_axis=0, concat_axis...]
    gather x9 -> x0, local copies, waits for them, and re-layouts: 70.4 us -> none  [the longest x1 19.1 us: on_device(): padded_grad[owners].reshape(local_experts, devices, capacity, width_dim)]
  transfers between devices with their start and end apart: 19 -> 10, of which waited for: 17 -> 5; matrix products, arithmetic and copies ran while one was open for 13% -> 8% of each run, Pallas kernels for 0% -> 0%
where the time goes in v1:
time: 865 us; the launch traced here: 858 us
  Pallas kernels  341 us (39%)
  matrix products  193 us (22%)
  waiting for transfers between devices  181 us (21%)
  local copies, waits for them, and re-layouts  65.6 us (8%)
  other arithmetic  47.3 us (5%)
  between operations  15.7 us (2%)
  starting transfers between devices  11.1 us (1%)
    pallas_call x3, Pallas kernels, plane_gather(): pl.pallas_call(functools.partial(gather_kernel, nf, tuple(specs)), out_sh...  341 us
    reduce_scatter x2, waiting for transfers between devices, block_sum(): lax.psum_scatter(partial, ('fsdp', 'ctx'), scatter_dimension=0, tiled=True)  162 us
    dot_general x2, matrix products, select(): out = jnp.einsum('bjst,btd->jbsd', pick, blocks, preferred_element_type=f32)  20.4 us
    ppermute x7, waiting for transfers between devices, swap(): return lax.ppermute(value, axis_name, [(0, 1), (1, 0)])  19.4 us
    dot_general x2, matrix products, spread(): out = jnp.einsum('bjst,jbsd->btd', pick, blocks, preferred_element_type=f32)  18.5 us
  transfers between devices with their start and end apart: 10, of which 5 were waited for; matrix products, arithmetic and copies ran while one was open for 8% of the time, Pallas kernels for 0%

profile of v1, /device:TPU:0, one launch (start us, length us, event | category | flops | bytes accessed | tf_op | source)
XLA Modules:
  0.0 858.0 jit_solution(16180133451779390544)
XLA Ops:
  9.7 147.7 %shard_map.246 = (bf16[1280,128]{1,0:T(8,128)(2,1)}, bf16[2048,2048]{1,0:T(8,128)(2,1)}, bf16[2048,256]{1,0:T(8,128)(2,1)}, bf16[2048,256]{1,0:T(8,128)(2,1)}, b...) custom-call(bf16[80,128]{1,0:T(8,128)(2,1)} %fusion.87.refs_0_, bf16[256,2048]{1,0:T(8,128)(2,1)} %refs_1_.1, ...), custom_call_target="tpu_custom_call" | custom-call | tf_op jit(solution)/shard_map/pallas_call | solution.py:330
  174.9 4.8 fusion.112
  188.8 5.7 convolution_convert_fusion.2
  199.9 9.1 %collective-permute-done = bf16[128,2048]{1,0:T(8,128)(2,1)} collective-permute-done((bf16[128,2048]{1,0:T(8,128)(2,1)}, bf16[128,2048]{1,0:T(8,128)(2,1)}, u32[]{:S(2)}, u32[]{:S(2)}) %collective-permute-start) | collective-permute-done | bytes 524320 | tf_op jit(solution)/shard_map/ppermute | solution.py:400
  216.5 67.6 %shard_map.247 = (bf16[2048,2048]{1,0:T(8,128)(2,1)}, f32[512,128]{1,0:T(8,128)}, bf16[2048,256]{1,0:T(8,128)(2,1)}) custom-call(bf16[128,2048]{1,0:T(8,128)(2,1)} %copy-done.23, f32[32,128]{1,0:T(8,128)} %fusion.93.refs_1_, bf16[1024,256]{1,0:T(8,128)(2,1)} %bitcast.277), custom_call_target="tpu_custom_call" | custom-call | tf_op jit(solution)/shard_map/pallas_call | solution.py:330
  289.4 8.9 %convert_bitcast_fusion.1 = bf16[2,16,64,2048]{3,2,0,1:T(8,128)(2,1)} fusion(bf16[16,128,2048,1]{2,1,3,0:T(8,128)(2,1)} %bitcast.260, s32[16,2,128]{2,1,0:T(2,128)S(1)} %copy.196, pred[16,2,128]{2,1,0:T(4,128)(4,1)} %copy.195), kind=kOutput, calls=%fused_computation.15 | convolution fusion | flops 1078460416 | bytes 16797696 | tf_op jit(solution)/shard_map/bjst,btd->jbsd/dot_general | solution.py:560
  298.3 8.3 copy.199
  306.6 11.5 %convert_bitcast_fusion = f32[2,16,64,2048]{3,2,0,1:T(8,128)} fusion(bf16[16,128,2048,1]{2,1,3,0:T(8,128)(2,1)} %bitcast.259, s32[16,2,128]{2,1,0:T(2,128)S(1)} %copy.196, pred[16,2,128]{2,1,0:T(4,128)(4,1)S(1)} %copy-done.61), kind=kOutput, calls=%fused_computation.9 | convolution fusion | flops 1082654720 | bytes 25186304 | tf_op jit(solution)/shard_map/bjst,btd->jbsd/dot_general | solution.py:560
  318.1 13.7 %copy.201 = f32[2,16,64,2048]{3,2,1,0:T(8,128)} copy(f32[2,16,64,2048]{3,2,0,1:T(8,128)} %convert_bitcast_fusion) | data formatting | bytes 33554432 | tf_op jit(solution)/shard_map/convert_element_type | solution.py:589
  333.0 4.5 fusion.114
  337.6 6.2 multiply_convert_fusion.2
  343.8 11.5 %fusion.2 = (f32[2,1024]{1,0:T(2,128)}, bf16[2,1024,2048]{2,1,0:T(8,128)(2,1)}) fusion(f32[2,16,64,2048]{3,2,1,0:T(8,128)} %copy.201, bf16[2,1024,384]{2,1,0:T(8,128)(2,1)S(1)} %get-tuple-element.92, bf16[2,384,2048]{2,1,0:T(8,128)(2,1)S(1)} %copy-done), kind=kOutput, calls=%fused_computation.4 | convolution fusion | flops 3238000640 | bytes 29892608 | tf_op jit(solution)/shard_map/jrf,jfd->jrd/dot_general | solution.py:575
  361.5 13.0 %fusion.3 = (bf16[2,1024,2048]{2,1,0:T(8,128)(2,1)S(1)}, bf16[2,1024,2048]{2,1,0:T(8,128)(2,1)}) fusion(f32[2,16,64,2048]{3,2,1,0:T(8,128)} %copy.201, f32[2,1024]{1,0:T(2,128)} %mul.478, bf16[2,1024,2048]{2,1,0:T(8,128)(2,1)} %get-tuple-element.95), kind=kLoop, calls=%fused_computation.7 | loop fusion | flops 20971520 | bytes 41951232 | tf_op jit(solution)/shard_map/convert_element_type | solution.py:589
  374.5 12.5 %multiply_convert_fusion = (bf16[2,1024,384]{2,1,0:T(8,128)(2,1)}, bf16[2,1024,384]{2,1,0:T(8,128)(2,1)}) fusion(f32[2,1024,384]{2,1,0:T(8,128)} %copy-done.89, f32[2,1024,384]{2,1,0:T(8,128)} %get-tuple-element.93, bf16[2,1024,2048]{2,1,0:T(8,128)(2,1)S(1)} %get-tuple-element.84, bf16[2,384,2048]{2,1,0:T(8,128)(2,1)S(1)} %copy-done), kind=kOutput, calls=%fused_computation.17 | convolution fusion | flops 3231449088 | bytes 20971520 | tf_op jit(solution)/shard_map/jrd,jfd->jrf/dot_general | solution.py:590
  387.0 9.7 %fusion.115 = f32[2,1024,2048]{2,1,0:T(8,128)} fusion(bf16[2,1024,384]{2,1,0:T(8,128)(2,1)} %get-tuple-element.62, bf16[2,2048,384]{2,1,0:T(8,128)(2,1)S(1)} %copy-done.34), kind=kOutput, calls=%fused_computation.215 | convolution fusion | flops 3221225472 | bytes 21495808 | tf_op jit(solution)/shard_map/jrf,jdf->jrd/dot_general | solution.py:595
  396.7 10.7 %add_convert_fusion = bf16[2,1024,2048]{2,1,0:T(8,128)(2,1)} fusion(f32[2,1024,2048]{2,1,0:T(8,128)} %fusion.115, bf16[2,1024,384]{2,1,0:T(8,128)(2,1)} %get-tuple-element.61, bf16[2,2048,384]{2,1,0:T(8,128)(2,1)S(1)} %copy-done.32), kind=kOutput, calls=%fused_computation.10 | convolution fusion | flops 3229614080 | bytes 29884416 | tf_op jit(solution)/shard_map/jrf,jdf->jrd/dot_general | solution.py:597
  407.4 9.0 %bitcast_convert_fusion = bf16[16,128,2048]{2,1,0:T(8,128)(2,1)} fusion(bf16[2,16,64,2048]{3,2,1,0:T(8,128)(2,1)} %bitcast.251, s32[16,2,128]{2,1,0:T(2,128)S(1)} %copy.196, pred[16,2,128]{2,1,0:T(4,128)(4,1)} %copy.195), kind=kOutput, calls=%fused_computation.5 | convolution fusion | flops 1078460416 | bytes 16797696 | tf_op jit(solution)/shard_map/bjst,jbsd->btd/dot_general | solution.py:565
  417.1 9.4 %bitcast_convert_fusion.1 = bf16[16,128,2048]{2,1,0:T(8,128)(2,1)} fusion(bf16[2,16,64,2048]{3,2,1,0:T(8,128)(2,1)} %bitcast.254, s32[16,2,128]{2,1,0:T(2,128)S(1)} %copy.196, pred[16,2,128]{2,1,0:T(4,128)(4,1)S(1)} %copy-done.62), kind=kOutput, calls=%fused_computation.8 | convolution fusion | flops 1078460416 | bytes 16797696 | tf_op jit(solution)/shard_map/bjst,jbsd->btd/dot_general | solution.py:565
  431.1 4.4 all-to-all-start
  435.4 11.4 %fusion.122 = f32[2,2048,384]{2,1,0:T(8,128)} fusion(bf16[2,1024,2048]{2,1,0:T(8,128)(2,1)} %bitcast.261, bf16[2,1024,384]{2,1,0:T(8,128)(2,1)} %get-tuple-element.62), kind=kOutput, calls=%fused_computation.222 | convolution fusion | flops 3221225472 | bytes 16252928 | tf_op jit(solution)/shard_map/jrd,jrf->jdf/dot_general | solution.py:601
  448.5 70.2 %reduce-scatter.5.cloned.1.call-done = bf16[128,2048]{1,0:T(8,128)(2,1)} async-done(((bf16[2048,2048]{1,0:T(8,128)(2,1)}), bf16[128,2048]{1,0:T(8,128)(2,1)}) %reduce-scatter.5.cloned.1.call-update) | async-done | bytes 524304 | tf_op jit(solution)/shard_map/reduce_scatter | solution.py:409
  520.1 11.2 %fusion.123 = f32[2,2048,384]{2,1,0:T(8,128)} fusion(bf16[2,1024,2048]{2,1,0:T(8,128)(2,1)} %bitcast.262, bf16[2,1024,384]{2,1,0:T(8,128)(2,1)} %get-tuple-element.61), kind=kOutput, calls=%fused_computation.223 | convolution fusion | flops 3221225472 | bytes 16252928 | tf_op jit(solution)/shard_map/jrd,jrf->jdf/dot_general | solution.py:602
  534.1 91.7 %reduce-scatter.3.cloned.1.call-done = bf16[128,2048]{1,0:T(8,128)(2,1)} async-done(((bf16[2048,2048]{1,0:T(8,128)(2,1)}), bf16[128,2048]{1,0:T(8,128)(2,1)}) %reduce-scatter.3.cloned.1.call-update) | async-done | bytes 524304 | tf_op jit(solution)/shard_map/reduce_scatter | solution.py:409
  629.2 10.2 %collective-permute-done.1 = bf16[128,2048]{1,0:T(8,128)(2,1)S(1)} collective-permute-done((bf16[128,2048]{1,0:T(8,128)(2,1)}, bf16[128,2048]{1,0:T(8,128)(2,1)S(1)}, u32[]{:S(2)}, u32[]{:S(2)}) %collective-permute-start.1) | collective-permute-done | bytes 524320 | tf_op jit(solution)/shard_map/ppermute | solution.py:400
  642.2 6.8 fusion.25
  651.0 5.5 fusion.20
  656.5 5.4 fusion.19
  673.7 6.5 fusion.116
  688.7 9.6 %fusion.124 = f32[2,384,2048]{2,1,0:T(8,128)} fusion(bf16[2,1024,384]{2,1,0:T(8,128)(2,1)S(1)} %copy-done.10, bf16[2,1024,2048]{2,1,0:T(8,128)(2,1)} %copy-done.2), kind=kOutput, calls=%fused_computation.224 | convolution fusion | flops 3221225472 | bytes 16252928 | tf_op jit(solution)/shard_map/jrf,jrd->jfd/dot_general | solution.py:600
  701.9 126.0 %shard_map.248 = (bf16[2048,2048]{1,0:T(8,128)(2,1)}, bf16[2048,256]{1,0:T(8,128)(2,1)}, bf16[2048,256]{1,0:T(8,128)(2,1)}, bf16[2048,2048]{1,0:T(8,128)(2,1)}, ...) custom-call(bf16[128,2048]{1,0:T(8,128)(2,1)} %copy-done.22, ...), custom_call_target="tpu_custom_call" | custom-call | tf_op jit(solution)/shard_map/pallas_call | solution.py:330
  829.0 7.2 fusion.118
  839.8 7.6 fusion.121
  (325 shorter events, 104.9 us)
Async XLA Ops:
  7.2 336.6 %copy-start = (bf16[2,384,2048]{2,1,0:T(8,128)(2,1)S(1)}, bf16[2,384,2048]{2,1,0:T(8,128)(2,1)}, u32[]{:S(2)}) copy-start(bf16[2,384,2048]{2,1,0:T(8,128)(2,1)} %param.28) | copy-start | bytes 9437188
  7.2 153.5 %copy-start.88 = (s32[128]{0:T(128)S(1)}, s32[128]{0:T(128)}, u32[]{:S(2)}) copy-start(s32[128]{0:T(128)} %param.16) | copy-start | bytes 1540
  7.2 511.4 %reduce-scatter.5.cloned.1.call-start = ((), (), s32[]{:S(2)}) async-start(), calls=%async_computation.4 | async-start | bytes 8912896 | tf_op jit(solution)/shard_map/reduce_scatter | solution.py:409
  166.0 13.7 %copy-start.41 = (f32[128,2,128]{2,1,0:T(2,128)}, f32[128,2,128]{2,1,0:T(2,128)S(1)}, u32[]{:S(2)}) copy-start(f32[128,2,128]{2,1,0:T(2,128)S(1)} %reshape.353) | copy-start | bytes 393220
  181.1 486.6 %copy-start.48 = (f32[128,16]{1,0:T(8,128)}, f32[128,16]{1,0:T(8,128)S(1)}, u32[]{:S(2)}) copy-start(f32[128,16]{1,0:T(8,128)S(1)} %add_rsqrt_fusion) | copy-start | bytes 24580
  194.5 14.5 %collective-permute-start = (bf16[128,2048]{1,0:T(8,128)(2,1)}, bf16[128,2048]{1,0:T(8,128)(2,1)}, u32[]{:S(2)}, u32[]{:S(2)}) collective-permute-start(bf16[128,2048]{1,0:T(8,128)(2,1)} %convolution_convert_fusion.2), channel_id=1, source_target_pairs={{0,1},{1,0},{2,3},{3,2},{4,5},{5,4},{6,7},{7,6},{8,9},{9,8},{10,11... | collective-permute-start | bytes 1572872 | tf_op jit(solution)/shard_map/ppermute | solution.py:400
  195.7 16.2 %copy-start.67 = (f32[1,2,8,128]{3,1,2,0:T(2,128)}, f32[1,2,8,128]{3,1,2,0:T(2,128)S(1)}, u32[]{:S(2)}) copy-start(f32[1,2,8,128]{3,1,2,0:T(2,128)S(1)} %copy.257) | copy-start | bytes 24580
  197.8 14.1 %copy-start.68 = (pred[128,32]{0,1:T(8,128)(4,1)}, pred[128,32]{0,1:T(8,128)(4,1)S(1)}, u32[]{:S(2)}) copy-start(pred[128,32]{0,1:T(8,128)(4,1)S(1)} %fusion.71) | copy-start | bytes 12292
  198.0 16.6 %copy-start.59 = (pred[128,32]{1,0:T(8,128)(4,1)}, pred[128,32]{1,0:T(8,128)(4,1)S(1)}, u32[]{:S(2)}) copy-start(pred[128,32]{1,0:T(8,128)(4,1)S(1)} %copy.190) | copy-start | bytes 12292
  199.9 12.9 %copy-start.24 = (bf16[2048,32]{1,0:T(8,128)(2,1)S(1)}, bf16[2048,32]{1,0:T(8,128)(2,1)}, u32[]{:S(2)}) copy-start(bf16[2048,32]{1,0:T(8,128)(2,1)} %reshape.358) | copy-start | bytes 393220
  318.1 13.7 %copy-start.17 = (bf16[2,16,64,2048]{3,2,1,0:T(8,128)(2,1)S(1)}, bf16[2,16,64,2048]{3,2,1,0:T(8,128)(2,1)}, u32[]{:S(2)}) copy-start(bf16[2,16,64,2048]{3,2,1,0:T(8,128)(2,1)} %copy.199) | copy-start | bytes 25165828
  318.1 14.9 %copy-start.33 = (bf16[2,2048,384]{2,1,0:T(8,128)(2,1)S(1)}, bf16[2,2048,384]{2,1,0:T(8,128)(2,1)}, u32[]{:S(2)}) copy-start(bf16[2,2048,384]{2,1,0:T(8,128)(2,1)} %param.26) | copy-start | bytes 9437188
  374.5 12.5 %copy-start.2 = (bf16[2,1024,2048]{2,1,0:T(8,128)(2,1)}, bf16[2,1024,2048]{2,1,0:T(8,128)(2,1)S(1)}, u32[]{:S(2)}) copy-start(bf16[2,1024,2048]{2,1,0:T(8,128)(2,1)S(1)} %get-tuple-element.84) | copy-start | bytes 25165828
  374.5 12.5 %copy-start.34 = (bf16[2,2048,384]{2,1,0:T(8,128)(2,1)S(1)}, bf16[2,2048,384]{2,1,0:T(8,128)(2,1)}, u32[]{:S(2)}) copy-start(bf16[2,2048,384]{2,1,0:T(8,128)(2,1)} %param.26) | copy-start | bytes 9437188
  416.5 209.4 %reduce-scatter.3.cloned.1.call-start = ((), (), s32[]{:S(2)}) async-start(), calls=%async_computation.3 | async-start | bytes 8912896 | tf_op jit(solution)/shard_map/reduce_scatter | solution.py:409
  431.1 15.8 %all-to-all-start = ((f32[16,2,128]{2,1,0:T(2,128)}), f32[16,2,128]{2,1,0:T(2,128)S(1)}, u32[]{:S(2)}, u32[]{:S(2)}) async-start(f32[16,2,128]{2,1,0:T(2,128)} %get-tuple-element.49), calls=%async_computation.2 | async-start | bytes 32768 | tf_op jit(solution)/shard_map/all_to_all | solution.py:605
  447.6 83.8 %copy-start.60 = (pred[128,32]{1,0:T(8,128)(4,1)S(1)}, pred[128,32]{1,0:T(8,128)(4,1)}, u32[]{:S(2)}) copy-start(pred[128,32]{1,0:T(8,128)(4,1)} %copy-done.59) | copy-start | bytes 12292
  447.6 179.7 %copy-start.7 = (f32[128,2048]{1,0:T(8,128)S(1)}, f32[128,2048]{1,0:T(8,128)}, u32[]{:S(2)}) copy-start(f32[128,2048]{1,0:T(8,128)} %copy-done.6) | copy-start | bytes 3145732
  447.6 179.7 %copy-start.25 = (bf16[2048,32]{1,0:T(8,128)(2,1)S(1)}, bf16[2048,32]{1,0:T(8,128)(2,1)}, u32[]{:S(2)}) copy-start(bf16[2048,32]{1,0:T(8,128)(2,1)} %reshape.358) | copy-start | bytes 393220
  447.6 83.7 %collective-permute-start.3 = (f32[32,128]{0,1:T(8,128)}, f32[32,128]{0,1:T(8,128)}, u32[]{:S(2)}, u32[]{:S(2)}) collective-permute-start(f32[32,128]{0,1:T(8,128)} %copy.205), channel_id=1, source_target_pairs={{0,1},{1,0},{2,3},{3,2},{4,5},{5,4},{6,7},{7,6},{8,9},{9,8},{10,11... | collective-permute-start | bytes 49160 | tf_op jit(solution)/shard_map/ppermute | solution.py:400
  518.7 108.7 %collective-permute-start.2 = (bf16[128,2048]{1,0:T(8,128)(2,1)}, bf16[128,2048]{1,0:T(8,128)(2,1)}, u32[]{:S(2)}, u32[]{:S(2)}) collective-permute-start(bf16[128,2048]{1,0:T(8,128)(2,1)} %reduce-scatter.5.cloned.1.call-done), channel_id=1, source_target_pairs={{0,1},{1,0},{2,3},{3,2},{4,5},{5,4},{6,7},{7,6},{8,9},{9,8},{10,11... | collective-permute-start | bytes 1572872 | tf_op jit(solution)/shard_map/ppermute | solution.py:400
  531.3 108.0 %copy-start.39 = (bf16[128,2048]{1,0:T(8,128)(2,1)S(1)}, bf16[128,2048]{1,0:T(8,128)(2,1)}, u32[]{:S(2)}) copy-start(bf16[128,2048]{1,0:T(8,128)(2,1)} %refs_5_.1) | copy-start | bytes 1572868
  625.8 13.5 %copy-start.40 = (bf16[128,2048]{1,0:T(8,128)(2,1)S(1)}, bf16[128,2048]{1,0:T(8,128)(2,1)}, u32[]{:S(2)}) copy-start(bf16[128,2048]{1,0:T(8,128)(2,1)} %reduce-scatter.5.cloned.1.call-done) | copy-start | bytes 1572868
  625.8 13.5 %copy-start.57 = (bf16[128,2048]{1,0:T(8,128)(2,1)S(1)}, bf16[128,2048]{1,0:T(8,128)(2,1)}, u32[]{:S(2)}) copy-start(bf16[128,2048]{1,0:T(8,128)(2,1)} %reduce-scatter.3.cloned.1.call-done) | copy-start | bytes 1572868
  625.8 13.5 %collective-permute-start.1 = (bf16[128,2048]{1,0:T(8,128)(2,1)}, bf16[128,2048]{1,0:T(8,128)(2,1)S(1)}, u32[]{:S(2)}, u32[]{:S(2)}) collective-permute-start(bf16[128,2048]{1,0:T(8,128)(2,1)} %reduce-scatter.3.cloned.1.call-done), channel_id=1, source_target_pairs={{0,1},{1,0},{2,3},{3,2},{4,5},{5,4},{6,7},{7,6},{8,9},{9,8},{10,11... | collective-permute-start | bytes 1572872 | tf_op jit(solution)/shard_map/ppermute | solution.py:400
  671.1 9.2 %collective-permute-start.4 = (bf16[128,512]{1,0:T(8,128)(2,1)S(1)}, bf16[128,512]{1,0:T(8,128)(2,1)S(1)}, u32[]{:S(2)}, u32[]{:S(2)}) collective-permute-start(bf16[128,512]{1,0:T(8,128)(2,1)S(1)} %fusion.63), channel_id=1, source_target_pairs={{0,2},{2,0},{1,3},{3,1},{4,6},{6,4},{5,7},{7,5},{8,10},{10,8},{9,1... | collective-permute-start | bytes 393224 | tf_op jit(solution)/shard_map/ppermute | solution.py:400
  682.8 15.4 %copy-start.54 = (bf16[128,256]{1,0:T(8,128)(2,1)}, bf16[128,256]{1,0:T(8,128)(2,1)S(1)}, u32[]{:S(2)}) copy-start(bf16[128,256]{1,0:T(8,128)(2,1)S(1)} %get-tuple-element.73.refs_1_) | copy-start | bytes 196612
  686.3 14.2 %copy-start.26 = (bf16[128,2048]{1,0:T(8,128)(2,1)}, bf16[128,2048]{1,0:T(8,128)(2,1)S(1)}, u32[]{:S(2)}) copy-start(bf16[128,2048]{1,0:T(8,128)(2,1)S(1)} %fusion.13) | copy-start | bytes 1572868
  686.3 14.2 %collective-permute-start.5 = (bf16[128,2048]{1,0:T(8,128)(2,1)S(1)}, bf16[128,2048]{1,0:T(8,128)(2,1)S(1)}, u32[]{:S(2)}, u32[]{:S(2)}) collective-permute-start(bf16[128,2048]{1,0:T(8,128)(2,1)S(1)} %fusion.13), channel_id=1, source_target_pairs={{0,1},{1,0},{2,3},{3,2},{4,5},{5,4},{6,7},{7,6},{8,9},{9,8},{10,11... | collective-permute-start | bytes 1572872 | tf_op jit(solution)/shard_map/ppermute | solution.py:400
  687.9 12.6 %copy-start.11 = (bf16[128,2048]{1,0:T(8,128)(2,1)S(1)}, bf16[128,2048]{1,0:T(8,128)(2,1)}, u32[]{:S(2)}) copy-start(bf16[128,2048]{1,0:T(8,128)(2,1)} %param.15) | copy-start | bytes 1572868
  688.1 12.4 %collective-permute-start.6 = (f32[256]{0:T(256)S(1)}, f32[256]{0:T(256)S(1)}, u32[]{:S(2)}, u32[]{:S(2)}) collective-permute-start(f32[256]{0:T(256)S(1)} %pad_maximum_fusion.7), channel_id=1, source_target_pairs={{0,1},{1,0},{2,3},{3,2},{4,5},{5,4},{6,7},{7,6},{8,9},{9,8},{10,11... | collective-permute-start | bytes 3080 | tf_op jit(solution)/shard_map/ppermute | solution.py:400
  698.2 130.7 %copy-start.13 = (bf16[2048,256]{1,0:T(8,128)(2,1)S(1)}, bf16[2048,256]{1,0:T(8,128)(2,1)}, u32[]{:S(2)}) copy-start(bf16[2048,256]{1,0:T(8,128)(2,1)} %get-tuple-element.38) | copy-start | bytes 3145732
  (68 other events, 318.6 us)
Sparse Core Ops, SparseCore 0:
  416.6 102.0 reduce-scatter.4
  522.7 103.0 reduce-scatter.2

commit v2 on v1

--- a/solution.py
+++ b/solution.py
@@ -37,11 +37,267 @@
         return (2 * nf * rows, cols)
 
 
+def gather_engine(nf, specs, ins, outs, stage, recv, send, local):
+    n = len(specs)
+    nz = nf // 2
+    f, c, t = lax.axis_index("fsdp"), lax.axis_index("ctx"), lax.axis_index("tp")
+    z, x = f // 2, lax.rem(f, 2)
+    has_up, has_down = z + 1 < nz, z > 0
+    device = {
+        UP: (f + 2, c, t),
+        DOWN: (f - 2, c, t),
+        ACROSS: (z * 2 + 1 - x, c, t),
+        PARTNER: (f, 1 - c, t),
+        SIDE: (f, c, 1 - t),
+    }
+    first = [sum(s.chunks for s in specs[:a]) for a in range(n)]
+
+    def src(a, q, dest_f=None):
+        s = specs[a]
+        lo = q * s.step
+        if s.half:
+            lo = c * s.rows + lo
+        if s.form == "a2a":
+            lo = dest_f * (s.rows // nf) + lo
+        return ins[a].at[pl.ds(lo, s.step)]
+
+    def dst(a, q, bf, bc):
+        s = specs[a]
+        if s.form == "col":
+            width = s.shape[1]
+            return outs[a].at[
+                pl.ds(bc * s.rows + q * s.step, s.step),
+                pl.ds(pl.multiple_of(bf * width, width), width),
+            ]
+        rows = s.rows // nf if s.form == "a2a" else s.rows
+        return outs[a].at[pl.ds((bf * 2 + bc) * rows + q * s.step, s.step)]
+
+    def copy(a, q, bf, bc, source, kind, dev=None, slot=None):
+        block = bf * 2 + bc if slot is None else slot
+        return pltpu.make_async_remote_copy(
+            src_ref=source,
+            dst_ref=dst(a, q, bf, bc),
+            send_sem=send.at[kind, block, first[a] + q],
+            recv_sem=recv.at[bf * 2 + bc, first[a] + q],
+            device_id=device[kind] if dev is None else dev,
+            device_id_type=MESH,
+        )
+
+    def in_half(a, q):
+        return (q * 2) // specs[a].chunks == t
+
+    def both(*conds):
+        conds = [k for k in conds if k is not None]
+        if not conds:
+            return None
+        return functools.reduce(lambda u, v: u & v, conds)
+
+    def when(cond, fn):
+        if cond is None:
+            fn()
+        else:
+            pl.when(cond)(fn)
+
+    def go_up(a, q, dist):
+        far = (dist + 1 < nz - 1) | in_half(a, q) if specs[a].rep else None
+        return both(has_up, far)
+
+    def go_down(a, q, dist):
+        far = (dist + 1 < nz - 1) | in_half(a, q) if specs[a].rep else None
+        return both(has_down, far)
+
+    def go_across(a, q):
+        return in_half(a, q) if specs[a].rep else None
+
+    relays = [(a, q) for a in range(n) if specs[a].form != "a2a" for q in range(specs[a].chunks)]
+    direct = [(a, q) for a in range(n) if specs[a].form == "a2a" for q in range(specs[a].chunks)]
+
+    def start():
+        for a, q in relays:
+            source = src(a, q)
+            when(go_up(a, q, 0), lambda: copy(a, q, f, c, source, UP).start())
+            when(go_down(a, q, 0), lambda: copy(a, q, f, c, source, DOWN).start())
+            when(go_across(a, q), lambda: copy(a, q, f, c, source, ACROSS).start())
+            copy(a, q, f, c, source, PARTNER).start()
+        for a in range(n):
+            own_in(a).start()
+        for a in range(n):
+            own_in(a).wait()
+            own_out(a).start()
+
+    def start_direct():
+        for a, q in direct:
+            copy(a, q, f, c, src(a, q, f), PARTNER).start()
+
+            def far_send(d, carry):
+                there = lax.rem(f + d, nf)
+                copy(a, q, f, c, src(a, q, there), UP, dev=(there, c, t), slot=there).start()
+                return carry
+
+            lax.fori_loop(1, nf, far_send, 0)
+
+    def own_in(a):
+        s = specs[a]
+        if s.form == "a2a":
+            view = ins[a].at[pl.ds(f * s.step, s.step)]
+        elif s.half:
+            view = ins[a].at[pl.ds(c * s.rows, s.rows)]
+        else:
+            view = ins[a]
+        return pltpu.make_async_copy(view, stage[a], local.at[0, a])
+
+    def own_out(a):
+        s = specs[a]
+        if s.form == "col":
+            width = s.shape[1]
+            view = outs[a].at[
+                pl.ds(c * s.rows, s.rows), pl.ds(pl.multiple_of(f * width, width), width)
+            ]
+        else:
+            rows = s.rows // nf if s.form == "a2a" else s.rows
+            view = outs[a].at[pl.ds((f * 2 + c) * rows, rows)]
+        return pltpu.make_async_copy(stage[a], view, local.at[1, a])
+
+    def arrived(a, q, bf, bc):
+        copy(a, q, bf, bc, dst(a, q, bf, bc), PARTNER).wait_recv()
+
+    def pass_on(a, q, bf, kind, cond=None):
+        when(cond, lambda: copy(a, q, bf, c, dst(a, q, bf, c), kind).start())
+
+    def column(k):
+        for a, q in relays:
+            rep = specs[a].rep
+            came = ((k < nz - 1) | in_half(a, q)) if rep else None
+            aside = (k == nz - 1) if rep else None
+
+            def below():
+                bf = (z - k) * 2 + x
+                arrived(a, q, bf, c)
+                pass_on(a, q, bf, UP, go_up(a, q, k))
+                pass_on(a, q, bf, ACROSS, go_across(a, q))
+                pass_on(a, q, bf, PARTNER)
+                if rep:
+                    pass_on(a, q, bf, SIDE, aside)
+
+            def above():
+                bf = (z + k) * 2 + x
+                arrived(a, q, bf, c)
+                pass_on(a, q, bf, DOWN, go_down(a, q, k))
+                pass_on(a, q, bf, ACROSS, go_across(a, q))
+                pass_on(a, q, bf, PARTNER)
+                if rep:
+                    pass_on(a, q, bf, SIDE, aside)
+
+            when(both(z - k >= 0, came), below)
+            when(both(z + k < nz, came), above)
+
+    def across(k):
+        for a, q in relays:
+            rep = specs[a].rep
+
+            def take(zz):
+                bf = zz * 2 + 1 - x
+                arrived(a, q, bf, c)
+                pass_on(a, q, bf, PARTNER)
+                if rep:
+                    pass_on(a, q, bf, SIDE)
+
+            mine = in_half(a, q) if rep else None
+            when(both(z - k >= 0, mine), lambda: take(z - k))
+            when(both(z + k < nz, k > 0, mine), lambda: take(z + k))
+
+    def aside(k):
+        for a, q in relays:
+            if not specs[a].rep:
+                continue
+            other = jnp.logical_not(in_half(a, q))
+
+            def take(bf):
+                arrived(a, q, bf, c)
+                pass_on(a, q, bf, PARTNER)
+
+            when((z - k >= 0) & other, lambda: take((z - k) * 2 + 1 - x))
+            when((z + k < nz) & (k > 0) & other, lambda: take((z + k) * 2 + 1 - x))
+            when((z - k >= 0) & (k == nz - 1) & other, lambda: take((z - k) * 2 + x))
+            when((z + k < nz) & (k == nz - 1) & other, lambda: take((z + k) * 2 + x))
+
+    def step(k, carry):
+        column(k)
+        across(k - 1)
+
+        @pl.when(k > 1)
+        def _():
+            aside(k - 2)
+
+        return carry
+
+    def run():
+        lax.fori_loop(1, nz, step, 0)
+        across(nz - 1)
+        if any(s.rep for s in specs):
+            aside(nz - 2)
+            aside(nz - 1)
+
+    def run_direct():
+        for a, q in direct:
+
+            def far_take(d, carry):
+                there = lax.rem(f + nf - d, nf)
+                arrived(a, q, there, c)
+                pass_on(a, q, there, PARTNER)
+                return carry
+
+            lax.fori_loop(1, nf, far_take, 0)
+
+    def take_partner(bf, carry):
+        for a, q in relays:
+            arrived(a, q, bf, 1 - c)
+        return carry
+
+    def land():
+        lax.fori_loop(0, nf, take_partner, 0)
+        for a in range(n):
+            own_out(a).wait()
+
+    def finish(bf, carry):
+        zz, xx = bf // 2, lax.rem(bf, 2)
+        dist = jnp.abs(zz - z)
+        here = xx == x
+        for a, q in relays:
+            rep = specs[a].rep
+            view = dst(a, q, bf, c)
+
+            def sent(kind, cond):
+                when(cond, lambda: copy(a, q, bf, c, view, kind).wait_send())
+
+            half = in_half(a, q) if rep else None
+            by_z = ((dist < nz - 1) | half) if rep else None
+            sent(PARTNER, None)
+            sent(UP, both(here, zz <= z, by_z, go_up(a, q, dist)))
+            sent(DOWN, both(here, zz >= z, by_z, go_down(a, q, dist)))
+            sent(ACROSS, both(here, by_z, go_across(a, q)))
+            if rep:
+                sent(SIDE, half & (jnp.logical_not(here) | (dist == nz - 1)))
+        for a, q in direct:
+            arrived(a, q, bf, 1 - c)
+            view = dst(a, q, bf, c)
+            copy(a, q, bf, c, view, PARTNER).wait_send()
+
+            @pl.when(bf != f)
+            def _():
+                copy(a, q, bf, c, view, UP, slot=bf).wait_send()
+
+        return carry
+
+    def drain():
+        lax.fori_loop(0, nf, finish, 0)
+
+    return start, run, land, start_direct, run_direct, drain
+
+
 def gather_kernel(nf, specs, *refs):
     n = len(specs)
     ins, outs, scratch = refs[:n], refs[n : 2 * n], refs[2 * n :]
-    stage = scratch[:n]
-    recv, send, local = scratch[n:]
     nz = nf // 2
     f, c, t = lax.axis_index("fsdp"), lax.axis_index("ctx"), lax.axis_index("tp")
     z, x = f // 2, lax.rem(f, 2)
@@ -88,251 +344,32 @@
             barrier, greeted + 1 + has_up.astype(jnp.int32) + has_down.astype(jnp.int32)
         )
 
-    first = [sum(s.chunks for s in specs[:a]) for a in range(n)]
-
-    def src(a, q, dest_f=None):
-        s = specs[a]
-        lo = q * s.step
-        if s.half:
-            lo = c * s.rows + lo
-        if s.form == "a2a":
-            lo = dest_f * (s.rows // nf) + lo
-        return ins[a].at[pl.ds(lo, s.step)]
-
-    def dst(a, q, bf, bc):
-        s = specs[a]
-        if s.form == "col":
-            width = s.shape[1]
-            return outs[a].at[
-                pl.ds(bc * s.rows + q * s.step, s.step),
-                pl.ds(pl.multiple_of(bf * width, width), width),
-            ]
-        rows = s.rows // nf if s.form == "a2a" else s.rows
-        return outs[a].at[pl.ds((bf * 2 + bc) * rows + q * s.step, s.step)]
-
-    def copy(a, q, bf, bc, source, kind, dev=None, slot=None):
-        block = bf * 2 + bc if slot is None else slot
-        return pltpu.make_async_remote_copy(
-            src_ref=source,
-            dst_ref=dst(a, q, bf, bc),
-            send_sem=send.at[kind, block, first[a] + q],
-            recv_sem=recv.at[bf * 2 + bc, first[a] + q],
-            device_id=device[kind] if dev is None else dev,
-            device_id_type=MESH,
-        )
-
-    def in_half(a, q):
-        return (q * 2) // specs[a].chunks == t
-
-    def both(*conds):
-        conds = [k for k in conds if k is not None]
-        if not conds:
-            return None
-        return functools.reduce(lambda u, v: u & v, conds)
-
-    def when(cond, fn):
-        if cond is None:
-            fn()
-        else:
-            pl.when(cond)(fn)
-
-    def go_up(a, q, dist):
-        far = (dist + 1 < nz - 1) | in_half(a, q) if specs[a].rep else None
-        return both(has_up, far)
-
-    def go_down(a, q, dist):
-        far = (dist + 1 < nz - 1) | in_half(a, q) if specs[a].rep else None
-        return both(has_down, far)
-
-    def go_across(a, q):
-        return in_half(a, q) if specs[a].rep else None
-
-    relays = [(a, q) for a in range(n) if specs[a].form != "a2a" for q in range(specs[a].chunks)]
-    direct = [(a, q) for a in range(n) if specs[a].form == "a2a" for q in range(specs[a].chunks)]
-
-    for a, q in relays:
-        source = src(a, q)
-        when(go_up(a, q, 0), lambda: copy(a, q, f, c, source, UP).start())
-        when(go_down(a, q, 0), lambda: copy(a, q, f, c, source, DOWN).start())
-        when(go_across(a, q), lambda: copy(a, q, f, c, source, ACROSS).start())
-        copy(a, q, f, c, source, PARTNER).start()
-    for a, q in direct:
-        copy(a, q, f, c, src(a, q, f), PARTNER).start()
-
-        def far_send(d, carry):
-            there = lax.rem(f + d, nf)
-            copy(a, q, f, c, src(a, q, there), UP, dev=(there, c, t), slot=there).start()
-            return carry
-
-        lax.fori_loop(1, nf, far_send, 0)
-
-    def own_in(a):
-        s = specs[a]
-        if s.form == "a2a":
-            view = ins[a].at[pl.ds(f * s.step, s.step)]
-        elif s.half:
-            view = ins[a].at[pl.ds(c * s.rows, s.rows)]
-        else:
-            view = ins[a]
-        return pltpu.make_async_copy(view, stage[a], local.at[0, a])
-
-    def own_out(a):
-        s = specs[a]
-        if s.form == "col":
-            width = s.shape[1]
-            view = outs[a].at[
-                pl.ds(c * s.rows, s.rows), pl.ds(pl.multiple_of(f * width, width), width)
-            ]
-        else:
-            rows = s.rows // nf if s.form == "a2a" else s.rows
-            view = outs[a].at[pl.ds((f * 2 + c) * rows, rows)]
-        return pltpu.make_async_copy(stage[a], view, local.at[1, a])
-
-    for a in range(n):
-        own_in(a).start()
-    for a in range(n):
-        own_in(a).wait()
-        own_out(a).start()
-
-    def arrived(a, q, bf, bc):
-        copy(a, q, bf, bc, dst(a, q, bf, bc), PARTNER).wait_recv()
-
-    def pass_on(a, q, bf, kind, cond=None):
-        when(cond, lambda: copy(a, q, bf, c, dst(a, q, bf, c), kind).start())
-
-    def column(k):
-        for a, q in relays:
-            rep = specs[a].rep
-            came = ((k < nz - 1) | in_half(a, q)) if rep else None
-            aside = (k == nz - 1) if rep else None
-
-            def below():
-                bf = (z - k) * 2 + x
-                arrived(a, q, bf, c)
-                pass_on(a, q, bf, UP, go_up(a, q, k))
-                pass_on(a, q, bf, ACROSS, go_across(a, q))
-                pass_on(a, q, bf, PARTNER)
-                if rep:
-                    pass_on(a, q, bf, SIDE, aside)
-
-            def above():
-                bf = (z + k) * 2 + x
-                arrived(a, q, bf, c)
-                pass_on(a, q, bf, DOWN, go_down(a, q, k))
-                pass_on(a, q, bf, ACROSS, go_across(a, q))
-                pass_on(a, q, bf, PARTNER)
-                if rep:
-                    pass_on(a, q, bf, SIDE, aside)
-
-            when(both(z - k >= 0, came), below)
-            when(both(z + k < nz, came), above)
-
-    def across(k):
-        for a, q in relays:
-            rep = specs[a].rep
-
-            def take(zz):
-                bf = zz * 2 + 1 - x
-                arrived(a, q, bf, c)
-                pass_on(a, q, bf, PARTNER)
-                if rep:
-                    pass_on(a, q, bf, SIDE)
-
-            mine = in_half(a, q) if rep else None
-            when(both(z - k >= 0, mine), lambda: take(z - k))
-            when(both(z + k < nz, k > 0, mine), lambda: take(z + k))
-
-    def aside(k):
-        for a, q in relays:
-            if not specs[a].rep:
-                continue
-            other = jnp.logical_not(in_half(a, q))
-
-            def take(bf):
-                arrived(a, q, bf, c)
-                pass_on(a, q, bf, PARTNER)
-
-            when((z - k >= 0) & other, lambda: take((z - k) * 2 + 1 - x))
-            when((z + k < nz) & (k > 0) & other, lambda: take((z + k) * 2 + 1 - x))
-            when((z - k >= 0) & (k == nz - 1) & other, lambda: take((z - k) * 2 + x))
-            when((z + k < nz) & (k == nz - 1) & other, lambda: take((z + k) * 2 + x))
-
-    def step(k, carry):
-        column(k)
-        across(k - 1)
-
-        @pl.when(k > 1)
-        def _():
-            aside(k - 2)
-
-        return carry
-
-    lax.fori_loop(1, nz, step, 0)
-    across(nz - 1)
-    if any_rep:
-        aside(nz - 2)
-        aside(nz - 1)
-
-    for a, q in direct:
-
-        def far_take(d, carry):
-            there = lax.rem(f + nf - d, nf)
-            arrived(a, q, there, c)
-            pass_on(a, q, there, PARTNER)
-            return carry
-
-        lax.fori_loop(1, nf, far_take, 0)
-
-    def finish(bf, carry):
-        zz, xx = bf // 2, lax.rem(bf, 2)
-        dist = jnp.abs(zz - z)
-        here = xx == x
-        for a, q in relays:
-            rep = specs[a].rep
-            arrived(a, q, bf, 1 - c)
-            view = dst(a, q, bf, c)
-
-            def sent(kind, cond):
-                when(cond, lambda: copy(a, q, bf, c, view, kind).wait_send())
-
-            half = in_half(a, q) if rep else None
-            by_z = ((dist < nz - 1) | half) if rep else None
-            sent(PARTNER, None)
-            sent(UP, both(here, zz <= z, by_z, go_up(a, q, dist)))
-            sent(DOWN, both(here, zz >= z, by_z, go_down(a, q, dist)))
-            sent(ACROSS, both(here, by_z, go_across(a, q)))
-            if rep:
-                sent(SIDE, half & (jnp.logical_not(here) | (dist == nz - 1)))
-        for a, q in direct:
-            arrived(a, q, bf, 1 - c)
-            view = dst(a, q, bf, c)
-            copy(a, q, bf, c, view, PARTNER).wait_send()
-
-            @pl.when(bf != f)
-            def _():
-                copy(a, q, bf, c, view, UP, slot=bf).wait_send()
-
-        return carry
-
-    lax.fori_loop(0, nf, finish, 0)
-    for a in range(n):
-        own_out(a).wait()
+    start, run, land, start_direct, run_direct, drain = gather_engine(
+        nf, specs, ins, outs, scratch[:n], *scratch[n:]
+    )
+    start()
+    start_direct()
+    run()
+    run_direct()
+    land()
+    drain()
+
+
+def stage_of(s, nf):
+    rows = s.rows // nf if s.form == "a2a" else s.rows
+    return pltpu.VMEM((rows, s.shape[1]), s.array.dtype)
 
 
 def plane_gather(specs, collective_id, nf):
     n = len(specs)
     total = sum(s.chunks for s in specs)
-
-    def stage_of(s):
-        rows = s.rows // nf if s.form == "a2a" else s.rows
-        return pltpu.VMEM((rows, s.shape[1]), s.array.dtype)
 
     return pl.pallas_call(
         functools.partial(gather_kernel, nf, tuple(specs)),
         out_shape=tuple(jax.ShapeDtypeStruct(s.out_shape(nf), s.array.dtype) for s in specs),
         in_specs=[pl.BlockSpec(memory_space=pl.ANY)] * n,
         out_specs=tuple(pl.BlockSpec(memory_space=pl.ANY) for _ in specs),
-        scratch_shapes=[stage_of(s) for s in specs]
+        scratch_shapes=[stage_of(s, nf) for s in specs]
         + [
             pltpu.SemaphoreType.DMA((2 * nf, total)),
             pltpu.SemaphoreType.DMA((5, 2 * nf, total)),
@@ -342,6 +379,553 @@
             collective_id=collective_id, has_side_effects=True
         ),
     )(*[s.array for s in specs])
+
+
+CUT = 4
+
+
+def expert_kernel(nf, capacity, specs, *refs):
+    n = len(specs)
+    ins, refs = refs[:n], refs[n:]
+    (grad_all, wg_hbm, wu_hbm, wd_hbm), refs = refs[:4], refs[4:]
+    gathered, refs = refs[:n], refs[n:]
+    (out_part, xs_out, de_out, act_out, dg_out, du_out, grad_tok, prob_tok), refs = (
+        refs[:8],
+        refs[8:],
+    )
+    stage, refs = refs[:n], refs[n:]
+    (recv, send, local), refs = refs[:3], refs[3:]
+    (
+        wg,
+        wu,
+        wd,
+        x_buf,
+        y_buf,
+        xs,
+        ys,
+        de,
+        pe,
+        bs,
+        act,
+        dg,
+        du,
+        w_slot,
+        dp_slot,
+        pick,
+        mk,
+        rk,
+        y_out,
+        part,
+        from_partner,
+        from_across,
+        from_z,
+        from_side,
+        dp_send,
+        dp_recv,
+        dp_side,
+        marks_v,
+        w_sem,
+        load_sem,
+        store_sem,
+        p_send,
+        p_recv,
+        x_send,
+        x_recv,
+        z_send,
+        z_recv,
+        s_send,
+        s_recv,
+        d_send,
+        d_recv,
+    ) = refs
+    f32, bf16 = jnp.float32, jnp.bfloat16
+    nz = nf // 2
+    f, c, t = lax.axis_index("fsdp"), lax.axis_index("ctx"), lax.axis_index("tp")
+    z, x = f // 2, lax.rem(f, 2)
+    me = f * 2 + c
+    up, down = (f + 2, c, t), (f - 2, c, t)
+    across_dev, partner, side = (z * 2 + 1 - x, c, t), (f, 1 - c, t), (f, c, 1 - t)
+    has_up, has_down = z + 1 < nz, z > 0
+    tokens = x_buf.shape[0] // 4
+    width = x_buf.shape[1]
+    slots = 2 * capacity
+    rows_unit = 4 * capacity
+    hidden = wg.shape[2]
+    experts = specs[1].shape[0]
+    step_rows = tokens // CUT
+
+    barrier = pltpu.get_barrier_semaphore()
+
+    def greet(d, carry):
+        there = lax.rem(me + d, 2 * nf)
+        pl.semaphore_signal(
+            barrier, 1, device_id=(there // 2, lax.rem(there, 2), t), device_id_type=MESH
+        )
+        return carry
+
+    lax.fori_loop(1, 2 * nf, greet, 0)
+    pl.semaphore_signal(barrier, 1, device_id=side, device_id_type=MESH)
+    pl.semaphore_wait(barrier, 2 * nf)
+
+    start, run, land, start_direct, run_direct, drain = gather_engine(
+        nf, specs, ins, gathered, stage, recv, send, local
+    )
+    start()
+    weight_loads = [
+        pltpu.make_async_copy(src, dst, w_sem.at[i])
+        for i, (src, dst) in enumerate(((wg_hbm, wg), (wu_hbm, wu), (wd_hbm, wd)))
+    ]
+    for load in weight_loads:
+        load.start()
+
+    order = 0
+    for at, seq in enumerate(visiting_order(nz)):
+        code = sum(u * nz**i for i, u in enumerate(seq))
+        order = order + code * (z == at).astype(jnp.int32)
+
+    def unit_at(i):
+        code = order
+        for k in range(nz):
+            code = jnp.where(i > k, code // nz, code)
+        return lax.rem(code, nz)
+
+    def load_rows(u, which):
+        rows = pl.ds(pl.multiple_of(u * 4 * tokens, 4 * tokens), 4 * tokens)
+        if which == 0:
+            return pltpu.make_async_copy(gathered[0].at[rows], x_buf, load_sem.at[0])
+        return pltpu.make_async_copy(grad_all.at[rows], y_buf, load_sem.at[1])
+
+    load_rows(unit_at(0), 1).start()
+    run()
+    land()
+    start_direct()
+    load_rows(unit_at(0), 0).start()
+    marks_in = pltpu.make_async_copy(gathered[1], marks_v, load_sem.at[2])
+    marks_in.start()
+    marks_in.wait()
+    dp_send[...] = jnp.zeros_like(dp_send)
+    first_expert = me * 2
+    for b in range(2 * nf):
+        for j in range(2):
+            mk[2 * b + j : 2 * b + j + 1, :] = marks_v[pl.ds(b * experts + first_expert + j, 1), :]
+    taken = jnp.where(mk[...] >= 0.0, 1.0, 0.0).astype(bf16)
+    before = lax.broadcasted_iota(jnp.int32, (tokens, tokens), 0)
+    after = lax.broadcasted_iota(jnp.int32, (tokens, tokens), 1)
+    upper = jnp.where(before <= after, 1.0, 0.0).astype(bf16)
+    rk[...] = jnp.dot(taken, upper, preferred_element_type=f32) - 1.0
+    for load in weight_loads:
+        load.wait()
+
+    def store_unit(u):
+        rows = pl.ds(pl.multiple_of(u * rows_unit, rows_unit), rows_unit)
+        pairs = [(xs, xs_out), (de, de_out), (act, act_out), (dg, dg_out), (du, du_out)]
+        copies = [
+            pltpu.make_async_copy(src, dst.at[:, rows], store_sem.at[i])
+            for i, (src, dst) in enumerate(pairs)
+        ]
+        out_rows = pl.ds(pl.multiple_of(u * 4 * tokens, 4 * tokens), 4 * tokens)
+        copies.append(pltpu.make_async_copy(y_out, out_part.at[out_rows], store_sem.at[5]))
+        return copies
+
+    def chunk(q):
+        return pl.ds(q * step_rows, step_rows)
+
+    def p_copy(u, xx, q):
+        return pltpu.make_async_remote_copy(
+            src_ref=part.at[u * 4 + xx * 2 + 1 - c, chunk(q)],
+            dst_ref=from_partner.at[u * 2 + xx, chunk(q)],
+            send_sem=p_send.at[u * 2 + xx, q],
+            recv_sem=p_recv.at[u * 2 + xx, q],
+            device_id=partner,
+            device_id_type=MESH,
+        )
+
+    def x_copy(u, q):
+        return pltpu.make_async_remote_copy(
+            src_ref=part.at[u * 4 + (1 - x) * 2 + c, chunk(q)],
+            dst_ref=from_across.at[u, chunk(q)],
+            send_sem=x_send.at[u, q],
+            recv_sem=x_recv.at[u, q],
+            device_id=across_dev,
+            device_id_type=MESH,
+        )
+
+    def z_copy(u, q, way):
+        return pltpu.make_async_remote_copy(
+            src_ref=part.at[u * 4 + x * 2 + c, chunk(q)],
+            dst_ref=from_z.at[way, u, chunk(q)],
+            send_sem=z_send.at[u, q],
+            recv_sem=z_recv.at[way, u, q],
+            device_id=up if way == 0 else down,
+            device_id_type=MESH,
+        )
+
+    def z_wait(u, q, way):
+        pltpu.make_async_remote_copy(
+            src_ref=part.at[me, chunk(q)],
+            dst_ref=from_z.at[way, u, chunk(q)],
+            send_sem=z_send.at[u, q],
+            recv_sem=z_recv.at[way, u, q],
+            device_id=partner,
+            device_id_type=MESH,
+        ).wait_recv()
+
+    def s_copy(q):
+        return pltpu.make_async_remote_copy(
+            src_ref=part.at[me, chunk(q)],
+            dst_ref=from_side.at[chunk(q)],
+            send_sem=s_send.at[q],
+            recv_sem=s_recv.at[q],
+            device_id=side,
+            device_id_type=MESH,
+        )
+
+    def d_copy(b, source=None):
+        return pltpu.make_async_remote_copy(
+            src_ref=dp_send.at[b],
+            dst_ref=dp_recv.at[me if source is None else source],
+            send_sem=d_send.at[b],
+            recv_sem=d_recv.at[me if source is None else source],
+            device_id=(b // 2, lax.rem(b, 2), t),
+            device_id_type=MESH,
+        )
+
+    def compute(i, u):
+        load_rows(u, 0).wait()
+        load_rows(u, 1).wait()
+
+        @pl.when(i > 0)
+        def _():
+            for cp in store_unit(unit_at(i - 1)):
+                cp.wait()
+
+        slot_ids = lax.broadcasted_iota(jnp.int32, (capacity, tokens), 0).astype(f32)
+        for b in range(4):
+            for j in range(2):
+                row = pl.ds(2 * (u * 4 + b) + j, 1)
+                mark = mk[row, :]
+                hit = (rk[row, :] == slot_ids) & (mark >= 0.0)
+                pick[b, j * capacity : (j + 1) * capacity, :] = jnp.where(hit, 1.0, 0.0)
+                w_slot[j, b * capacity : (b + 1) * capacity, :] = jnp.sum(
+                    jnp.where(hit, mark, 0.0), axis=1, keepdims=True
+                )
+        tile = 512
+        for b in range(4):
+            chosen = pick[b].astype(bf16)
+            for k in range(width // tile):
+                cols = slice(k * tile, (k + 1) * tile)
+                got = jnp.dot(
+                    chosen, x_buf[b * tokens : (b + 1) * tokens, cols], preferred_element_type=f32
+                ).astype(bf16)
+                gy = jnp.dot(
+                    chosen, y_buf[b * tokens : (b + 1) * tokens, cols], preferred_element_type=f32
+                )
+                for j in range(2):
+                    to = slice(b * capacity, (b + 1) * capacity)
+                    of = slice(j * capacity, (j + 1) * capacity)
+                    xs[j, to, cols] = got[of]
+                    ys[j, to, cols] = gy[of].astype(bf16)
+                    de[j, to, cols] = (w_slot[j, to, :] * gy[of]).astype(bf16)
+
+        @pl.when(i + 1 < nz)
+        def _():
+            load_rows(unit_at(i + 1), 0).start()
+            load_rows(unit_at(i + 1), 1).start()
+
+        def expert(j, carry):
+            gate = jnp.dot(xs[j], wg[j], preferred_element_type=f32)
+            upv = jnp.dot(xs[j], wu[j], preferred_element_type=f32)
+            sig = 1.0 / (1.0 + jnp.exp(-gate))
+            silu = gate * sig
+            act[j] = (silu * upv).astype(bf16)
+            grad_act = lax.dot_general(
+                de[j], wd[j], (((1,), (1,)), ((), ())), preferred_element_type=f32
+            )
+            dg[j] = (grad_act * upv * (sig * (1.0 + gate * (1.0 - sig)))).astype(bf16)
+            du[j] = (grad_act * silu).astype(bf16)
+            total = jnp.zeros((rows_unit, 1), f32)
+            for k in range(width // tile):
+                cols = slice(k * tile, (k + 1) * tile)
+                made = jnp.dot(act[j], wd[j, :, cols], preferred_element_type=f32)
+                made = made.astype(bf16).astype(f32)
+                total = total + jnp.sum(made * ys[j, :, cols].astype(f32), axis=1, keepdims=True)
+                weighted = (w_slot[j] * made).astype(bf16)
+                back = lax.dot_general(
+                    dg[j], wg[j, cols, :], (((1,), (1,)), ((), ())), preferred_element_type=f32
+                ) + lax.dot_general(
+                    du[j], wu[j, cols, :], (((1,), (1,)), ((), ())), preferred_element_type=f32
+                )
+                back = back.astype(bf16)
+                for b in range(4):
+                    of = slice(b * capacity, (b + 1) * capacity)
+                    to = pl.ds(pl.multiple_of(j * capacity, capacity), capacity)
+                    pe[b, to, cols] = weighted[of]
+                    bs[b, to, cols] = back[of]
+            for b in range(4):
+                to = pl.ds(pl.multiple_of(j * capacity, capacity), capacity)
+                dp_slot[b, to, :] = total[b * capacity : (b + 1) * capacity]
+            return carry
+
+        lax.fori_loop(0, 2, expert, 0)
+
+        def spread(b):
+            chosen = pick[b]
+            back = jnp.transpose(chosen).astype(bf16)
+            for k in range(width // tile):
+                cols = slice(k * tile, (k + 1) * tile)
+                part[u * 4 + b, :, cols] = jnp.dot(
+                    back, bs[b, :, cols], preferred_element_type=f32
+                ).astype(bf16)
+
+        for b in range(4):
+            spread(b)
+        for xx in range(2):
+            for q in range(CUT):
+                p_copy(u, xx, q).start()
+        for b in range(4):
+            back = jnp.transpose(pick[b]).astype(bf16)
+            for k in range(width // tile):
+                cols = slice(k * tile, (k + 1) * tile)
+                y_out[b * tokens : (b + 1) * tokens, cols] = jnp.dot(
+                    back, pe[b, :, cols], preferred_element_type=f32
+                ).astype(bf16)
+            for j in range(2):
+                of = slice(j * capacity, (j + 1) * capacity)
+                dp_send[u * 4 + b, j : j + 1, :] = jnp.sum(
+                    pick[b, of, :] * dp_slot[b, of, :], axis=0, keepdims=True
+                )
+        for cp in store_unit(u):
+            cp.start()
+        for b in range(4):
+            bb = u * 4 + b
+
+            @pl.when(bb != me)
+            def _():
+                d_copy(bb).start()
+
+    def wide(ref):
+        return ref.astype(f32)
+
+    def to_across(u):
+        for q in range(CUT):
+            for xx in range(2):
+                p_copy(u, xx, q).wait_recv()
+            blk = u * 4 + (1 - x) * 2 + c
+            part[blk, chunk(q)] = (
+                wide(part[blk, chunk(q)]) + wide(from_partner[u * 2 + 1 - x, chunk(q)])
+            ).astype(bf16)
+            x_copy(u, q).start()
+
+    def along(u):
+        blk = u * 4 + x * 2 + c
+        for q in range(CUT):
+            x_copy(u, q).wait_recv()
+
+            def total():
+                return (
+                    wide(part[blk, chunk(q)])
+                    + wide(from_partner[u * 2 + x, chunk(q)])
+                    + wide(from_across[u, chunk(q)])
+                )
+
+            def hop(way, has_before):
+                @pl.when(has_before)
+                def _():
+                    z_wait(u, q, way)
+                    part[blk, chunk(q)] = (total() + wide(from_z[way, u, chunk(q)])).astype(bf16)
+
+                @pl.when(jnp.logical_not(has_before))
+                def _():
+                    part[blk, chunk(q)] = total().astype(bf16)
+
+                z_copy(u, q, way).start()
+
+            @pl.when(u > z)
+            def _():
+                hop(0, has_down)
+
+            @pl.when(u < z)
+            def _():
+                hop(1, has_up)
+
+            @pl.when(u == z)
+            def _():
+                grad_tok[chunk(q)] = total()
+
+                @pl.when(has_down)
+                def _():
+                    z_wait(u, q, 0)
+                    grad_tok[chunk(q)] = grad_tok[chunk(q)] + wide(from_z[0, u, chunk(q)])
+
+                @pl.when(has_up)
+                def _():
+                    z_wait(u, q, 1)
+                    grad_tok[chunk(q)] = grad_tok[chunk(q)] + wide(from_z[1, u, chunk(q)])
+
+                part[blk, chunk(q)] = grad_tok[chunk(q)].astype(bf16)
+                s_copy(q).start()
+
+    def unit(i, carry):
+        u = unit_at(i)
+        compute(i, u)
+
+        @pl.when(i > 0)
+        def _():
+            along(unit_at(i - 1))
+
+        to_across(u)
+        return carry
+
+    lax.fori_loop(0, nz, unit, 0)
+    along(z)
+
+    dp_recv[me] = dp_send[me]
+
+    def take_prob(d, carry):
+        d_copy(me, lax.rem(me + d, 2 * nf)).wait_recv()
+        return carry
+
+    lax.fori_loop(1, 2 * nf, take_prob, 0)
+    swap_prob = pltpu.make_async_remote_copy(
+        src_ref=dp_recv,
+        dst_ref=dp_side,
+        send_sem=s_send.at[CUT],
+        recv_sem=s_recv.at[CUT],
+        device_id=side,
+        device_id_type=MESH,
+    )
+    swap_prob.start()
+    run_direct()
+    for q in range(CUT):
+        s_copy(q).wait_recv()
+        grad_tok[chunk(q)] = wide(part[me, chunk(q)]) + wide(from_side[chunk(q)])
+    swap_prob.wait_recv()
+    prob_tok[...] = dp_recv[...] + dp_side[...]
+
+    for cp in store_unit(z):
+        cp.wait()
+    swap_prob.wait_send()
+
+    def ends(u, carry):
+        for q in range(CUT):
+            for xx in range(2):
+                p_copy(u, xx, q).wait_send()
+            x_copy(u, q).wait_send()
+
+            @pl.when(u > z)
+            def _():
+                z_copy(u, q, 0).wait_send()
+
+            @pl.when(u < z)
+            def _():
+                z_copy(u, q, 1).wait_send()
+
+        for b in range(4):
+
+            @pl.when(u * 4 + b != me)
+            def _():
+                d_copy(u * 4 + b).wait_send()
+
+        return carry
+
+    lax.fori_loop(0, nz, ends, 0)
+    for q in range(CUT):
+        s_copy(q).wait_send()
+
+    drain()
+
+
+def visiting_order(nz):
+    rows = []
+    for at in range(nz):
+        rows.append(sorted(range(nz), key=lambda u: (-abs(u - at), u if at < nz // 2 else -u)))
+    return rows
+
+
+def expert_pass(hidden_two, marks, hidden_slices, grad_all, w_gate, w_up, w_down, capacity, nf):
+    specs = [
+        Gather(hidden_two, nf, rep=True, chunks=4),
+        Gather(marks, nf, chunks=1),
+        Gather(hidden_slices, nf, form="a2a", chunks=1),
+    ]
+    n = len(specs)
+    f32, bf16 = jnp.float32, jnp.bfloat16
+    tokens, width = hidden_two.shape
+    nz = nf // 2
+    total = sum(s.chunks for s in specs)
+    hidden = w_gate.shape[2]
+    rows = 2 * nf * capacity
+    unit_rows = 4 * capacity
+    slots = 2 * capacity
+    any_spec = pl.BlockSpec(memory_space=pl.ANY)
+    vmem = pl.BlockSpec(memory_space=pltpu.VMEM)
+    dma = pltpu.SemaphoreType.DMA
+    outs = [jax.ShapeDtypeStruct(s.out_shape(nf), s.array.dtype) for s in specs] + [
+        jax.ShapeDtypeStruct((2 * nf * tokens, width), bf16),
+        jax.ShapeDtypeStruct((2, rows, width), bf16),
+        jax.ShapeDtypeStruct((2, rows, width), bf16),
+        jax.ShapeDtypeStruct((2, rows, hidden), bf16),
+        jax.ShapeDtypeStruct((2, rows, hidden), bf16),
+        jax.ShapeDtypeStruct((2, rows, hidden), bf16),
+        jax.ShapeDtypeStruct((tokens, width), f32),
+        jax.ShapeDtypeStruct((2 * nf, 8, tokens), f32),
+    ]
+    result = pl.pallas_call(
+        functools.partial(expert_kernel, nf, capacity, tuple(specs)),
+        out_shape=tuple(outs),
+        in_specs=[any_spec] * (n + 4),
+        out_specs=tuple([any_spec] * (n + 6) + [vmem, vmem]),
+        scratch_shapes=[stage_of(s, nf) for s in specs]
+        + [dma((2 * nf, total)), dma((5, 2 * nf, total)), dma((2, n))]
+        + [
+            pltpu.VMEM(w_gate.shape, bf16),
+            pltpu.VMEM(w_up.shape, bf16),
+            pltpu.VMEM(w_down.shape, bf16),
+            pltpu.VMEM((4 * tokens, width), bf16),
+            pltpu.VMEM((4 * tokens, width), bf16),
+            pltpu.VMEM((2, unit_rows, width), bf16),
+            pltpu.VMEM((2, unit_rows, width), bf16),
+            pltpu.VMEM((2, unit_rows, width), bf16),
+            pltpu.VMEM((4, slots, width), bf16),
+            pltpu.VMEM((4, slots, width), bf16),
+            pltpu.VMEM((2, unit_rows, hidden), bf16),
+            pltpu.VMEM((2, unit_rows, hidden), bf16),
+            pltpu.VMEM((2, unit_rows, hidden), bf16),
+            pltpu.VMEM((2, unit_rows, 1), f32),
+            pltpu.VMEM((4, slots, 1), f32),
+            pltpu.VMEM((4, slots, tokens), f32),
+            pltpu.VMEM((4 * nf, tokens), f32),
+            pltpu.VMEM((4 * nf, tokens), f32),
+            pltpu.VMEM((4 * tokens, width), bf16),
+            pltpu.VMEM((2 * nf, tokens, width), bf16),
+            pltpu.VMEM((nf, tokens, width), bf16),
+            pltpu.VMEM((nz, tokens, width), bf16),
+            pltpu.VMEM((2, nz, tokens, width), bf16),
+            pltpu.VMEM((tokens, width), bf16),
+            pltpu.VMEM((2 * nf, 8, tokens), f32),
+            pltpu.VMEM((2 * nf, 8, tokens), f32),
+            pltpu.VMEM((2 * nf, 8, tokens), f32),
+            pltpu.VMEM(specs[1].out_shape(nf), f32),
+            dma((3,)),
+            dma((3,)),
+            dma((6,)),
+            dma((nf, CUT)),
+            dma((nf, CUT)),
+            dma((nz, CUT)),
+            dma((nz, CUT)),
+            dma((nz, CUT)),
+            dma((2, nz, CUT)),
+            dma((CUT + 1,)),
+            dma((CUT + 1,)),
+            dma((2 * nf,)),
+            dma((2 * nf,)),
+        ],
+        compiler_params=pltpu.CompilerParams(
+            collective_id=7, has_side_effects=True, vmem_limit_bytes=67043328
+        ),
+    )(*[s.array for s in specs], grad_all, w_gate, w_up, w_down)
+    hidden_all, _, hidden_slice = result[:3]
+    return (hidden_all, hidden_slice) + tuple(result[3:])
 
 
 def norm_forward(values, gain_row):
@@ -534,79 +1118,106 @@
     probs = raised / jnp.sum(raised, axis=1, keepdims=True)
     marks = jnp.where(routed, probs, -1.0).T
 
-    hidden_all, marks_all, hidden_first_slice = plane_gather(
-        [
-            Gather(hidden_two, nf, rep=True, chunks=4),
-            Gather(marks, nf, chunks=1),
-            Gather(by_shard(hidden_first, nf), nf, form="a2a", chunks=1),
-        ],
-        2,
-        nf,
-    )
-    first_expert = (f_index * 2 + c_index) * local_experts
-    marks_here = lax.dynamic_slice_in_dim(
-        marks_all.reshape(devices, experts, tokens_dev), first_expert, local_experts, axis=1
-    )
-    taken = marks_here >= 0.0
-    ranks = jnp.cumsum(taken.astype(jnp.int32), axis=2) - 1
-    slots = jnp.arange(capacity, dtype=jnp.int32)
-    chosen = taken[:, :, None, :] & (ranks[:, :, None, :] == slots[None, None, :, None])
-    pick = chosen.astype(bf16)
-    weight_slot = jnp.sum(jnp.where(chosen, marks_here[:, :, None, :], 0.0), axis=3)
-    weight_slot = weight_slot.transpose(1, 0, 2).reshape(local_experts, devices * capacity)
-
-    def select(rows):
-        blocks = rows.reshape(devices, tokens_dev, width_dim)
-        out = jnp.einsum("bjst,btd->jbsd", pick, blocks, preferred_element_type=f32)
-        return out.astype(bf16).reshape(local_experts, devices * capacity, width_dim)
-
-    def spread(rows):
-        blocks = rows.reshape(local_experts, devices, capacity, width_dim)
-        out = jnp.einsum("bjst,jbsd->btd", pick, blocks, preferred_element_type=f32)
-        return out.astype(bf16).reshape(devices * tokens_dev, width_dim)
-
-    rows_in = select(hidden_all)
-    grad_rows_in = select(grad_all)
-    gate_pre = jnp.einsum("jrd,jdf->jrf", rows_in, w_gate, preferred_element_type=f32)
-    up_pre = jnp.einsum("jrd,jdf->jrf", rows_in, w_up, preferred_element_type=f32)
-    sigmoid_gate = jax.nn.sigmoid(gate_pre)
-    silu_gate = gate_pre * sigmoid_gate
-    activated = (silu_gate * up_pre).astype(bf16)
-    produced = jnp.einsum("jrf,jfd->jrd", activated, w_down, preferred_element_type=f32).astype(
-        bf16
-    )
-    wide = produced.astype(f32)
-    grad_prob_slot = jnp.sum(wide * grad_rows_in.astype(f32), axis=2)
-    grad_prob_part = jnp.sum(
-        jnp.where(
-            chosen,
-            grad_prob_slot.reshape(local_experts, devices, capacity).transpose(1, 0, 2)[..., None],
-            0.0,
-        ),
-        axis=2,
-    )
-    moe_partial = spread((weight_slot[:, :, None] * wide).astype(bf16))
-    grad_prod = (weight_slot[:, :, None] * grad_rows_in.astype(f32)).astype(bf16)
-    grad_act = jnp.einsum("jrd,jfd->jrf", grad_prod, w_down, preferred_element_type=f32)
-    grad_gate_pre = (
-        grad_act * up_pre * (sigmoid_gate * (1.0 + gate_pre * (1.0 - sigmoid_gate)))
-    ).astype(bf16)
-    grad_up_pre = (grad_act * silu_gate).astype(bf16)
-    grad_slots = jnp.einsum("jrf,jdf->jrd", grad_gate_pre, w_gate, preferred_element_type=f32)
-    grad_slots = (
-        grad_slots + jnp.einsum("jrf,jdf->jrd", grad_up_pre, w_up, preferred_element_type=f32)
-    ).astype(bf16)
-    hidden_grad_partial = spread(grad_slots)
+    if nf == 8:
+        (
+            hidden_all,
+            hidden_first_slice,
+            moe_partial,
+            rows_in,
+            grad_prod,
+            activated,
+            grad_gate_pre,
+            grad_up_pre,
+            grad_hidden_moe,
+            grad_prob,
+        ) = expert_pass(
+            hidden_two,
+            marks,
+            by_shard(hidden_first, nf),
+            grad_all,
+            w_gate,
+            w_up,
+            w_down,
+            capacity,
+            nf,
+        )
+        grad_prob = grad_prob.reshape(devices, 8, tokens_dev)[:, :local_experts]
+        grad_prob = grad_prob.reshape(experts, tokens_dev).T
+    else:
+        hidden_all, marks_all, hidden_first_slice = plane_gather(
+            [
+                Gather(hidden_two, nf, rep=True, chunks=4),
+                Gather(marks, nf, chunks=1),
+                Gather(by_shard(hidden_first, nf), nf, form="a2a", chunks=1),
+            ],
+            2,
+            nf,
+        )
+        first_expert = (f_index * 2 + c_index) * local_experts
+        marks_here = lax.dynamic_slice_in_dim(
+            marks_all.reshape(devices, experts, tokens_dev), first_expert, local_experts, axis=1
+        )
+        taken = marks_here >= 0.0
+        ranks = jnp.cumsum(taken.astype(jnp.int32), axis=2) - 1
+        slots = jnp.arange(capacity, dtype=jnp.int32)
+        chosen = taken[:, :, None, :] & (ranks[:, :, None, :] == slots[None, None, :, None])
+        pick = chosen.astype(bf16)
+        weight_slot = jnp.sum(jnp.where(chosen, marks_here[:, :, None, :], 0.0), axis=3)
+        weight_slot = weight_slot.transpose(1, 0, 2).reshape(local_experts, devices * capacity)
+
+        def select(rows):
+            blocks = rows.reshape(devices, tokens_dev, width_dim)
+            out = jnp.einsum("bjst,btd->jbsd", pick, blocks, preferred_element_type=f32)
+            return out.astype(bf16).reshape(local_experts, devices * capacity, width_dim)
+
+        def spread(rows):
+            blocks = rows.reshape(local_experts, devices, capacity, width_dim)
+            out = jnp.einsum("bjst,jbsd->btd", pick, blocks, preferred_element_type=f32)
+            return out.astype(bf16).reshape(devices * tokens_dev, width_dim)
+
+        rows_in = select(hidden_all)
+        grad_rows_in = select(grad_all)
+        gate_pre = jnp.einsum("jrd,jdf->jrf", rows_in, w_gate, preferred_element_type=f32)
+        up_pre = jnp.einsum("jrd,jdf->jrf", rows_in, w_up, preferred_element_type=f32)
+        sigmoid_gate = jax.nn.sigmoid(gate_pre)
+        silu_gate = gate_pre * sigmoid_gate
+        activated = (silu_gate * up_pre).astype(bf16)
+        produced = jnp.einsum("jrf,jfd->jrd", activated, w_down, preferred_element_type=f32).astype(
+            bf16
+        )
+        wide = produced.astype(f32)
+        grad_prob_slot = jnp.sum(wide * grad_rows_in.astype(f32), axis=2)
+        grad_prob_part = jnp.sum(
+            jnp.where(
+                chosen,
+                grad_prob_slot.reshape(local_experts, devices, capacity).transpose(1, 0, 2)[..., None],
+                0.0,
+            ),
+            axis=2,
+        )
+        moe_partial = spread((weight_slot[:, :, None] * wide).astype(bf16))
+        grad_prod = (weight_slot[:, :, None] * grad_rows_in.astype(f32)).astype(bf16)
+        grad_act = jnp.einsum("jrd,jfd->jrf", grad_prod, w_down, preferred_element_type=f32)
+        grad_gate_pre = (
+            grad_act * up_pre * (sigmoid_gate * (1.0 + gate_pre * (1.0 - sigmoid_gate)))
+        ).astype(bf16)
+        grad_up_pre = (grad_act * silu_gate).astype(bf16)
+        grad_slots = jnp.einsum("jrf,jdf->jrd", grad_gate_pre, w_gate, preferred_element_type=f32)
+        grad_slots = (
+            grad_slots + jnp.einsum("jrf,jdf->jrd", grad_up_pre, w_up, preferred_element_type=f32)
+        ).astype(bf16)
+        hidden_grad_partial = spread(grad_slots)
+
+        grad_hidden_moe = sum_over_tp(block_sum(hidden_grad_partial, nf))
+        grad_prob = lax.all_to_all(
+            grad_prob_part, ("fsdp", "ctx"), split_axis=0, concat_axis=0, tiled=True
+        ).reshape(experts, tokens_dev)
+        grad_prob = grad_prob + swap(grad_prob, "tp")
+        grad_prob = grad_prob.T
     grad_down = jnp.einsum("jrf,jrd->jfd", activated, grad_prod, preferred_element_type=f32)
     grad_gate = jnp.einsum("jrd,jrf->jdf", rows_in, grad_gate_pre, preferred_element_type=f32)
     grad_up = jnp.einsum("jrd,jrf->jdf", rows_in, grad_up_pre, preferred_element_type=f32)
 
-    grad_hidden_moe = sum_over_tp(block_sum(hidden_grad_partial, nf))
-    grad_prob = lax.all_to_all(
-        grad_prob_part, ("fsdp", "ctx"), split_axis=0, concat_axis=0, tiled=True
-    ).reshape(experts, tokens_dev)
-    grad_prob = grad_prob + swap(grad_prob, "tp")
-    grad_prob = grad_prob.T
     block_out = (resid_mid + sum_over_tp(block_sum(moe_partial, nf))).astype(bf16)
 
     grad_rows = grad_out.astype(f32)

time: 865 us -> 610 us (0.71)
  waiting for transfers between devices: 181 us -> 19.2 us
  matrix products: 193 us -> 93.1 us
  Pallas kernels: 341 us -> 419 us
  local copies, waits for them, and re-layouts: 65.6 us -> 31.6 us
  other arithmetic: 47.3 us -> 18.2 us
    reduce_scatter x2 -> x1, waiting for transfers between devices: 162 us -> 0.01 us  [block_sum(): lax.psum_scatter(partial, ('fsdp', 'ctx'), scatter_dimension=0, tiled=True)]
    pallas_call x0 -> x1, Pallas kernels: none -> 132 us  [expert_pass(): pl.pallas_call(functools.partial(expert_kernel, nf, capacity, tuple(specs...]
    dot_general x10 -> x0, matrix products: 93.9 us -> none  [the longest x2 20.4 us: select(): out = jnp.einsum('bjst,btd->jbsd', pick, blocks, preferred_element_type=f32)]
    pallas_call x3 -> x2, Pallas kernels: 341 us -> 287 us  [plane_gather(): pl.pallas_call(functools.partial(gather_kernel, nf, tuple(specs)), out_sh...]
    convert_element_type x2 -> x0, local copies, waits for them, and re-layouts: 22 us -> none  [the longest x1 13.7 us: on_device(): grad_rows_in.astype(f32)]
    convert_element_type x2 -> x0, other arithmetic: 13.6 us -> none  [the longest x1 13 us: on_device(): (weight_slot[:, :, None] * grad_rows_in.astype(f32)).astype(bf16)]
    ppermute x7 -> x5, waiting for transfers between devices: 19.4 us -> 19.2 us  [swap(): return lax.ppermute(value, axis_name, [(0, 1), (1, 0)])]
  transfers between devices with their start and end apart: 10 -> 6, of which waited for: 5 -> 3; matrix products, arithmetic and copies ran while one was open for 8% -> 19% of each run, Pallas kernels for 0% -> 23%
where the time goes in v2:
time: 610 us; the launch traced here: 603 us
  Pallas kernels  419 us (69%)
  matrix products  93.1 us (15%)
  local copies, waits for them, and re-layouts  31.6 us (5%)
  waiting for transfers between devices  19.2 us (3%)
  other arithmetic  18.2 us (3%)
  between operations  16 us (3%)
    pallas_call x2, Pallas kernels, plane_gather(): pl.pallas_call(functools.partial(gather_kernel, nf, tuple(specs)), out_sh...  287 us
    pallas_call x1, Pallas kernels, expert_pass(): pl.pallas_call(functools.partial(expert_kernel, nf, capacity, tuple(specs...  132 us
    ppermute x5, waiting for transfers between devices, swap(): return lax.ppermute(value, axis_name, [(0, 1), (1, 0)])  19.2 us
    unnamed x193, local copies, waits for them, and re-layouts  13.2 us
  transfers between devices with their start and end apart: 6, of which 3 were waited for; matrix products, arithmetic and copies ran while one was open for 19% of the time, Pallas kernels for 23%

profile of v2, /device:TPU:0, one launch (start us, length us, event | category | flops | bytes accessed | tf_op | source)
XLA Modules:
  0.0 603.3 jit_solution(9114663977267327697)
XLA Ops:
  8.2 1.4 fusion.62.refs_0_
  9.5 147.6 %shard_map.246 = (bf16[1280,128]{1,0:T(8,128)(2,1)}, bf16[2048,2048]{1,0:T(8,128)(2,1)}, bf16[2048,256]{1,0:T(8,128)(2,1)}, bf16[2048,256]{1,0:T(8,128)(2,1)}, b...) custom-call(bf16[80,128]{1,0:T(8,128)(2,1)} %fusion.62.refs_0_, bf16[256,2048]{1,0:T(8,128)(2,1)} %refs_1_.1, ...), custom_call_target="tpu_custom_call" | custom-call | tf_op jit(solution)/shard_map/pallas_call | solution.py:367
  161.7 3.0 all_gather.3
  165.0 4.7 fusion.86
  175.5 4.7 convolution_convert_fusion.1
  182.8 11.7 %collective-permute-done = bf16[128,2048]{1,0:T(8,128)(2,1)S(1)} collective-permute-done((bf16[128,2048]{1,0:T(8,128)(2,1)S(1)}, bf16[128,2048]{1,0:T(8,128)(2,1)S(1)}, u32[]{:S(2)}, u32[]{:S(2)}) %collective-permute-start) | collective-permute-done | bytes 524320 | tf_op jit(solution)/shard_map/ppermute | solution.py:984
  198.6 132.1 %shard_map.247 = (bf16[2048,2048]{1,0:T(8,128)(2,1)}, f32[512,128]{1,0:T(8,128)}, bf16[2048,256]{1,0:T(8,128)(2,1)}, bf16[2048,2048]{1,0:T(8,128)(2,1)}, bf16[2,...) custom-call(bf16[128,2048]{1,0:T(8,128)(2,1)} %copy-done.18, ...), custom_call_target="tpu_custom_call" | custom-call | tf_op jit(solution)/shard_map/pallas_call | solution.py:873
  332.0 1.8 copy.109
  336.2 2.3 multiply_reduce_fusion
  340.0 6.4 %fusion.13 = bf16[16,8,16,128]{3,1,2,0:T(8,128)(2,1)S(1)} fusion(bf16[128,2048]{1,0:T(8,128)(2,1)S(1)} %fusion.78, bf16[2048,2048]{1,0:T(8,128)(2,1)} %get-tuple-element.40), kind=kOutput, calls=%fused_computation.27 | convolution fusion | flops 1074003968 | bytes 9437184 | tf_op jit(solution)/shard_map/td,qd->tq/dot_general | solution.py:1233
  348.7 1.8 fusion.35
  350.5 6.3 %fusion.7 = f32[2,128,256,1]{2,1,3,0:T(8,128)} fusion(f32[2,256,128,8]{2,1,3,0:T(8,128)} %fusion.35, f32[2,8,128,256]{2,3,1,0:T(8,128)} %copy-done.2, f32[2,8,128]{2,1,0:T(8,128)S(1)} %copy-done.66, bf16[128,2,8,64]{3,0,2,1:T(8,128)(2,1)S(1)} %bitcast.221, bf16[128,2,8,64]{3,0,2,1:T(8,128)(2,1)S(1)} %bitcast.219), kind=kOutput, calls=%fused_computation.17 | convolution fusion | flops 138938624 | bytes 4988928 | tf_op jit(solution)/shard_map/kgqs,qkgd->skd/dot_general | solution.py:1251
  358.6 5.3 fusion.8
  365.0 1.6 copy.139
  366.6 2.4 copy.140
  369.0 1.5 multiply_add_fusion
  372.7 1.6 fusion.24
  374.5 11.8 %fusion.95 = f32[2,2048,384]{2,1,0:T(8,128)} fusion(bf16[2,1024,2048]{2,1,0:T(8,128)(2,1)} %get-tuple-element.54, bf16[2,1024,384]{2,1,0:T(8,128)(2,1)S(1)} %copy-done.87), kind=kOutput, calls=%fused_computation.184 | convolution fusion | flops 3221225472 | bytes 16252928 | tf_op jit(solution)/shard_map/jrd,jrf->jdf/dot_general | solution.py:1219
  386.3 11.9 %fusion.94 = f32[2,2048,384]{2,1,0:T(8,128)} fusion(bf16[2,1024,2048]{2,1,0:T(8,128)(2,1)} %get-tuple-element.54, bf16[2,1024,384]{2,1,0:T(8,128)(2,1)S(1)} %copy-done.86), kind=kOutput, calls=%fused_computation.183 | convolution fusion | flops 3221225472 | bytes 16252928 | tf_op jit(solution)/shard_map/jrd,jrf->jdf/dot_general | solution.py:1218
  398.3 3.8 fusion.88
  404.3 1.3 multiply_reduce_fusion.5
  405.9 1.2 mul.396
  407.9 1.2 collective-permute-start.4
  411.1 9.8 %fusion.96 = f32[2,384,2048]{2,1,0:T(8,128)} fusion(bf16[2,1024,384]{2,1,0:T(8,128)(2,1)S(1)} %copy-done.16, bf16[2,1024,2048]{2,1,0:T(8,128)(2,1)} %get-tuple-element.58), kind=kOutput, calls=%fused_computation.185 | convolution fusion | flops 3221225472 | bytes 16252928 | tf_op jit(solution)/shard_map/jrf,jrd->jfd/dot_general | solution.py:1217
  425.0 139.1 %shard_map.248 = (bf16[2048,2048]{1,0:T(8,128)(2,1)}, bf16[2048,256]{1,0:T(8,128)(2,1)}, bf16[2048,256]{1,0:T(8,128)(2,1)}, bf16[2048,2048]{1,0:T(8,128)(2,1)}, ...) custom-call(bf16[128,2048]{1,0:T(8,128)(2,1)} %copy-done.17, ...), custom_call_target="tpu_custom_call" | custom-call | tf_op jit(solution)/shard_map/pallas_call | solution.py:367
  566.5 2.3 fusion.25
  568.8 2.5 fusion.92
  571.3 1.2 fusion.91
  572.5 7.2 %fusion.93 = f32[2048,256]{1,0:T(8,128)} fusion(bf16[2048,2048]{1,0:T(8,128)(2,1)} %get-tuple-element.50, bf16[2048,256]{1,0:T(8,128)(2,1)S(1)} %copy-done.88), kind=kOutput, calls=%fused_computation.182 | convolution fusion | flops 2147483648 | bytes 11534336 | tf_op jit(solution)/shard_map/td,tq->dq/dot_general | solution.py:1317
  580.3 7.2 %fusion.90 = f32[256,2048]{1,0:T(8,128)} fusion(bf16[2048,256]{1,0:T(8,128)(2,1)S(1)} %copy-done.7, bf16[2048,2048]{1,0:T(8,128)(2,1)} %get-tuple-element.47), kind=kOutput, calls=%fused_computation.179 | convolution fusion | flops 2147483648 | bytes 11534336 | tf_op jit(solution)/shard_map/td,tq->dq/dot_general | solution.py:1314
  587.5 6.6 %collective-permute-done.1 = bf16[128,2048]{1,0:T(8,128)(2,1)S(1)} collective-permute-done((bf16[128,2048]{1,0:T(8,128)(2,1)}, bf16[128,2048]{1,0:T(8,128)(2,1)S(1)}, u32[]{:S(2)}, u32[]{:S(2)}) %collective-permute-start.1) | collective-permute-done | bytes 524320 | tf_op jit(solution)/shard_map/ppermute | solution.py:984
  594.1 1.8 fusion.18
  (298 shorter events, 42.3 us)
Async XLA Ops:
  7.2 572.5 %reduce-scatter.2.cloned.1.call-start = ((), (), s32[]{:S(2)}) async-start(), calls=%async_computation.1 | async-start | bytes 8912896 | tf_op jit(solution)/shard_map/reduce_scatter | solution.py:993
  8.2 150.3 %copy-start.5 = (bf16[128,2048]{1,0:T(8,128)(2,1)S(1)}, bf16[128,2048]{1,0:T(8,128)(2,1)}, u32[]{:S(2)}) copy-start(bf16[128,2048]{1,0:T(8,128)(2,1)} %param.15) | copy-start | bytes 1572868
  160.8 11.0 %copy-start.37 = (f32[128,64]{1,0:T(8,128)}, f32[128,64]{1,0:T(8,128)S(1)}, u32[]{:S(2)}) copy-start(f32[128,64]{1,0:T(8,128)S(1)} %get-tuple-element.93) | copy-start | bytes 98308
  160.8 11.0 %copy-start.39 = (f32[128,64]{1,0:T(8,128)}, f32[128,64]{1,0:T(8,128)S(1)}, u32[]{:S(2)}) copy-start(f32[128,64]{1,0:T(8,128)S(1)} %get-tuple-element.94) | copy-start | bytes 98308
  165.0 7.7 %copy-start.55 = (bf16[256,2,128,1]{0,2,3,1:T(8,128)(2,1)}, bf16[256,2,128,1]{0,2,3,1:T(8,128)(2,1)S(1)}, u32[]{:S(2)}) copy-start(bf16[256,2,128,1]{0,2,3,1:T(8,128)(2,1)S(1)} %copy.119) | copy-start | bytes 393220
  171.4 10.8 %copy-start.74 = (f32[128]{0:T(128)}, f32[128]{0:T(128)S(1)}, u32[]{:S(2)}) copy-start(f32[128]{0:T(128)S(1)} %slice.84) | copy-start | bytes 1540
  180.2 14.3 %collective-permute-start = (bf16[128,2048]{1,0:T(8,128)(2,1)S(1)}, bf16[128,2048]{1,0:T(8,128)(2,1)S(1)}, u32[]{:S(2)}, u32[]{:S(2)}) collective-permute-start(bf16[128,2048]{1,0:T(8,128)(2,1)S(1)} %convolution_convert_fusion.1), channel_id=1, source_target_pairs={{0,1},{1,0},{2,3},{3,2},{4,5},{5,4},{6,7},{7,6},{8,9},{9,8},{10,11... | collective-permute-start | bytes 1572872 | tf_op jit(solution)/shard_map/ppermute | solution.py:984
  180.8 14.1 %copy-start.61 = (f32[1,2,8,128]{3,1,2,0:T(2,128)}, f32[1,2,8,128]{3,1,2,0:T(2,128)S(1)}, u32[]{:S(2)}) copy-start(f32[1,2,8,128]{3,1,2,0:T(2,128)S(1)} %copy.146) | copy-start | bytes 24580
  181.2 14.8 %copy-start.21 = (bf16[2048,32]{1,0:T(8,128)(2,1)}, bf16[2048,32]{1,0:T(8,128)(2,1)S(1)}, u32[]{:S(2)}) copy-start(bf16[2048,32]{1,0:T(8,128)(2,1)S(1)} %reshape.317) | copy-start | bytes 393220
  181.3 15.9 %copy-start.57 = (pred[128,32]{1,0:T(8,128)(4,1)}, pred[128,32]{1,0:T(8,128)(4,1)S(1)}, u32[]{:S(2)}) copy-start(pred[128,32]{1,0:T(8,128)(4,1)S(1)} %copy.95) | copy-start | bytes 12292
  338.6 7.7 %copy-start.84 = (f32[128]{0:T(128)}, f32[128]{0:T(128)S(1)}, u32[]{:S(2)}) copy-start(f32[128]{0:T(128)S(1)} %broadcast_multiply_fusion.3) | copy-start | bytes 1540
  350.5 8.1 %copy-start.56 = (bf16[256,2,128,1]{0,2,3,1:T(8,128)(2,1)S(1)}, bf16[256,2,128,1]{0,2,3,1:T(8,128)(2,1)}, u32[]{:S(2)}) copy-start(bf16[256,2,128,1]{0,2,3,1:T(8,128)(2,1)} %copy-done.55) | copy-start | bytes 393220
  358.6 43.5 %collective-permute-start.2 = (bf16[128,512]{1,0:T(8,128)(2,1)}, bf16[128,512]{1,0:T(8,128)(2,1)}, u32[]{:S(2)}, u32[]{:S(2)}) collective-permute-start(bf16[128,512]{1,0:T(8,128)(2,1)} %fusion.38), channel_id=1, source_target_pairs={{0,2},{2,0},{1,3},{3,1},{4,6},{6,4},{5,7},{7,5},{8,10},{10,8},{9,1... | collective-permute-start | bytes 393224 | tf_op jit(solution)/shard_map/ppermute | solution.py:984
  374.3 23.9 %copy-start.17 = (bf16[128,2048]{1,0:T(8,128)(2,1)}, bf16[128,2048]{1,0:T(8,128)(2,1)S(1)}, u32[]{:S(2)}) copy-start(bf16[128,2048]{1,0:T(8,128)(2,1)S(1)} %get-tuple-element.70.refs_0_) | copy-start | bytes 1572868
  374.5 11.8 %copy-start.86 = (bf16[2,1024,384]{2,1,0:T(8,128)(2,1)S(1)}, bf16[2,1024,384]{2,1,0:T(8,128)(2,1)}, u32[]{:S(2)}) copy-start(bf16[2,1024,384]{2,1,0:T(8,128)(2,1)} %get-tuple-element.55) | copy-start | bytes 4718596
  374.5 23.8 %slice-start = ((s8[8388608]{0:T(1024)(128)(4,1)}), s8[4194304]{0:T(1024)(128)(4,1)S(1)}, s32[]{:S(2)}) async-start(s8[8388608]{0:T(1024)(128)(4,1)} %bitcast.204), calls=%async_computation.2 | async-start | bytes 8388608
  386.3 12.0 %slice-start.1 = ((s8[8388608]{0:T(1024)(128)(4,1)}), s8[4194304]{0:T(1024)(128)(4,1)S(1)}, s32[]{:S(2)}) async-start(s8[8388608]{0:T(1024)(128)(4,1)} %bitcast.204), calls=%async_computation.3 | async-start | bytes 8388608
  402.1 7.0 %copy-start.23 = (f32[128,2048]{1,0:T(8,128)S(1)}, f32[128,2048]{1,0:T(8,128)}, u32[]{:S(2)}) copy-start(f32[128,2048]{1,0:T(8,128)} %fusion.88) | copy-start | bytes 3145732
  407.9 15.1 %collective-permute-start.4 = (f32[256]{0:T(256)S(1)}, f32[256]{0:T(256)S(1)}, u32[]{:S(2)}, u32[]{:S(2)}) collective-permute-start(f32[256]{0:T(256)S(1)} %pad_maximum_fusion.7), channel_id=1, source_target_pairs={{0,1},{1,0},{2,3},{3,2},{4,5},{5,4},{6,7},{7,6},{8,9},{9,8},{10,11... | collective-permute-start | bytes 3080 | tf_op jit(solution)/shard_map/ppermute | solution.py:984
  410.1 13.8 %collective-permute-start.3 = (bf16[128,2048]{1,0:T(8,128)(2,1)S(1)}, bf16[128,2048]{1,0:T(8,128)(2,1)S(1)}, u32[]{:S(2)}, u32[]{:S(2)}) collective-permute-start(bf16[128,2048]{1,0:T(8,128)(2,1)S(1)} %fusion.1), channel_id=1, source_target_pairs={{0,1},{1,0},{2,3},{3,2},{4,5},{5,4},{6,7},{7,6},{8,9},{9,8},{10,11... | collective-permute-start | bytes 1572872 | tf_op jit(solution)/shard_map/ppermute | solution.py:984
  411.0 10.6 %copy-start.60 = (bf16[128,32]{1,0:T(8,128)(2,1)S(1)}, bf16[128,32]{1,0:T(8,128)(2,1)}, u32[]{:S(2)}) copy-start(bf16[128,32]{1,0:T(8,128)(2,1)} %copy-done.59) | copy-start | bytes 24580
  411.0 12.9 %copy-start.6 = (bf16[128,2048]{1,0:T(8,128)(2,1)S(1)}, bf16[128,2048]{1,0:T(8,128)(2,1)}, u32[]{:S(2)}) copy-start(bf16[128,2048]{1,0:T(8,128)(2,1)} %param.15) | copy-start | bytes 1572868
  411.0 12.9 %copy-start.64 = (f32[1,2,8,128]{3,1,2,0:T(2,128)S(1)}, f32[1,2,8,128]{3,1,2,0:T(2,128)}, u32[]{:S(2)}) copy-start(f32[1,2,8,128]{3,1,2,0:T(2,128)} %copy-done.63) | copy-start | bytes 24580
  411.0 12.9 %copy-start.79 = (f32[128]{0:T(128)S(1)}, f32[128]{0:T(128)}, u32[]{:S(2)}) copy-start(f32[128]{0:T(128)} %copy-done.78) | copy-start | bytes 1540
  425.0 143.8 %copy-start.7 = (bf16[2048,256]{1,0:T(8,128)(2,1)S(1)}, bf16[2048,256]{1,0:T(8,128)(2,1)}, u32[]{:S(2)}) copy-start(bf16[2048,256]{1,0:T(8,128)(2,1)} %get-tuple-element.46) | copy-start | bytes 3145732
  579.7 14.4 %collective-permute-start.1 = (bf16[128,2048]{1,0:T(8,128)(2,1)}, bf16[128,2048]{1,0:T(8,128)(2,1)S(1)}, u32[]{:S(2)}, u32[]{:S(2)}) collective-permute-start(bf16[128,2048]{1,0:T(8,128)(2,1)} %reduce-scatter.2.cloned.1.call-done), channel_id=1, source_target_pairs={{0,1},{1,0},{2,3},{3,2},{4,5},{5,4},{6,7},{7,6},{8,9},{9,8},{10,11... | collective-permute-start | bytes 1572872 | tf_op jit(solution)/shard_map/ppermute | solution.py:984
  580.3 13.8 %copy-start.11 = (f32[128,2048]{1,0:T(8,128)S(1)}, f32[128,2048]{1,0:T(8,128)}, u32[]{:S(2)}) copy-start(f32[128,2048]{1,0:T(8,128)} %copy-done.10) | copy-start | bytes 3145732
  580.3 13.8 %copy-start.20 = (bf16[128,2048]{1,0:T(8,128)(2,1)S(1)}, bf16[128,2048]{1,0:T(8,128)(2,1)}, u32[]{:S(2)}) copy-start(bf16[128,2048]{1,0:T(8,128)(2,1)} %refs_5_.2) | copy-start | bytes 1572868
  580.3 13.8 %copy-start.34 = (bf16[128,2048]{1,0:T(8,128)(2,1)S(1)}, bf16[128,2048]{1,0:T(8,128)(2,1)}, u32[]{:S(2)}) copy-start(bf16[128,2048]{1,0:T(8,128)(2,1)} %copy-done.33) | copy-start | bytes 1572868
  580.3 13.8 %copy-start.54 = (bf16[128,2048]{1,0:T(8,128)(2,1)S(1)}, bf16[128,2048]{1,0:T(8,128)(2,1)}, u32[]{:S(2)}) copy-start(bf16[128,2048]{1,0:T(8,128)(2,1)} %reduce-scatter.2.cloned.1.call-done) | copy-start | bytes 1572868
  580.3 13.8 %copy-start.73 = (f32[128]{0:T(128)S(1)}, f32[128]{0:T(128)}, u32[]{:S(2)}) copy-start(f32[128]{0:T(128)} %copy-done.71) | copy-start | bytes 1540
  580.3 13.8 %copy-start.85 = (f32[128]{0:T(128)S(1)}, f32[128]{0:T(128)}, u32[]{:S(2)}) copy-start(f32[128]{0:T(128)} %copy-done.84) | copy-start | bytes 1540
  (66 other events, 178.0 us)
Sparse Core Ops, SparseCore 0:
  330.9 116.0 reduce-scatter.1

commit v3 on v2

--- a/solution.py
+++ b/solution.py
@@ -54,7 +54,7 @@
 
     def src(a, q, dest_f=None):
         s = specs[a]
-        lo = q * s.step
+        lo = row_chunk(a, q) * s.step
         if s.half:
             lo = c * s.rows + lo
         if s.form == "a2a":
@@ -66,44 +66,52 @@
         if s.form == "col":
             width = s.shape[1]
             return outs[a].at[
-                pl.ds(bc * s.rows + q * s.step, s.step),
+                pl.ds(bc * s.rows + row_chunk(a, q) * s.step, s.step),
                 pl.ds(pl.multiple_of(bf * width, width), width),
             ]
         rows = s.rows // nf if s.form == "a2a" else s.rows
-        return outs[a].at[pl.ds((bf * 2 + bc) * rows + q * s.step, s.step)]
+        return outs[a].at[pl.ds((bf * 2 + bc) * rows + row_chunk(a, q) * s.step, s.step)]
 
     def copy(a, q, bf, bc, source, kind, dev=None, slot=None):
         block = bf * 2 + bc if slot is None else slot
         return pltpu.make_async_remote_copy(
             src_ref=source,
             dst_ref=dst(a, q, bf, bc),
-            send_sem=send.at[kind, block, first[a] + q],
-            recv_sem=recv.at[bf * 2 + bc, first[a] + q],
+            send_sem=send.at[kind, block, first[a] + row_chunk(a, q)],
+            recv_sem=recv.at[bf * 2 + bc, first[a] + row_chunk(a, q)],
             device_id=device[kind] if dev is None else dev,
             device_id_type=MESH,
         )
 
+    def row_chunk(a, q):
+        n_chunks = specs[a].chunks
+        if not specs[a].rep:
+            return q
+        return lax.rem(q + t * (n_chunks // 2), n_chunks)
+
     def in_half(a, q):
-        return (q * 2) // specs[a].chunks == t
+        return 2 * q < specs[a].chunks
 
     def both(*conds):
-        conds = [k for k in conds if k is not None]
+        if any(k is False for k in conds):
+            return False
+        conds = [k for k in conds if k is not None and k is not True]
         if not conds:
             return None
         return functools.reduce(lambda u, v: u & v, conds)
 
     def when(cond, fn):
-        if cond is None:
+        if cond is None or cond is True:
             fn()
-        else:
+        elif cond is not False:
             pl.when(cond)(fn)
 
     def go_up(a, q, dist):
-        far = (dist + 1 < nz - 1) | in_half(a, q) if specs[a].rep else None
+        far = dist + 1 < nz - 1 if specs[a].rep and not in_half(a, q) else None
         return both(has_up, far)
 
     def go_down(a, q, dist):
-        far = (dist + 1 < nz - 1) | in_half(a, q) if specs[a].rep else None
+        far = dist + 1 < nz - 1 if specs[a].rep and not in_half(a, q) else None
         return both(has_down, far)
 
     def go_across(a, q):
@@ -112,20 +120,27 @@
     relays = [(a, q) for a in range(n) if specs[a].form != "a2a" for q in range(specs[a].chunks)]
     direct = [(a, q) for a in range(n) if specs[a].form == "a2a" for q in range(specs[a].chunks)]
 
-    def start():
+    def start(only=None):
+        only = range(n) if only is None else only
         for a, q in relays:
+            if a not in only:
+                continue
             source = src(a, q)
             when(go_up(a, q, 0), lambda: copy(a, q, f, c, source, UP).start())
             when(go_down(a, q, 0), lambda: copy(a, q, f, c, source, DOWN).start())
             when(go_across(a, q), lambda: copy(a, q, f, c, source, ACROSS).start())
             copy(a, q, f, c, source, PARTNER).start()
-        for a in range(n):
+        own_start([a for a in only if specs[a].form != "a2a"])
+
+    def own_start(only):
+        for a in only:
             own_in(a).start()
-        for a in range(n):
+        for a in only:
             own_in(a).wait()
             own_out(a).start()
 
     def start_direct():
+        own_start(sorted({a for a, _ in direct}))
         for a, q in direct:
             copy(a, q, f, c, src(a, q, f), PARTNER).start()
 
@@ -164,79 +179,116 @@
     def pass_on(a, q, bf, kind, cond=None):
         when(cond, lambda: copy(a, q, bf, c, dst(a, q, bf, c), kind).start())
 
-    def column(k):
-        for a, q in relays:
-            rep = specs[a].rep
-            came = ((k < nz - 1) | in_half(a, q)) if rep else None
-            aside = (k == nz - 1) if rep else None
-
-            def below():
-                bf = (z - k) * 2 + x
-                arrived(a, q, bf, c)
-                pass_on(a, q, bf, UP, go_up(a, q, k))
-                pass_on(a, q, bf, ACROSS, go_across(a, q))
-                pass_on(a, q, bf, PARTNER)
-                if rep:
-                    pass_on(a, q, bf, SIDE, aside)
-
-            def above():
-                bf = (z + k) * 2 + x
-                arrived(a, q, bf, c)
-                pass_on(a, q, bf, DOWN, go_down(a, q, k))
-                pass_on(a, q, bf, ACROSS, go_across(a, q))
-                pass_on(a, q, bf, PARTNER)
-                if rep:
-                    pass_on(a, q, bf, SIDE, aside)
-
-            when(both(z - k >= 0, came), below)
-            when(both(z + k < nz, came), above)
-
-    def across(k):
-        for a, q in relays:
-            rep = specs[a].rep
-
-            def take(zz):
-                bf = zz * 2 + 1 - x
-                arrived(a, q, bf, c)
-                pass_on(a, q, bf, PARTNER)
-                if rep:
-                    pass_on(a, q, bf, SIDE)
-
-            mine = in_half(a, q) if rep else None
-            when(both(z - k >= 0, mine), lambda: take(z - k))
-            when(both(z + k < nz, k > 0, mine), lambda: take(z + k))
-
-    def aside(k):
-        for a, q in relays:
-            if not specs[a].rep:
-                continue
-            other = jnp.logical_not(in_half(a, q))
-
-            def take(bf):
-                arrived(a, q, bf, c)
-                pass_on(a, q, bf, PARTNER)
-
-            when((z - k >= 0) & other, lambda: take((z - k) * 2 + 1 - x))
-            when((z + k < nz) & (k > 0) & other, lambda: take((z + k) * 2 + 1 - x))
-            when((z - k >= 0) & (k == nz - 1) & other, lambda: take((z - k) * 2 + x))
-            when((z + k < nz) & (k == nz - 1) & other, lambda: take((z + k) * 2 + x))
+    pair = z + 1 - 2 * lax.rem(z, 2)
+    even = lax.rem(z, 2) == 0
+
+    def shared(a, q):
+        return not specs[a].rep and specs[a].chunks > 1 and 2 * q >= specs[a].chunks
+
+    def column(k, a, q):
+        rep = specs[a].rep
+        came = k < nz - 1 if rep and not in_half(a, q) else None
+        far = (k == nz - 1) if rep and in_half(a, q) else False
+
+        def take(zz, kind, onward):
+            bf = zz * 2 + x
+            arrived(a, q, bf, c)
+            pass_on(a, q, bf, kind, onward)
+            cross = (zz != pair) if shared(a, q) else go_across(a, q)
+            pass_on(a, q, bf, ACROSS, cross)
+            pass_on(a, q, bf, PARTNER)
+            if rep:
+                pass_on(a, q, bf, SIDE, far)
+
+        when(both(z - k >= 0, came), lambda: take(z - k, UP, go_up(a, q, k)))
+        when(both(z + k < nz, came), lambda: take(z + k, DOWN, go_down(a, q, k)))
+
+    def across(k, a, q):
+        rep = specs[a].rep
+        mine = in_half(a, q) if rep else None
+
+        def take(zz):
+            bf = zz * 2 + 1 - x
+            arrived(a, q, bf, c)
+            pass_on(a, q, bf, PARTNER)
+            if rep:
+                pass_on(a, q, bf, SIDE)
+            if shared(a, q):
+                pass_on(a, q, bf, UP, (zz == z) & even)
+                pass_on(a, q, bf, DOWN, (zz == z) & jnp.logical_not(even))
+
+        when(both(z - k >= 0, mine), lambda: take(z - k))
+        when(both(z + k < nz, k > 0, mine), lambda: take(z + k))
+
+    def aside(k, a, q):
+        if not specs[a].rep:
+            return
+        if in_half(a, q):
+            return
+
+        def take(bf):
+            arrived(a, q, bf, c)
+            pass_on(a, q, bf, PARTNER)
+
+        when((z - k >= 0), lambda: take((z - k) * 2 + 1 - x))
+        when((z + k < nz) & (k > 0), lambda: take((z + k) * 2 + 1 - x))
+        when((z - k >= 0) & (k == nz - 1), lambda: take((z - k) * 2 + x))
+        when((z + k < nz) & (k == nz - 1), lambda: take((z + k) * 2 + x))
+
+    count = len(relays)
+    lag = 2
+
+    def late(fn, k, i):
+        if i >= 0:
+            fn(k, *relays[i])
+        else:
+            pl.when(k > 1)(lambda: fn(k - 1, *relays[count + i]))
+
+    by_chunk = all(specs[a].rep for a, _ in relays)
 
     def step(k, carry):
-        column(k)
-        across(k - 1)
-
-        @pl.when(k > 1)
+        if not by_chunk:
+            for a, q in relays:
+                column(k, a, q)
+            for a, q in relays:
+                across(k - 1, a, q)
+
+            @pl.when(k > 1)
+            def _():
+                for a, q in relays:
+                    aside(k - 2, a, q)
+
+            return carry
+        for i, (a, q) in enumerate(relays):
+            column(k, a, q)
+            pl.when(k == 1)(lambda: across(0, a, q))
+            late(across, k, i - lag)
+            if i >= lag:
+                pl.when(k == 1)(lambda: aside(0, *relays[i - lag]))
+            late(aside, k, i - 2 * lag)
+
+        @pl.when(k == 1)
         def _():
-            aside(k - 2)
+            for a, q in relays[count - lag :]:
+                aside(0, a, q)
 
         return carry
 
-    def run():
-        lax.fori_loop(1, nz, step, 0)
-        across(nz - 1)
-        if any(s.rep for s in specs):
-            aside(nz - 2)
-            aside(nz - 1)
+    def run(hook=None):
+        def body(k, carry):
+            step(k, carry)
+            if hook is not None:
+                hook(k)
+            return carry
+
+        lax.fori_loop(1, nz, body, 0)
+        for a, q in relays[count - lag if by_chunk else 0 :]:
+            across(nz - 1, a, q)
+        if not by_chunk:
+            for a, q in relays:
+                aside(nz - 2, a, q)
+        for a, q in relays[count - 2 * lag if by_chunk else 0 :]:
+            aside(nz - 1, a, q)
 
     def run_direct():
         for a, q in direct:
@@ -257,7 +309,8 @@
     def land():
         lax.fori_loop(0, nf, take_partner, 0)
         for a in range(n):
-            own_out(a).wait()
+            if specs[a].form != "a2a":
+                own_out(a).wait()
 
     def finish(bf, carry):
         zz, xx = bf // 2, lax.rem(bf, 2)
@@ -271,13 +324,18 @@
                 when(cond, lambda: copy(a, q, bf, c, view, kind).wait_send())
 
             half = in_half(a, q) if rep else None
-            by_z = ((dist < nz - 1) | half) if rep else None
+            by_z = dist < nz - 1 if rep and not half else None
             sent(PARTNER, None)
             sent(UP, both(here, zz <= z, by_z, go_up(a, q, dist)))
             sent(DOWN, both(here, zz >= z, by_z, go_down(a, q, dist)))
-            sent(ACROSS, both(here, by_z, go_across(a, q)))
-            if rep:
-                sent(SIDE, half & (jnp.logical_not(here) | (dist == nz - 1)))
+            cross = (zz != pair) if shared(a, q) else go_across(a, q)
+            sent(ACROSS, both(here, by_z, cross))
+            if shared(a, q):
+                there = jnp.logical_not(here) & (zz == z)
+                sent(UP, there & even)
+                sent(DOWN, there & jnp.logical_not(even))
+            if rep and half:
+                sent(SIDE, jnp.logical_not(here) | (dist == nz - 1))
         for a, q in direct:
             arrived(a, q, bf, 1 - c)
             view = dst(a, q, bf, c)
@@ -291,6 +349,9 @@
 
     def drain():
         lax.fori_loop(0, nf, finish, 0)
+        for a in range(n):
+            if specs[a].form == "a2a":
+                own_out(a).wait()
 
     return start, run, land, start_direct, run_direct, drain
 
@@ -845,7 +906,7 @@
 def expert_pass(hidden_two, marks, hidden_slices, grad_all, w_gate, w_up, w_down, capacity, nf):
     specs = [
         Gather(hidden_two, nf, rep=True, chunks=4),
-        Gather(marks, nf, chunks=1),
+        Gather(marks, nf, rep=True, chunks=2),
         Gather(hidden_slices, nf, form="a2a", chunks=1),
     ]
     n = len(specs)
@@ -928,6 +989,533 @@
     return (hidden_all, hidden_slice) + tuple(result[3:])
 
 
+NT = (((1,), (1,)), ((), ()))
+TN = (((0,), (0,)), ((), ()))
+
+
+def backward_kernel(nf, specs, *refs):
+    n = len(specs)
+    (
+        attended,
+        dh2_moe,
+        grad_prob,
+        probs,
+        router,
+        x_in,
+        x_mid,
+        gains,
+        grad_out,
+        wo_hbm,
+        wq_hbm,
+        wk_hbm,
+        wv_hbm,
+        q_raw,
+        k_raw,
+        q_rot,
+        keys,
+        values,
+        bias,
+        lse,
+        trig,
+        out_part,
+    ), refs = refs[:22], refs[22:]
+    gathered, grad_in, block_out, refs = refs[:n], refs[n], refs[n + 1], refs[n + 2 :]
+    stage, refs = refs[:n], refs[n:]
+    (recv, send, local), refs = refs[:3], refs[3:]
+    (
+        w_big,
+        w_key,
+        w_value,
+        dx1,
+        dh2,
+        d_out,
+        d_out_slices,
+        d_attn,
+        d_query,
+        d_key,
+        d_value,
+        logit,
+        tail,
+        dk_acc,
+        dv_acc,
+        qk_acc,
+        kv_send,
+        kv_recv,
+        dh1,
+        dh1_side,
+        qk_side,
+        row_sum,
+        w_sem,
+        kv_sem,
+        side_send,
+        side_recv,
+        sum_own,
+        sum_total,
+        sum_bufs,
+        sum_sems,
+    ) = refs[:28] + (refs[28:32], refs[32:])
+    f32, bf16 = jnp.float32, jnp.bfloat16
+    f, c, t = lax.axis_index("fsdp"), lax.axis_index("ctx"), lax.axis_index("tp")
+    partner, side = (f, 1 - c, t), (f, c, 1 - t)
+    tokens, width = x_in.shape
+    experts = probs.shape[1]
+    scale = HEAD_SIZE ** (-0.5)
+
+    barrier = pltpu.get_barrier_semaphore()
+
+    def greet(d, carry):
+        pl.semaphore_signal(
+            barrier, 1, device_id=(lax.rem(f + d, nf), c, t), device_id_type=MESH
+        )
+        return carry
+
+    lax.fori_loop(1, nf, greet, 0)
+    for dev in (partner, side):
+        pl.semaphore_signal(barrier, 1, device_id=dev, device_id_type=MESH)
+    pl.semaphore_wait(barrier, nf + 1)
+
+    ins = (attended, d_query, d_key, d_value, logit, tail, d_out_slices)
+    start, run, land, start_direct, run_direct, drain = gather_engine(
+        nf, specs, ins, gathered, stage, recv, send, local
+    )
+    nz = nf // 2
+    order = visit_code(nz, f // 2)
+    own_loads, to_partner, to_across, along, finish_sum, drain_sum = token_sum(
+        nf, out_part, sum_own, sum_total, sum_bufs, sum_sems
+    )
+    for cp in own_loads:
+        cp.start()
+    lax.fori_loop(0, nz, lambda i, carry: to_partner(visit(order, nz, i), carry), 0)
+    start((0,))
+
+    def load(src, dst, i):
+        return pltpu.make_async_copy(src, dst, w_sem.at[i])
+
+    load(wo_hbm, w_big, 0).start()
+    load(wk_hbm, w_key, 1).start()
+    load(wv_hbm, w_value, 2).start()
+
+    logit[...] = jnp.zeros_like(logit)
+    pr = probs[...]
+    gp = grad_prob[...]
+    dl = (pr * (gp - jnp.sum(pr * gp, axis=1, keepdims=True))).astype(bf16)
+    logit[:, :experts] = dl
+    tile = 512
+    for k in range(width // tile):
+        cols = slice(k * tile, (k + 1) * tile)
+        dh2[:, cols] = dh2_moe[:, cols] + lax.dot_general(
+            dl, router[cols, :], NT, preferred_element_type=f32
+        )
+    gain_one, gain_two = gains[0:1, :], gains[1:2, :]
+    gain_query, gain_key = gains[2:3, :HEAD_SIZE], gains[2:3, HEAD_SIZE : 2 * HEAD_SIZE]
+    row_sum[...] = jnp.zeros_like(row_sum)
+    part_rows = 16
+
+    def norm_two(i, carry):
+        rows = pl.ds(pl.multiple_of(i * part_rows, part_rows), part_rows)
+        x1 = x_mid[rows]
+        r2 = lax.rsqrt(jnp.mean(x1 * x1, axis=1, keepdims=True) + eps_norm)
+        n2 = x1 * r2
+        g = dh2[rows]
+        row_sum[1:2, :] += jnp.sum(g * n2, axis=0, keepdims=True)
+        scaled = g * gain_two
+        mean = jnp.mean(scaled * n2, axis=1, keepdims=True)
+        out = grad_out[rows].astype(f32) + r2 * (scaled - n2 * mean)
+        dx1[rows] = out
+        d_out[rows] = out.astype(bf16)
+        return carry
+
+    lax.fori_loop(0, tokens // part_rows, norm_two, 0)
+    shard = width // nf
+    for k in range(nf):
+        d_out_slices[k * tokens : (k + 1) * tokens, :] = d_out[:, k * shard : (k + 1) * shard]
+
+    load(wo_hbm, w_big, 0).wait()
+    heads_width = d_attn.shape[1]
+    tile = 256
+    for k in range(heads_width // tile):
+        cols = slice(k * tile, (k + 1) * tile)
+        d_attn[:, cols] = lax.dot_general(
+            d_out[...], w_big[cols, :], NT, preferred_element_type=f32
+        ).astype(bf16)
+    load(wq_hbm, w_big, 0).start()
+    for cp in own_loads:
+        cp.wait()
+    lax.fori_loop(0, nz, lambda i, carry: to_across(visit(order, nz, i), carry), 0)
+    dk_acc[...] = jnp.zeros_like(dk_acc)
+    dv_acc[...] = jnp.zeros_like(dv_acc)
+    qk_acc[...] = jnp.zeros_like(qk_acc)
+    group = QUERY_HEADS // KEY_VALUE_HEADS
+
+    def unrope(g):
+        return g * trig[0] + pltpu.roll(g, HEAD_SIZE // 2, 1) * trig[1]
+
+    def norm_back(g, raw, gain):
+        inv = lax.rsqrt(jnp.mean(raw * raw, axis=1, keepdims=True) + eps_norm)
+        hat = raw * inv
+        scaled = g * gain
+        mean = jnp.mean(scaled * hat, axis=1, keepdims=True)
+        return jnp.sum(g * hat, axis=0, keepdims=True), inv * (scaled - hat * mean)
+
+    def head(h, carry):
+        cols = pl.ds(pl.multiple_of(h * HEAD_SIZE, HEAD_SIZE), HEAD_SIZE)
+        kv_cols = pl.ds(pl.multiple_of((h // group) * HEAD_SIZE, HEAD_SIZE), HEAD_SIZE)
+        q, key, value, da = q_rot[:, cols], keys[:, kv_cols], values[:, kv_cols], d_attn[:, cols]
+        s = lax.dot_general(q, key, NT, preferred_element_type=f32) * scale + bias[...]
+        prob = jnp.exp(s - lse[h])
+        dp = lax.dot_general(da, value, NT, preferred_element_type=f32)
+        delta = jnp.sum(prob * dp, axis=1, keepdims=True)
+        ds = (prob * (dp - delta) * scale).astype(bf16)
+        dk_acc[:, kv_cols] += lax.dot_general(ds, q, TN, preferred_element_type=f32)
+        dv_acc[:, kv_cols] += lax.dot_general(
+            prob.astype(bf16), da, TN, preferred_element_type=f32
+        )
+        dq = unrope(jnp.dot(ds, key, preferred_element_type=f32))
+        gain_grad, dq = norm_back(dq, q_raw[:, cols], gain_query)
+        qk_acc[0:1, :] += gain_grad
+        d_query[:, cols] = dq.astype(bf16)
+        return carry
+
+    lax.fori_loop(0, heads_width // HEAD_SIZE, head, 0)
+
+    kv_width = dk_acc.shape[1]
+    theirs = pl.ds(pl.multiple_of((1 - c) * tokens, tokens), tokens)
+    mine = pl.ds(pl.multiple_of(c * tokens, tokens), tokens)
+    kv_send[:, :kv_width] = dk_acc[theirs].astype(bf16)
+    kv_send[:, kv_width:] = dv_acc[theirs].astype(bf16)
+    swap_kv = pltpu.make_async_remote_copy(
+        src_ref=kv_send,
+        dst_ref=kv_recv,
+        send_sem=kv_sem.at[0],
+        recv_sem=kv_sem.at[1],
+        device_id=partner,
+        device_id_type=MESH,
+    )
+    swap_kv.start()
+    start((1, 4))
+    start_direct()
+    swap_kv.wait()
+    for kv in range(kv_width // HEAD_SIZE):
+        cols = slice(kv * HEAD_SIZE, (kv + 1) * HEAD_SIZE)
+        g = dk_acc[mine, cols] + kv_recv[:, cols].astype(f32)
+        gain_grad, dk = norm_back(unrope(g), k_raw[:, cols], gain_key)
+        qk_acc[1:2, :] += gain_grad
+        d_key[:, cols] = dk.astype(bf16)
+    d_value[...] = (dv_acc[mine] + kv_recv[:, kv_width:].astype(f32)).astype(bf16)
+    start((2, 3))
+
+    def to_side(src, dst, i):
+        return pltpu.make_async_remote_copy(
+            src_ref=src,
+            dst_ref=dst,
+            send_sem=side_send.at[i],
+            recv_sem=side_recv.at[i],
+            device_id=side,
+            device_id_type=MESH,
+        )
+
+    swap_qk = to_side(qk_acc, qk_side, 4)
+    swap_qk.start()
+    load(wq_hbm, w_big, 0).wait()
+    load(wk_hbm, w_key, 1).wait()
+    load(wv_hbm, w_value, 2).wait()
+    quarter = width // 4
+
+    def dh1_copy(i):
+        cols = pl.ds(i * quarter, quarter)
+        return to_side(dh1.at[:, cols], dh1_side.at[:, cols], i)
+
+    for k in range(width // tile):
+        rows = slice(k * tile, (k + 1) * tile)
+        total = lax.dot_general(d_query[...], w_big[rows, :], NT, preferred_element_type=f32)
+        total = total + lax.dot_general(d_key[...], w_key[rows, :], NT, preferred_element_type=f32)
+        total = total + lax.dot_general(
+            d_value[...], w_value[rows, :], NT, preferred_element_type=f32
+        )
+        dh1[:, rows] = total.astype(bf16)
+        if (k + 1) * tile % quarter == 0:
+            dh1_copy((k + 1) * tile // quarter - 1).start()
+    for i in range(4):
+        dh1_copy(i).wait_recv()
+    swap_qk.wait_recv()
+
+    def norm_one(i, carry):
+        rows = pl.ds(pl.multiple_of(i * part_rows, part_rows), part_rows)
+        x0 = x_in[rows].astype(f32)
+        r1 = lax.rsqrt(jnp.mean(x0 * x0, axis=1, keepdims=True) + eps_norm)
+        n1 = x0 * r1
+        g = dh1[rows].astype(f32) + dh1_side[rows].astype(f32)
+        row_sum[0:1, :] += jnp.sum(g * n1, axis=0, keepdims=True)
+        scaled = g * gain_one
+        mean = jnp.mean(scaled * n1, axis=1, keepdims=True)
+        grad_in[rows] = dx1[rows] + r1 * (scaled - n1 * mean)
+        return carry
+
+    lax.fori_loop(0, tokens // part_rows, norm_one, 0)
+    lanes = width // 128
+    tail[...] = jnp.zeros_like(tail)
+    for which in range(2):
+        for k in range(lanes):
+            row = which * lanes + k
+            tail[row : row + 1, :] = row_sum[which : which + 1, k * 128 : (k + 1) * 128]
+    tail[2 * lanes : 2 * lanes + 2, :] = qk_acc[0:2, :] + qk_side[0:2, :]
+    start((5,))
+    run(lambda k: along(visit(order, nz, k - 1)))
+    along(f // 2)
+    run_direct()
+    land()
+
+    def put_out(rows, value):
+        block_out[rows] = (x_mid[rows] + value).astype(bf16)
+
+    finish_sum(put_out)
+    drain()
+    drain_sum()
+    for i in range(4):
+        dh1_copy(i).wait_send()
+    swap_qk.wait_send()
+
+
+def visit_code(nz, z):
+    order = 0
+    for at, seq in enumerate(visiting_order(nz)):
+        code = sum(u * nz**i for i, u in enumerate(seq))
+        order = order + code * (z == at).astype(jnp.int32)
+    return order
+
+
+def visit(code, nz, i):
+    for k in range(nz):
+        code = jnp.where(i > k, code // nz, code)
+    return lax.rem(code, nz)
+
+
+SUM_CUT = 2
+
+
+def token_sum(nf, partial, own, total_ref, bufs, sems):
+    from_partner, from_across, from_z, from_side = bufs
+    load_sem, p_send, p_recv, x_send, x_recv, z_send, z_recv, s_send, s_recv = sems
+    nz = nf // 2
+    f, c, t = lax.axis_index("fsdp"), lax.axis_index("ctx"), lax.axis_index("tp")
+    z, x = f // 2, lax.rem(f, 2)
+    has_up, has_down = z + 1 < nz, z > 0
+    up, down = (f + 2, c, t), (f - 2, c, t)
+    across_dev, partner, side = (z * 2 + 1 - x, c, t), (f, 1 - c, t), (f, c, 1 - t)
+    tokens = total_ref.shape[0]
+    rows = tokens // SUM_CUT
+    bf16 = jnp.bfloat16
+
+    def chunk(q):
+        return pl.ds(q * rows, rows)
+
+    def remote(src, dst, send, recv, dev):
+        return pltpu.make_async_remote_copy(
+            src_ref=src,
+            dst_ref=dst,
+            send_sem=send,
+            recv_sem=recv,
+            device_id=dev,
+            device_id_type=MESH,
+        )
+
+    own_loads = [
+        pltpu.make_async_copy(
+            partial.at[pl.ds((2 * b + c) * tokens, tokens)], own.at[b], load_sem.at[b]
+        )
+        for b in range(nf)
+    ]
+
+    def p_copy(u, xx, q):
+        b = u * 2 + xx
+        return remote(
+            partial.at[pl.ds((2 * b + 1 - c) * tokens + q * rows, rows)],
+            from_partner.at[b, chunk(q)],
+            p_send.at[b, q],
+            p_recv.at[b, q],
+            partner,
+        )
+
+    def x_copy(u, q):
+        return remote(
+            own.at[u * 2 + 1 - x, chunk(q)],
+            from_across.at[u, chunk(q)],
+            x_send.at[u, q],
+            x_recv.at[u, q],
+            across_dev,
+        )
+
+    def z_copy(u, q, way, dev):
+        return remote(
+            own.at[u * 2 + x, chunk(q)],
+            from_z.at[way, u, chunk(q)],
+            z_send.at[u, q],
+            z_recv.at[way, u, q],
+            dev,
+        )
+
+    def s_copy(q):
+        return remote(
+            own.at[f, chunk(q)], from_side.at[chunk(q)], s_send.at[q], s_recv.at[q], side
+        )
+
+    def wide(value):
+        return value.astype(jnp.float32)
+
+    def to_partner(u, carry):
+        for xx in range(2):
+            for q in range(SUM_CUT):
+                p_copy(u, xx, q).start()
+        return carry
+
+    def to_across(u, carry):
+        b = u * 2 + 1 - x
+        for q in range(SUM_CUT):
+            for xx in range(2):
+                p_copy(u, xx, q).wait_recv()
+            own[b, chunk(q)] = (wide(own[b, chunk(q)]) + wide(from_partner[b, chunk(q)])).astype(
+                bf16
+            )
+            x_copy(u, q).start()
+        return carry
+
+    def along(u):
+        b = u * 2 + x
+        for q in range(SUM_CUT):
+            x_copy(u, q).wait_recv()
+            total_ref[chunk(q)] = (
+                wide(own[b, chunk(q)])
+                + wide(from_partner[b, chunk(q)])
+                + wide(from_across[u, chunk(q)])
+            )
+
+            @pl.when((u >= z) & has_down)
+            def _():
+                z_copy(u, q, 0, partner).wait_recv()
+                total_ref[chunk(q)] += wide(from_z[0, u, chunk(q)])
+
+            @pl.when((u <= z) & has_up)
+            def _():
+                z_copy(u, q, 1, partner).wait_recv()
+                total_ref[chunk(q)] += wide(from_z[1, u, chunk(q)])
+
+            own[b, chunk(q)] = total_ref[chunk(q)].astype(bf16)
+
+            @pl.when(u > z)
+            def _():
+                z_copy(u, q, 0, up).start()
+
+            @pl.when(u < z)
+            def _():
+                z_copy(u, q, 1, down).start()
+
+            @pl.when(u == z)
+            def _():
+                s_copy(q).start()
+
+    def finish_sum(put):
+        for q in range(SUM_CUT):
+            s_copy(q).wait_recv()
+            put(chunk(q), wide(own[f, chunk(q)]) + wide(from_side[chunk(q)]))
+
+    def drain_sum():
+        def ends(u, carry):
+            for q in range(SUM_CUT):
+                for xx in range(2):
+                    p_copy(u, xx, q).wait_send()
+                x_copy(u, q).wait_send()
+
+                @pl.when(u != z)
+                def _():
+                    z_copy(u, q, 0, partner).wait_send()
+
+            return carry
+
+        lax.fori_loop(0, nz, ends, 0)
+        for q in range(SUM_CUT):
+            s_copy(q).wait_send()
+
+    return own_loads, to_partner, to_across, along, finish_sum, drain_sum
+
+
+def backward_pass(nf, arrays, attended, shapes):
+    f32, bf16 = jnp.float32, jnp.bfloat16
+    tokens, width, heads_width, kv_width, keys = shapes
+    tail_rows = -(-(2 * width // 128 + 2) // 8) * 8
+    shape = jax.ShapeDtypeStruct
+    specs = [
+        Gather(attended, nf, chunks=2),
+        Gather(shape((tokens, heads_width), bf16), nf, chunks=2),
+        Gather(shape((tokens, kv_width), bf16), nf, chunks=1),
+        Gather(shape((tokens, kv_width), bf16), nf, chunks=1),
+        Gather(shape((tokens, 128), bf16), nf, chunks=1),
+        Gather(shape((tail_rows, 128), f32), nf, chunks=1),
+        Gather(shape((nf * tokens, width // nf), bf16), nf, form="a2a", chunks=1),
+    ]
+    n = len(specs)
+    total = sum(s.chunks for s in specs)
+    any_spec = pl.BlockSpec(memory_space=pl.ANY)
+    vmem = pl.BlockSpec(memory_space=pltpu.VMEM)
+    dma = pltpu.SemaphoreType.DMA
+    in_any = {0, 9, 10, 11, 12, 21}
+    nz = nf // 2
+    return pl.pallas_call(
+        functools.partial(backward_kernel, nf, tuple(specs)),
+        out_shape=tuple(shape(s.out_shape(nf), s.array.dtype) for s in specs)
+        + (shape((tokens, width), f32), shape((tokens, width), bf16)),
+        in_specs=[any_spec if i in in_any else vmem for i in range(22)],
+        out_specs=tuple([any_spec] * n + [vmem, vmem]),
+        scratch_shapes=[stage_of(s, nf) for s in specs]
+        + [dma((2 * nf, total)), dma((5, 2 * nf, total)), dma((2, n))]
+        + [
+            pltpu.VMEM((width, max(width, heads_width)), bf16),
+            pltpu.VMEM((width, kv_width), bf16),
+            pltpu.VMEM((width, kv_width), bf16),
+            pltpu.VMEM((tokens, width), f32),
+            pltpu.VMEM((tokens, width), f32),
+            pltpu.VMEM((tokens, width), bf16),
+            pltpu.VMEM((nf * tokens, width // nf), bf16),
+            pltpu.VMEM((tokens, heads_width), bf16),
+            pltpu.VMEM((tokens, heads_width), bf16),
+            pltpu.VMEM((tokens, kv_width), bf16),
+            pltpu.VMEM((tokens, kv_width), bf16),
+            pltpu.VMEM((tokens, 128), bf16),
+            pltpu.VMEM((tail_rows, 128), f32),
+            pltpu.VMEM((keys, kv_width), f32),
+            pltpu.VMEM((keys, kv_width), f32),
+            pltpu.VMEM((8, 128), f32),
+            pltpu.VMEM((tokens, 2 * kv_width), bf16),
+            pltpu.VMEM((tokens, 2 * kv_width), bf16),
+            pltpu.VMEM((tokens, width), bf16),
+            pltpu.VMEM((tokens, width), bf16),
+            pltpu.VMEM((8, 128), f32),
+            pltpu.VMEM((2, width), f32),
+            dma((3,)),
+            dma((2,)),
+            dma((5,)),
+            dma((5,)),
+            pltpu.VMEM((nf, tokens, width), bf16),
+            pltpu.VMEM((tokens, width), f32),
+            pltpu.VMEM((nf, tokens, width), bf16),
+            pltpu.VMEM((nz, tokens, width), bf16),
+            pltpu.VMEM((2, nz, tokens, width), bf16),
+            pltpu.VMEM((tokens, width), bf16),
+            dma((nf,)),
+            dma((nf, SUM_CUT)),
+            dma((nf, SUM_CUT)),
+            dma((nz, SUM_CUT)),
+            dma((nz, SUM_CUT)),
+            dma((nz, SUM_CUT)),
+            dma((2, nz, SUM_CUT)),
+            dma((SUM_CUT,)),
+            dma((SUM_CUT,)),
+        ],
+        compiler_params=pltpu.CompilerParams(
+            collective_id=8, has_side_effects=True, vmem_limit_bytes=67043328
+        ),
+    )(attended, *arrays)
+
+
 def norm_forward(values, gain_row):
     inverse = lax.rsqrt(jnp.mean(values * values, axis=-1, keepdims=True) + eps_norm)
     normed = values * inverse
@@ -1218,96 +1806,142 @@
     grad_gate = jnp.einsum("jrd,jrf->jdf", rows_in, grad_gate_pre, preferred_element_type=f32)
     grad_up = jnp.einsum("jrd,jrf->jdf", rows_in, grad_up_pre, preferred_element_type=f32)
 
-    block_out = (resid_mid + sum_over_tp(block_sum(moe_partial, nf))).astype(bf16)
-
-    grad_rows = grad_out.astype(f32)
-    grad_logits = (
-        probs * (grad_prob - jnp.sum(probs * grad_prob, axis=1, keepdims=True))
-    ).astype(bf16)
-    grad_hidden_two = grad_hidden_moe + jnp.einsum(
-        "te,de->td", grad_logits, router_weight, preferred_element_type=f32
-    )
-    grad_ffn_local = jnp.sum(grad_hidden_two * normed_two, axis=0)
-    grad_mid = grad_rows + rms_norm_gradient(grad_hidden_two, normed_two, inverse_two, gain_two)
-    grad_proj = grad_mid.astype(bf16)
-    attended_gradient = jnp.einsum(
-        "td,qd->tq", grad_proj, out_weight, preferred_element_type=f32
-    ).astype(bf16)
-    attended_gradient = attended_gradient.reshape(
-        tokens_dev, kv_local, query_group_width, HEAD_SIZE
-    )
-    probs_att = jnp.exp(scores - log_total)
-    grad_value_all = jnp.einsum(
-        "kgqs,qkgd->skd", weights_att, attended_gradient, preferred_element_type=f32
-    )
-    grad_probs = jnp.einsum(
-        "qkgd,skd->kgqs", attended_gradient, value_all, preferred_element_type=f32
-    )
-    delta_row = jnp.sum(probs_att * grad_probs, axis=-1, keepdims=True)
-    grad_scores = (probs_att * (grad_probs - delta_row) * HEAD_SIZE ** (-0.5)).astype(bf16)
-    grad_query_rot = jnp.einsum(
-        "kgqs,skd->qkgd", grad_scores, key_all, preferred_element_type=f32
-    ).reshape(tokens_dev, head_local, HEAD_SIZE)
-    grad_key_all = jnp.einsum(
-        "kgqs,qkgd->skd", grad_scores, query_rotated, preferred_element_type=f32
-    )
-    grad_kv_all = jnp.concatenate(
-        [grad_key_all.reshape(-1, kv_width), grad_value_all.reshape(-1, kv_width)], axis=1
-    )
-    theirs = lax.dynamic_slice_in_dim(grad_kv_all, (1 - c_index) * tokens_dev, tokens_dev, axis=0)
-    mine = lax.dynamic_slice_in_dim(grad_kv_all, c_index * tokens_dev, tokens_dev, axis=0)
-    grad_kv = mine + swap(theirs.astype(bf16), "ctx").astype(f32)
-    key_rotated_gradient = grad_kv[:, :kv_width].reshape(tokens_dev, kv_local, HEAD_SIZE)
-    grad_query_norm = inverse_rotation(grad_query_rot, cosine_table, sine_values)
-    key_normed_gradient = inverse_rotation(key_rotated_gradient, cosine_table, sine_values)
-    grad_qk_local = jnp.concatenate(
-        [
-            jnp.sum(grad_query_norm * query_hat, axis=(0, 1)),
-            jnp.sum(key_normed_gradient * key_unit_rows, axis=(0, 1)),
-        ]
-    )
-    grad_query_raw = (
-        rms_norm_gradient(grad_query_norm, query_hat, query_inverse, gain_query)
-        .astype(bf16)
-        .reshape(tokens_dev, head_local * HEAD_SIZE)
-    )
-    key_projected_gradient = (
-        rms_norm_gradient(key_normed_gradient, key_unit_rows, key_inverse_norm, gain_key)
-        .astype(bf16)
-        .reshape(tokens_dev, kv_width)
-    )
-    value_projected_gradient = grad_kv[:, kv_width:].astype(bf16)
-    grad_hidden_part = jnp.einsum(
-        "tq,dq->td", grad_query_raw, query_weight, preferred_element_type=f32
-    )
-    grad_hidden_part = grad_hidden_part + jnp.einsum(
-        "tq,dq->td", key_projected_gradient, key_weight, preferred_element_type=f32
-    )
-    grad_hidden_part = grad_hidden_part + jnp.einsum(
-        "tq,dq->td", value_projected_gradient, value_weight, preferred_element_type=f32
-    )
-    grad_hidden_one = sum_over_tp(grad_hidden_part)
-    grad_in = grad_mid + rms_norm_gradient(grad_hidden_one, normed_one, inverse_one, gain_one)
-    grad_attn_local = jnp.sum(grad_hidden_one * normed_one, axis=0)
-    grad_qk_local = grad_qk_local + swap(grad_qk_local, "tp")
-    tail = jnp.concatenate([grad_attn_local, grad_ffn_local, grad_qk_local])
-    tail = jnp.pad(tail, (0, -tail.shape[0] % 1024)).reshape(-1, 128)
-    tail_rows = tail.shape[0]
-    logit_pad = jnp.pad(grad_logits, ((0, 0), (0, -experts % 128)))
-
-    dq_all, dk_all, dv_all, attended_all, proj_slice, logits_all, tail_all = plane_gather(
-        [
-            Gather(grad_query_raw, nf, chunks=2),
-            Gather(key_projected_gradient, nf, chunks=1),
-            Gather(value_projected_gradient, nf, chunks=1),
-            Gather(attended, nf, chunks=2),
-            Gather(by_shard(grad_proj, nf), nf, form="a2a", chunks=1),
-            Gather(logit_pad, nf, chunks=1),
-            Gather(tail, nf, chunks=1),
-        ],
-        3,
-        nf,
-    )
+    if nf == 8:
+        gains = jnp.stack([gain_one, gain_two, jnp.pad(gain_qk, (0, width_dim - gain_qk.shape[0]))])
+        cosine_row, sine_row = cosine_table[:, 0], sine_values[:, 0]
+        trig = jnp.stack(
+            [
+                jnp.concatenate([cosine_row, cosine_row], axis=1),
+                jnp.concatenate([sine_row, -sine_row], axis=1),
+            ]
+        )
+        operands = (
+            grad_hidden_moe,
+            grad_prob,
+            probs,
+            router_weight,
+            hidden_in,
+            resid_mid,
+            gains,
+            grad_out,
+            out_weight,
+            query_weight,
+            key_weight,
+            value_weight,
+            query_raw.reshape(tokens_dev, -1),
+            key_projected.reshape(tokens_dev, -1),
+            query_rotated.reshape(tokens_dev, -1),
+            key_all.reshape(-1, kv_width),
+            value_all.reshape(-1, kv_width),
+            jnp.where(allowed, 0.0, -jnp.inf),
+            log_total.reshape(head_local, tokens_dev, 1),
+            trig,
+            moe_partial,
+        )
+        shapes = (tokens_dev, width_dim, head_local * HEAD_SIZE, kv_width, key_all.shape[0])
+        (
+            attended_all,
+            dq_all,
+            dk_all,
+            dv_all,
+            logits_all,
+            tail_all,
+            proj_slice,
+            grad_in,
+            block_out,
+        ) = backward_pass(nf, operands, attended, shapes)
+        tail_rows = tail_all.shape[0] // devices
+    else:
+        block_out = (resid_mid + sum_over_tp(block_sum(moe_partial, nf))).astype(bf16)
+
+        grad_rows = grad_out.astype(f32)
+        grad_logits = (
+            probs * (grad_prob - jnp.sum(probs * grad_prob, axis=1, keepdims=True))
+        ).astype(bf16)
+        grad_hidden_two = grad_hidden_moe + jnp.einsum(
+            "te,de->td", grad_logits, router_weight, preferred_element_type=f32
+        )
+        grad_ffn_local = jnp.sum(grad_hidden_two * normed_two, axis=0)
+        grad_mid = grad_rows + rms_norm_gradient(grad_hidden_two, normed_two, inverse_two, gain_two)
+        grad_proj = grad_mid.astype(bf16)
+        attended_gradient = jnp.einsum(
+            "td,qd->tq", grad_proj, out_weight, preferred_element_type=f32
+        ).astype(bf16)
+        attended_gradient = attended_gradient.reshape(
+            tokens_dev, kv_local, query_group_width, HEAD_SIZE
+        )
+        probs_att = jnp.exp(scores - log_total)
+        grad_value_all = jnp.einsum(
+            "kgqs,qkgd->skd", weights_att, attended_gradient, preferred_element_type=f32
+        )
+        grad_probs = jnp.einsum(
+            "qkgd,skd->kgqs", attended_gradient, value_all, preferred_element_type=f32
+        )
+        delta_row = jnp.sum(probs_att * grad_probs, axis=-1, keepdims=True)
+        grad_scores = (probs_att * (grad_probs - delta_row) * HEAD_SIZE ** (-0.5)).astype(bf16)
+        grad_query_rot = jnp.einsum(
+            "kgqs,skd->qkgd", grad_scores, key_all, preferred_element_type=f32
+        ).reshape(tokens_dev, head_local, HEAD_SIZE)
+        grad_key_all = jnp.einsum(
+            "kgqs,qkgd->skd", grad_scores, query_rotated, preferred_element_type=f32
+        )
+        grad_kv_all = jnp.concatenate(
+            [grad_key_all.reshape(-1, kv_width), grad_value_all.reshape(-1, kv_width)], axis=1
+        )
+        theirs = lax.dynamic_slice_in_dim(grad_kv_all, (1 - c_index) * tokens_dev, tokens_dev, axis=0)
+        mine = lax.dynamic_slice_in_dim(grad_kv_all, c_index * tokens_dev, tokens_dev, axis=0)
+        grad_kv = mine + swap(theirs.astype(bf16), "ctx").astype(f32)
+        key_rotated_gradient = grad_kv[:, :kv_width].reshape(tokens_dev, kv_local, HEAD_SIZE)
+        grad_query_norm = inverse_rotation(grad_query_rot, cosine_table, sine_values)
+        key_normed_gradient = inverse_rotation(key_rotated_gradient, cosine_table, sine_values)
+        grad_qk_local = jnp.concatenate(
+            [
+                jnp.sum(grad_query_norm * query_hat, axis=(0, 1)),
+                jnp.sum(key_normed_gradient * key_unit_rows, axis=(0, 1)),
+            ]
+        )
+        grad_query_raw = (
+            rms_norm_gradient(grad_query_norm, query_hat, query_inverse, gain_query)
+            .astype(bf16)
+            .reshape(tokens_dev, head_local * HEAD_SIZE)
+        )
+        key_projected_gradient = (
+            rms_norm_gradient(key_normed_gradient, key_unit_rows, key_inverse_norm, gain_key)
+            .astype(bf16)
+            .reshape(tokens_dev, kv_width)
+        )
+        value_projected_gradient = grad_kv[:, kv_width:].astype(bf16)
+        grad_hidden_part = jnp.einsum(
+            "tq,dq->td", grad_query_raw, query_weight, preferred_element_type=f32
+        )
+        grad_hidden_part = grad_hidden_part + jnp.einsum(
+            "tq,dq->td", key_projected_gradient, key_weight, preferred_element_type=f32
+        )
+        grad_hidden_part = grad_hidden_part + jnp.einsum(
+            "tq,dq->td", value_projected_gradient, value_weight, preferred_element_type=f32
+        )
+        grad_hidden_one = sum_over_tp(grad_hidden_part)
+        grad_in = grad_mid + rms_norm_gradient(grad_hidden_one, normed_one, inverse_one, gain_one)
+        grad_attn_local = jnp.sum(grad_hidden_one * normed_one, axis=0)
+        grad_qk_local = grad_qk_local + swap(grad_qk_local, "tp")
+        tail = jnp.concatenate([grad_attn_local, grad_ffn_local, grad_qk_local])
+        tail = jnp.pad(tail, (0, -tail.shape[0] % 1024)).reshape(-1, 128)
+        tail_rows = tail.shape[0]
+        logit_pad = jnp.pad(grad_logits, ((0, 0), (0, -experts % 128)))
+
+        dq_all, dk_all, dv_all, attended_all, proj_slice, logits_all, tail_all = plane_gather(
+            [
+                Gather(grad_query_raw, nf, chunks=2),
+                Gather(key_projected_gradient, nf, chunks=1),
+                Gather(value_projected_gradient, nf, chunks=1),
+                Gather(attended, nf, chunks=2),
+                Gather(by_shard(grad_proj, nf), nf, form="a2a", chunks=1),
+                Gather(logit_pad, nf, chunks=1),
+                Gather(tail, nf, chunks=1),
+            ],
+            3,
+            nf,
+        )
     over_tokens = functools.partial(
         jnp.einsum, "td,tq->dq", preferred_element_type=f32
     )

time: 610 us -> 580 us (0.951)
  the two profiles are of different devices: /device:TPU:0 before, /device:TPU:10 now
where the time goes in v3:
time: 580 us; the launch traced here: 574 us
  Pallas kernels  469 us (81%)
  matrix products  64 us (11%)
  local copies, waits for them, and re-layouts  18.9 us (3%)
  other arithmetic  13.2 us (2%)
    pallas_call x1, Pallas kernels, backward_pass(): pl.pallas_call(functools.partial(backward_kernel, nf, tuple(specs)), out_...  181 us
    pallas_call x1, Pallas kernels, expert_pass(): pl.pallas_call(functools.partial(expert_kernel, nf, capacity, tuple(specs...  154 us
    pallas_call x1, Pallas kernels, plane_gather(): pl.pallas_call(functools.partial(gather_kernel, nf, tuple(specs)), out_sh...  134 us
  transfers between devices with their start and end apart: 1, of which 1 were waited for; matrix products, arithmetic and copies ran while one was open for 2% of the time, Pallas kernels for 0%

profile of v3, /device:TPU:10, one launch (start us, length us, event | category | flops | bytes accessed | tf_op | source)
XLA Modules:
  0.0 574.3 jit_solution(225037818891517825)
XLA Ops:
  1.6 1.3 fusion.24.refs_0_
  2.9 133.8 %shard_map.246 = (bf16[1280,128]{1,0:T(8,128)(2,1)}, bf16[2048,2048]{1,0:T(8,128)(2,1)}, bf16[2048,256]{1,0:T(8,128)(2,1)}, bf16[2048,256]{1,0:T(8,128)(2,1)}, b...) custom-call(bf16[80,128]{1,0:T(8,128)(2,1)} %fusion.24.refs_0_, bf16[256,2048]{1,0:T(8,128)(2,1)} %refs_1_.1, ...), custom_call_target="tpu_custom_call" | custom-call | tf_op jit(solution)/shard_map/pallas_call | solution.py:428
  136.8 1.1 reshape.292
  138.1 1.2 fusion
  139.4 1.2 fusion.2
  140.6 1.5 fusion.37.refs_14_
  144.0 3.2 all_gather.3
  147.7 4.6 fusion.38.refs_13_
  152.4 1.0 copy-done.1
  157.7 1.4 convolution_convert_fusion.1
  159.2 5.5 convolution_convert_fusion
  165.9 1.0 copy.133.refs_0_
  167.3 1.3 reshape.298.refs_4_
  168.9 0.9 copy.118
  169.8 1.3 copy.120.refs_19_
  171.1 0.9 copy.151
  173.5 1.4 broadcast_select_fusion.refs_18_
  174.9 4.3 collective-permute-done
  179.2 1.5 multiply_reduce_fusion
  180.8 1.0 copy-done
  184.8 153.7 %shard_map.247 = (bf16[2048,2048]{1,0:T(8,128)(2,1)}, f32[512,128]{1,0:T(8,128)}, bf16[2048,256]{1,0:T(8,128)(2,1)}, bf16[2048,2048]{1,0:T(8,128)(2,1)}, bf16[2,...) custom-call(bf16[128,2048]{1,0:T(8,128)(2,1)} %copy-done.9, ...), custom_call_target="tpu_custom_call" | custom-call | tf_op jit(solution)/shard_map/pallas_call | solution.py:934
  338.6 11.2 %fusion.45 = f32[2,2048,384]{2,1,0:T(8,128)} fusion(bf16[2,1024,2048]{2,1,0:T(8,128)(2,1)} %get-tuple-element.58, bf16[2,1024,384]{2,1,0:T(8,128)(2,1)} %get-tuple-element.60), kind=kOutput, calls=%fused_computation.96 | convolution fusion | flops 3221225472 | bytes 16252928 | tf_op jit(solution)/shard_map/jrd,jrf->jdf/dot_general | solution.py:1807
  349.8 6.4 %fusion.44 = f32[2,2048,384]{2,1,0:T(8,128)} fusion(bf16[2,1024,2048]{2,1,0:T(8,128)(2,1)S(1)} %copy-done.19, bf16[2,1024,384]{2,1,0:T(8,128)(2,1)S(1)} %copy-done.20), kind=kOutput, calls=%fused_computation.95 | convolution fusion | flops 3221225472 | bytes 16252928 | tf_op jit(solution)/shard_map/jrd,jrf->jdf/dot_general | solution.py:1806
  356.2 0.8 slice.70
  357.8 181.1 %shard_map.248 = (bf16[2048,2048]{1,0:T(8,128)(2,1)}, bf16[2048,2048]{1,0:T(8,128)(2,1)}, bf16[2048,256]{1,0:T(8,128)(2,1)}, bf16[2048,256]{1,0:T(8,128)(2,1)}, ...) custom-call(bf16[128,2048]{1,0:T(8,128)(2,1)} %copy.133.refs_0_, ...), custom_call_target="tpu_custom_call" | custom-call | tf_op jit(solution)/shard_map/pallas_call | solution.py:1462
  538.9 2.7 fusion.42
  541.6 2.7 fusion.41
  544.3 7.5 %fusion.40 = f32[256,2048]{1,0:T(8,128)} fusion(bf16[2048,256]{1,0:T(8,128)(2,1)} %get-tuple-element.50, bf16[2048,2048]{1,0:T(8,128)(2,1)} %get-tuple-element.51), kind=kOutput, calls=%fused_computation.91 | convolution fusion | flops 2147483648 | bytes 11534336 | tf_op jit(solution)/shard_map/td,tq->dq/dot_general | solution.py:1948
  552.0 9.6 %fusion.46 = f32[2,384,2048]{2,1,0:T(8,128)} fusion(bf16[2,1024,384]{2,1,0:T(8,128)(2,1)S(1)} %copy-done.3, bf16[2,1024,2048]{2,1,0:T(8,128)(2,1)} %get-tuple-element.62), kind=kOutput, calls=%fused_computation.97 | convolution fusion | flops 3221225472 | bytes 16252928 | tf_op jit(solution)/shard_map/jrf,jrd->jfd/dot_general | solution.py:1805
  561.6 7.3 %fusion.43 = f32[2048,256]{1,0:T(8,128)} fusion(bf16[2048,2048]{1,0:T(8,128)(2,1)} %get-tuple-element.54, bf16[2048,256]{1,0:T(8,128)(2,1)S(1)} %copy-done.21), kind=kOutput, calls=%fused_computation.94 | convolution fusion | flops 2147483648 | bytes 11534336 | tf_op jit(solution)/shard_map/td,tq->dq/dot_general | solution.py:1951
  570.2 2.2 fusion.3
  573.1 1.0 copy.157
  (117 shorter events, 16.7 us)
Async XLA Ops:
  0.6 143.3 %copy-start.23 = (s32[128]{0:T(128)S(1)}, s32[128]{0:T(128)}, u32[]{:S(2)}) copy-start(s32[128]{0:T(128)} %param.16) | copy-start | bytes 1540
  136.8 6.8 %copy-start.10 = (bf16[2048,256]{1,0:T(8,128)(2,1)S(1)}, bf16[2048,256]{1,0:T(8,128)(2,1)}, u32[]{:S(2)}) copy-start(bf16[2048,256]{1,0:T(8,128)(2,1)} %get-tuple-element.40.refs_12_) | copy-start | bytes 3145732
  138.1 14.3 %copy-start.18 = (s32[128]{0:T(128)}, s32[128]{0:T(128)S(1)}, u32[]{:S(2)}) copy-start(s32[128]{0:T(128)S(1)} %iota_add_fusion) | copy-start | bytes 1540
  142.1 10.2 %copy-start.13 = (f32[128,256]{1,0:T(8,128)}, f32[128,256]{1,0:T(8,128)S(1)}, u32[]{:S(2)}) copy-start(f32[128,256]{1,0:T(8,128)S(1)} %fusion.37.refs_14_) | copy-start | bytes 393220
  147.4 5.0 copy-start.11
  147.4 9.5 %copy-start.12 = (bf16[256,256]{1,0:T(8,128)(2,1)}, bf16[256,256]{1,0:T(8,128)(2,1)S(1)}, u32[]{:S(2)}) copy-start(bf16[256,256]{1,0:T(8,128)(2,1)S(1)} %get-tuple-element.68.refs_17_) | copy-start | bytes 393220
  152.4 1.0 copy-start.1
  155.1 0.8 copy-start.5
  155.1 1.0 copy-start.7
  159.1 7.8 %copy-start.6 = (bf16[128,16,64]{2,1,0:T(8,128)(2,1)S(1)}, bf16[128,16,64]{2,1,0:T(8,128)(2,1)}, u32[]{:S(2)}) copy-start(bf16[128,16,64]{2,1,0:T(8,128)(2,1)} %copy-done.5) | copy-start | bytes 786436
  159.2 7.8 %copy-start.8 = (bf16[128,16,64]{2,1,0:T(8,128)(2,1)S(1)}, bf16[128,16,64]{2,1,0:T(8,128)(2,1)}, u32[]{:S(2)}) copy-start(bf16[128,16,64]{2,1,0:T(8,128)(2,1)} %copy-done.7) | copy-start | bytes 786436
  159.2 9.4 %copy-start.17 = (s32[128,8]{0,1:T(8,128)S(1)}, s32[128,8]{0,1:T(8,128)}, u32[]{:S(2)}) copy-start(s32[128,8]{0,1:T(8,128)} %param.17) | copy-start | bytes 12292
  164.7 14.5 %copy-start.2 = (bf16[128,2048]{1,0:T(8,128)(2,1)S(1)}, bf16[128,2048]{1,0:T(8,128)(2,1)}, u32[]{:S(2)}) copy-start(bf16[128,2048]{1,0:T(8,128)(2,1)} %refs_5_.5) | copy-start | bytes 1572868
  164.7 14.5 %collective-permute-start = (bf16[128,2048]{1,0:T(8,128)(2,1)}, bf16[128,2048]{1,0:T(8,128)(2,1)}, u32[]{:S(2)}, u32[]{:S(2)}) collective-permute-start(bf16[128,2048]{1,0:T(8,128)(2,1)} %convolution_convert_fusion), channel_id=1, source_target_pairs={{0,1},{1,0},{2,3},{3,2},{4,5},{5,4},{6,7},{7,6},{8,9},{9,8},{10,11... | collective-permute-start | bytes 1572872 | tf_op jit(solution)/shard_map/ppermute | solution.py:1572
  168.6 13.3 %copy-start.4 = (bf16[2048,32]{1,0:T(8,128)(2,1)}, bf16[2048,32]{1,0:T(8,128)(2,1)S(1)}, u32[]{:S(2)}) copy-start(bf16[2048,32]{1,0:T(8,128)(2,1)S(1)} %reshape.298.refs_4_) | copy-start | bytes 393220
  180.8 1.0 copy-start
  181.9 0.8 copy-start.9
  338.6 11.2 %copy-start.19 = (bf16[2,1024,2048]{2,1,0:T(8,128)(2,1)S(1)}, bf16[2,1024,2048]{2,1,0:T(8,128)(2,1)}, u32[]{:S(2)}) copy-start(bf16[2,1024,2048]{2,1,0:T(8,128)(2,1)} %get-tuple-element.58) | copy-start | bytes 25165828
  338.6 11.2 %copy-start.20 = (bf16[2,1024,384]{2,1,0:T(8,128)(2,1)S(1)}, bf16[2,1024,384]{2,1,0:T(8,128)(2,1)}, u32[]{:S(2)}) copy-start(bf16[2,1024,384]{2,1,0:T(8,128)(2,1)} %get-tuple-element.59) | copy-start | bytes 4718596
  544.3 7.5 %copy-start.16 = (f32[640,128]{1,0:T(8,128)S(1)}, f32[640,128]{1,0:T(8,128)}, u32[]{:S(2)}) copy-start(f32[640,128]{1,0:T(8,128)} %get-tuple-element.49) | copy-start | bytes 983044
  544.3 7.6 %copy-start.3 = (bf16[2,1024,384]{2,1,0:T(8,128)(2,1)S(1)}, bf16[2,1024,384]{2,1,0:T(8,128)(2,1)}, u32[]{:S(2)}) copy-start(bf16[2,1024,384]{2,1,0:T(8,128)(2,1)} %get-tuple-element.61) | copy-start | bytes 4718596
  552.0 9.7 %copy-start.21 = (bf16[2048,256]{1,0:T(8,128)(2,1)S(1)}, bf16[2048,256]{1,0:T(8,128)(2,1)}, u32[]{:S(2)}) copy-start(bf16[2048,256]{1,0:T(8,128)(2,1)} %get-tuple-element.55) | copy-start | bytes 3145732
  561.6 8.6 %copy-start.22 = (bf16[2048,128]{1,0:T(8,128)(2,1)S(1)}, bf16[2048,128]{1,0:T(8,128)(2,1)}, u32[]{:S(2)}) copy-start(bf16[2048,128]{1,0:T(8,128)(2,1)} %get-tuple-element.57) | copy-start | bytes 1572868
  561.6 10.7 %copy-start.15 = (bf16[128,2048]{1,0:T(8,128)(2,1)S(1)}, bf16[128,2048]{1,0:T(8,128)(2,1)}, u32[]{:S(2)}) copy-start(bf16[128,2048]{1,0:T(8,128)(2,1)} %get-tuple-element.99) | copy-start | bytes 1572868
  561.6 11.5 %copy-start.14 = (f32[128,2048]{1,0:T(8,128)S(1)}, f32[128,2048]{1,0:T(8,128)}, u32[]{:S(2)}) copy-start(f32[128,2048]{1,0:T(8,128)} %get-tuple-element.100) | copy-start | bytes 3145732

commit v4 on v3

--- a/solution.py
+++ b/solution.py
@@ -289,6 +289,37 @@
                 aside(nz - 2, a, q)
         for a, q in relays[count - 2 * lag if by_chunk else 0 :]:
             aside(nz - 1, a, q)
+
+    def step_of(k, only):
+        some = [(a, q) for a, q in relays if a in only]
+        for a, q in some:
+            column(k, a, q)
+        for a, q in some:
+            across(k - 1, a, q)
+
+        if k > 1:
+            for a, q in some:
+                aside(k - 2, a, q)
+
+    def edge_of(only):
+        some = [(a, q) for a, q in relays if a in only]
+        for a, q in some:
+            across(nz - 1, a, q)
+        for a, q in some:
+            aside(nz - 2, a, q)
+        for a, q in some:
+            aside(nz - 1, a, q)
+
+    def land_of(only):
+        def take(bf, carry):
+            for a, q in relays:
+                if a in only:
+                    arrived(a, q, bf, 1 - c)
+            return carry
+
+        lax.fori_loop(0, nf, take, 0)
+        for a in only:
+            own_out(a).wait()
 
     def run_direct():
         for a, q in direct:
@@ -353,7 +384,7 @@
             if specs[a].form == "a2a":
                 own_out(a).wait()
 
-    return start, run, land, start_direct, run_direct, drain
+    return start, run, land, start_direct, run_direct, drain, step_of, edge_of, land_of
 
 
 def gather_kernel(nf, specs, *refs):
@@ -405,7 +436,7 @@
             barrier, greeted + 1 + has_up.astype(jnp.int32) + has_down.astype(jnp.int32)
         )
 
-    start, run, land, start_direct, run_direct, drain = gather_engine(
+    start, run, land, start_direct, run_direct, drain, *_ = gather_engine(
         nf, specs, ins, outs, scratch[:n], *scratch[n:]
     )
     start()
@@ -528,7 +559,7 @@
     pl.semaphore_signal(barrier, 1, device_id=side, device_id_type=MESH)
     pl.semaphore_wait(barrier, 2 * nf)
 
-    start, run, land, start_direct, run_direct, drain = gather_engine(
+    start, run, land, start_direct, run_direct, drain, *_ = gather_engine(
         nf, specs, ins, gathered, stage, recv, send, local
     )
     start()
@@ -991,6 +1022,7 @@
 
 NT = (((1,), (1,)), ((), ()))
 TN = (((0,), (0,)), ((), ()))
+NN = (((1,), (0,)), ((), ()))
 
 
 def backward_kernel(nf, specs, *refs):
@@ -1075,9 +1107,10 @@
     pl.semaphore_wait(barrier, nf + 1)
 
     ins = (attended, d_query, d_key, d_value, logit, tail, d_out_slices)
-    start, run, land, start_direct, run_direct, drain = gather_engine(
+    start, run, land, start_direct, run_direct, drain, step_of, edge_of, _ = gather_engine(
         nf, specs, ins, gathered, stage, recv, send, local
     )
+    early, late = (0,), (1, 2, 3, 4, 5)
     nz = nf // 2
     order = visit_code(nz, f // 2)
     own_loads, to_partner, to_across, along, finish_sum, drain_sum = token_sum(
@@ -1104,7 +1137,7 @@
     for k in range(width // tile):
         cols = slice(k * tile, (k + 1) * tile)
         dh2[:, cols] = dh2_moe[:, cols] + lax.dot_general(
-            dl, router[cols, :], NT, preferred_element_type=f32
+            dl, router[:, cols], NN, preferred_element_type=f32
         )
     gain_one, gain_two = gains[0:1, :], gains[1:2, :]
     gain_query, gain_key = gains[2:3, :HEAD_SIZE], gains[2:3, HEAD_SIZE : 2 * HEAD_SIZE]
@@ -1141,7 +1174,9 @@
     load(wq_hbm, w_big, 0).start()
     for cp in own_loads:
         cp.wait()
-    lax.fori_loop(0, nz, lambda i, carry: to_across(visit(order, nz, i), carry), 0)
+    for i in range(2):
+        to_across(visit(order, nz, i), 0)
+    step_of(1, early)
     dk_acc[...] = jnp.zeros_like(dk_acc)
     dv_acc[...] = jnp.zeros_like(dv_acc)
     qk_acc[...] = jnp.zeros_like(qk_acc)
@@ -1176,7 +1211,12 @@
         d_query[:, cols] = dq.astype(bf16)
         return carry
 
-    lax.fori_loop(0, heads_width // HEAD_SIZE, head, 0)
+    heads = heads_width // HEAD_SIZE
+    lax.fori_loop(0, heads // 2, head, 0)
+    for i in range(2, nz):
+        to_across(visit(order, nz, i), 0)
+    step_of(2, early)
+    lax.fori_loop(heads // 2, heads, head, 0)
 
     kv_width = dk_acc.shape[1]
     theirs = pl.ds(pl.multiple_of((1 - c) * tokens, tokens), tokens)
@@ -1235,6 +1275,8 @@
         dh1[:, rows] = total.astype(bf16)
         if (k + 1) * tile % quarter == 0:
             dh1_copy((k + 1) * tile // quarter - 1).start()
+    step_of(3, early)
+    along(visit(order, nz, 0))
     for i in range(4):
         dh1_copy(i).wait_recv()
     swap_qk.wait_recv()
@@ -1260,7 +1302,13 @@
             tail[row : row + 1, :] = row_sum[which : which + 1, k * 128 : (k + 1) * 128]
     tail[2 * lanes : 2 * lanes + 2, :] = qk_acc[0:2, :] + qk_side[0:2, :]
     start((5,))
-    run(lambda k: along(visit(order, nz, k - 1)))
+    step_of(1, late)
+    edge_of(early)
+    along(visit(order, nz, 1))
+    step_of(2, late)
+    along(visit(order, nz, 2))
+    step_of(3, late)
+    edge_of(late)
     along(f // 2)
     run_direct()
     land()
@@ -1516,6 +1564,315 @@
     )(attended, *arrays)
 
 
+def forward_kernel(nf, specs, *refs):
+    n = len(specs)
+    ins, refs = refs[:n], refs[n:]
+    (x_in, segments, routed, trig), refs = refs[:4], refs[4:]
+    gathered, refs = refs[:n], refs[n:]
+    (
+        hidden,
+        hidden_slices,
+        marks,
+        probs,
+        x_mid,
+        attended,
+        q_raw,
+        k_raw,
+        q_rot,
+        keys,
+        values,
+        bias,
+        lse,
+        gains,
+        router,
+    ), refs = refs[:15], refs[15:]
+    stage, refs = refs[:n], refs[n:]
+    (recv, send, local), refs = refs[:3], refs[3:]
+    (
+        w_big,
+        w_key,
+        w_value,
+        small,
+        hidden_one,
+        kv_all,
+        part,
+        part_side,
+        square,
+        w_sem,
+        kv_sem,
+        side_send,
+        side_recv,
+    ) = refs
+    f32, bf16 = jnp.float32, jnp.bfloat16
+    nz = nf // 2
+    f, c, t = lax.axis_index("fsdp"), lax.axis_index("ctx"), lax.axis_index("tp")
+    z, x = f // 2, lax.rem(f, 2)
+    partner, side = (f, 1 - c, t), (f, c, 1 - t)
+    has_up, has_down = z + 1 < nz, z > 0
+    tokens, width = x_in.shape
+    experts = routed.shape[1]
+    heads_width = q_raw.shape[1]
+    kv_width = k_raw.shape[1]
+    scale = HEAD_SIZE ** (-0.5)
+    barrier = pltpu.get_barrier_semaphore()
+
+    def greet(dev):
+        pl.semaphore_signal(barrier, 1, device_id=dev, device_id_type=MESH)
+
+    for dev in (partner, side, (z * 2 + 1 - x, c, t)):
+        greet(dev)
+
+    @pl.when(has_up)
+    def _():
+        greet((f + 2, c, t))
+
+    @pl.when(has_down)
+    def _():
+        greet((f - 2, c, t))
+
+    pl.semaphore_wait(barrier, 3 + has_up.astype(jnp.int32) + has_down.astype(jnp.int32))
+    start, _, _, _, _, drain, step_of, edge_of, land_of = gather_engine(
+        nf, specs, ins, gathered, stage, recv, send, local
+    )
+    first, second, third = (0, 1, 2, 3), (4,), (5,)
+    start(first)
+    for k in range(1, nz):
+        step_of(k, first)
+    start(second)
+    edge_of(first)
+    land_of(first)
+
+    def load(src, dst, i):
+        return pltpu.make_async_copy(src, dst, w_sem.at[i])
+
+    small_load = load(gathered[0], small, 3)
+    small_load.start()
+    load(gathered[2], w_key, 1).start()
+    load(gathered[3], w_value, 2).start()
+    load(gathered[1], w_big, 0).start()
+    small_load.wait()
+
+    size = specs[0].rows
+    halves = width // nf // 128
+    qk_sum = [jnp.zeros((1, 128), f32), jnp.zeros((1, 128), f32)]
+    for k in range(nf):
+        base = 2 * k * size
+        for h in range(halves):
+            cols = slice((k * halves + h) * 128, (k * halves + h + 1) * 128)
+            router[:, cols] = small[base + h * experts : base + (h + 1) * experts, :]
+            at = base + halves * experts
+            for g in range(2):
+                row = at + g * halves + h
+                gains[g : g + 1, cols] = small[row : row + 1, :].astype(f32)
+        at = base + halves * experts + 2 * halves
+        for h in range(2):
+            qk_sum[h] = qk_sum[h] + small[at + h : at + h + 1, :].astype(f32)
+    gains[2:3, :] = jnp.zeros((1, width), f32)
+    for h in range(2):
+        gains[2:3, h * 128 : (h + 1) * 128] = qk_sum[h]
+    gain_one, gain_two = gains[0:1, :], gains[1:2, :]
+    gain_query, gain_key = qk_sum
+    part_rows = 16
+
+    def norm_one(i, carry):
+        rows = pl.ds(pl.multiple_of(i * part_rows, part_rows), part_rows)
+        x0 = x_in[rows].astype(f32)
+        r1 = lax.rsqrt(jnp.mean(x0 * x0, axis=1, keepdims=True) + eps_norm)
+        hidden_one[rows] = (x0 * r1 * gain_one).astype(bf16)
+        return carry
+
+    lax.fori_loop(0, tokens // part_rows, norm_one, 0)
+    shard = width // nf
+    for k in range(nf):
+        hidden_slices[k * tokens : (k + 1) * tokens, :] = hidden_one[:, k * shard : (k + 1) * shard]
+
+    def norm_rope(raw, gain):
+        inv = lax.rsqrt(jnp.mean(raw * raw, axis=1, keepdims=True) + eps_norm)
+        normed = raw * inv * gain
+        turned = normed * trig[0] - pltpu.roll(normed, HEAD_SIZE // 2, 1) * trig[1]
+        return turned.astype(bf16)
+
+    load(gathered[2], w_key, 1).wait()
+    load(gathered[3], w_value, 2).wait()
+    mine = pl.ds(pl.multiple_of(c * tokens, tokens), tokens)
+    k_raw[...] = jnp.dot(hidden_one[...], w_key[...], preferred_element_type=f32)
+    kv_all[mine, kv_width : 2 * kv_width] = jnp.dot(
+        hidden_one[...], w_value[...], preferred_element_type=f32
+    ).astype(bf16)
+    for kv in range(kv_width // HEAD_SIZE):
+        cols = slice(kv * HEAD_SIZE, (kv + 1) * HEAD_SIZE)
+        kv_all[mine, cols] = norm_rope(k_raw[:, cols], gain_key)
+    kv_all[mine, 2 * kv_width :] = segments[...]
+    swap_kv = pltpu.make_async_remote_copy(
+        src_ref=kv_all.at[mine],
+        dst_ref=kv_all.at[mine],
+        send_sem=kv_sem.at[0],
+        recv_sem=kv_sem.at[1],
+        device_id=partner,
+        device_id_type=MESH,
+    )
+    swap_kv.start()
+    step_of(1, second)
+    load(gathered[1], w_big, 0).wait()
+    tile = 256
+    for k in range(heads_width // tile):
+        cols = slice(k * tile, (k + 1) * tile)
+        q_raw[:, cols] = jnp.dot(hidden_one[...], w_big[:, cols], preferred_element_type=f32)
+    swap_kv.wait()
+    keys[...] = kv_all[:, :kv_width]
+    values[...] = kv_all[:, kv_width : 2 * kv_width]
+    span = kv_all.shape[0]
+    theirs = jnp.transpose(kv_all[:, 2 * kv_width :].astype(f32))
+    own = segments[...].astype(f32)
+    query_at = c * tokens + lax.broadcasted_iota(jnp.int32, (tokens, 128), 0)
+    for h in range(span // 128):
+        cols = slice(h * 128, (h + 1) * 128)
+        key_at = h * 128 + lax.broadcasted_iota(jnp.int32, (tokens, 128), 1)
+        allowed = (key_at <= query_at) & (theirs[:, cols] == own)
+        bias[:, cols] = jnp.where(allowed, 0.0, -jnp.inf)
+    step_of(2, second)
+    group = QUERY_HEADS // KEY_VALUE_HEADS
+
+    def head(h, carry):
+        cols = pl.ds(pl.multiple_of(h * HEAD_SIZE, HEAD_SIZE), HEAD_SIZE)
+        kv_cols = pl.ds(pl.multiple_of((h // group) * HEAD_SIZE, HEAD_SIZE), HEAD_SIZE)
+        q = norm_rope(q_raw[:, cols], gain_query)
+        q_rot[:, cols] = q
+        s = lax.dot_general(q, keys[:, kv_cols], NT, preferred_element_type=f32) * scale
+        s = s + bias[...]
+        top = jnp.max(s, axis=1, keepdims=True)
+        total = top + jnp.log(jnp.sum(jnp.exp(s - top), axis=1, keepdims=True))
+        lse[h] = total
+        prob = jnp.exp(s - total).astype(bf16)
+        attended[:, cols] = jnp.dot(
+            prob, values[:, kv_cols], preferred_element_type=f32
+        ).astype(bf16)
+        return carry
+
+    heads = heads_width // HEAD_SIZE
+    lax.fori_loop(0, heads // 2, head, 0)
+    step_of(3, second)
+    start(third)
+    lax.fori_loop(heads // 2, heads, head, 0)
+    edge_of(second)
+    land_of(second)
+    load(gathered[4], w_big, 0).start()
+    step_of(1, third)
+    load(gathered[4], w_big, 0).wait()
+    quarter = width // 4
+
+    def side_copy(i):
+        cols = pl.ds(i * quarter, quarter)
+        return pltpu.make_async_remote_copy(
+            src_ref=part.at[:, cols],
+            dst_ref=part_side.at[:, cols],
+            send_sem=side_send.at[i],
+            recv_sem=side_recv.at[i],
+            device_id=side,
+            device_id_type=MESH,
+        )
+
+    for k in range(width // tile):
+        cols = slice(k * tile, (k + 1) * tile)
+        part[:, cols] = jnp.dot(
+            attended[...], w_big[:, cols], preferred_element_type=f32
+        ).astype(bf16)
+        if (k + 1) * tile % quarter == 0:
+            side_copy((k + 1) * tile // quarter - 1).start()
+    step_of(2, third)
+    for i in range(4):
+        side_copy(i).wait_recv()
+
+    def norm_two(i, carry):
+        rows = pl.ds(pl.multiple_of(i * part_rows, part_rows), part_rows)
+        x1 = x_in[rows].astype(f32) + (part[rows].astype(f32) + part_side[rows].astype(f32))
+        x_mid[rows] = x1
+        r2 = lax.rsqrt(jnp.mean(x1 * x1, axis=1, keepdims=True) + eps_norm)
+        hidden[rows] = (x1 * r2 * gain_two).astype(bf16)
+        return carry
+
+    lax.fori_loop(0, tokens // part_rows, norm_two, 0)
+    logits = lax.dot_general(hidden[...], router[...], NT, preferred_element_type=f32)
+    on = routed[...] > 0.0
+    kept = jnp.where(on, logits, -jnp.inf)
+    raised = jnp.where(on, jnp.exp(kept - jnp.max(kept, axis=1, keepdims=True)), 0.0)
+    shares = raised / jnp.sum(raised, axis=1, keepdims=True)
+    probs[...] = shares
+    square[...] = jnp.zeros_like(square)
+    square[:, :experts] = jnp.where(on, shares, -1.0)
+    marks[...] = jnp.transpose(square[...])[:experts, :]
+    step_of(3, third)
+    edge_of(third)
+    land_of(third)
+    drain()
+    for i in range(4):
+        side_copy(i).wait_send()
+
+
+def forward_pass(nf, arrays, operands, shapes):
+    f32, bf16 = jnp.float32, jnp.bfloat16
+    small, w_query, key_projection, value_projection, w_out, grad_out = arrays
+    tokens, width, heads_width, kv_width, experts = shapes
+    specs = [
+        Gather(small, nf, chunks=1),
+        Gather(w_query, nf, half=True, chunks=2),
+        Gather(key_projection, nf, half=True, chunks=1),
+        Gather(value_projection, nf, half=True, chunks=1),
+        Gather(w_out, nf, form="col", half=True, chunks=2),
+        Gather(grad_out, nf, rep=True, chunks=4),
+    ]
+    n = len(specs)
+    total = sum(s.chunks for s in specs)
+    any_spec = pl.BlockSpec(memory_space=pl.ANY)
+    vmem = pl.BlockSpec(memory_space=pltpu.VMEM)
+    dma = pltpu.SemaphoreType.DMA
+    shape = jax.ShapeDtypeStruct
+    span = 2 * tokens
+    made = [
+        shape((tokens, width), bf16),
+        shape((nf * tokens, width // nf), bf16),
+        shape((experts, tokens), f32),
+        shape((tokens, experts), f32),
+        shape((tokens, width), f32),
+        shape((tokens, heads_width), bf16),
+        shape((tokens, heads_width), f32),
+        shape((tokens, kv_width), f32),
+        shape((tokens, heads_width), bf16),
+        shape((span, kv_width), bf16),
+        shape((span, kv_width), bf16),
+        shape((tokens, span), f32),
+        shape((heads_width // HEAD_SIZE, tokens, 1), f32),
+        shape((3, width), f32),
+        shape((experts, width), bf16),
+    ]
+    return pl.pallas_call(
+        functools.partial(forward_kernel, nf, tuple(specs)),
+        out_shape=tuple(shape(s.out_shape(nf), s.array.dtype) for s in specs) + tuple(made),
+        in_specs=[any_spec] * n + [vmem] * 4,
+        out_specs=tuple([any_spec] * n + [vmem] * len(made)),
+        scratch_shapes=[stage_of(s, nf) for s in specs]
+        + [dma((2 * nf, total)), dma((5, 2 * nf, total)), dma((2, n))]
+        + [
+            pltpu.VMEM((width, max(width, heads_width)), bf16),
+            pltpu.VMEM((width, kv_width), bf16),
+            pltpu.VMEM((width, kv_width), bf16),
+            pltpu.VMEM(specs[0].out_shape(nf), bf16),
+            pltpu.VMEM((tokens, width), bf16),
+            pltpu.VMEM((span, 2 * kv_width + 128), bf16),
+            pltpu.VMEM((tokens, width), bf16),
+            pltpu.VMEM((tokens, width), bf16),
+            pltpu.VMEM((tokens, 128), f32),
+            dma((4,)),
+            dma((2,)),
+            dma((4,)),
+            dma((4,)),
+        ],
+        compiler_params=pltpu.CompilerParams(
+            collective_id=9, has_side_effects=True, vmem_limit_bytes=67043328
+        ),
+    )(*arrays, *operands)
+
+
 def norm_forward(values, gain_row):
     inverse = lax.rsqrt(jnp.mean(values * values, axis=-1, keepdims=True) + eps_norm)
     normed = values * inverse
@@ -1615,97 +1972,155 @@
     bf16 = jnp.bfloat16
     f32 = jnp.float32
 
-    pieces = [w_router.reshape(-1), attn_gain, ffn_gain, qk_gains]
-    flat = jnp.concatenate(pieces)
-    small_rows = -(-flat.shape[0] // 2048) * 16
-    small = jnp.pad(flat, (0, small_rows * 128 - flat.shape[0])).reshape(small_rows, 128)
-    out_form = "row" if shard_width % 128 else "col"
-    small_all, query_weight, key_weight, value_weight, out_weight, grad_all = plane_gather(
-        [
-            Gather(small, nf, chunks=1),
-            Gather(w_query, nf, half=True, chunks=2),
-            Gather(key_projection, nf, half=True, chunks=1),
-            Gather(value_projection, nf, half=True, chunks=1),
-            Gather(w_out, nf, form=out_form, half=True, chunks=2),
-            Gather(grad_out, nf, rep=True, chunks=4),
-        ],
-        1,
-        nf,
-    )
-    if out_form == "row":
-        out_weight = out_weight.reshape(nf, -1, shard_width).transpose(1, 0, 2)
-        out_weight = out_weight.reshape(-1, width_dim)
-    small_all = small_all.reshape(nf, 2, small_rows * 128)[:, 0]
-    ends = [0]
-    for piece in pieces:
-        ends.append(ends[-1] + piece.shape[0])
-    router_weight = small_all[:, ends[0] : ends[1]].reshape(width_dim, experts)
-    gain_one = small_all[:, ends[1] : ends[2]].reshape(-1).astype(f32)
-    gain_two = small_all[:, ends[2] : ends[3]].reshape(-1).astype(f32)
-    gain_qk = small_all[:, ends[3] : ends[4]].reshape(-1).astype(f32)
-    gain_query, gain_key = gain_qk[:HEAD_SIZE], gain_qk[HEAD_SIZE:]
-
-    kv_local = key_weight.shape[1] // HEAD_SIZE
-    head_local = query_weight.shape[1] // HEAD_SIZE
-    resid = hidden_in.astype(f32)
-    scaled_one, normed_one, inverse_one = norm_forward(resid, gain_one)
-    hidden_first = scaled_one.astype(bf16)
-    query_raw = jnp.dot(hidden_first, query_weight, preferred_element_type=f32).reshape(
-        tokens_dev, head_local, HEAD_SIZE
-    )
-    key_projected = jnp.dot(hidden_first, key_weight, preferred_element_type=f32).reshape(
-        tokens_dev, kv_local, HEAD_SIZE
-    )
-    value_rows = jnp.dot(hidden_first, value_weight, preferred_element_type=f32).astype(bf16)
-    query_normed, query_hat, query_inverse = norm_forward(query_raw, gain_query)
-    key_normed, key_unit_rows, key_inverse_norm = norm_forward(key_projected, gain_key)
-    own_positions = c_index * tokens_dev + jnp.arange(tokens_dev, dtype=jnp.int32)
-    cosine_table, sine_values = rope_tables(own_positions)
-    query_rotated = (
-        rotate(query_normed, cosine_table, sine_values)
-        .astype(bf16)
-        .reshape(tokens_dev, kv_local, query_group_width, HEAD_SIZE)
-    )
-    key_rotated = rotate(key_normed, cosine_table, sine_values).astype(bf16)
-    own_segments = segment_ids.astype(bf16)
-    packed_kv = jnp.concatenate(
-        [
-            key_rotated.reshape(tokens_dev, -1),
-            value_rows,
-            jnp.broadcast_to(own_segments[:, None], (tokens_dev, 128)),
-        ],
-        axis=1,
-    )
-    kv_all = lax.all_gather(packed_kv, "ctx", axis=0, tiled=True)
-    kv_width = kv_local * HEAD_SIZE
-    key_all = kv_all[:, :kv_width].reshape(-1, kv_local, HEAD_SIZE)
-    value_all = kv_all[:, kv_width : 2 * kv_width].reshape(-1, kv_local, HEAD_SIZE)
-    segment_all = kv_all[:, 2 * kv_width]
-    key_positions = jnp.arange(key_all.shape[0], dtype=jnp.int32)
-    allowed = (key_positions[None, :] <= own_positions[:, None]) & (
-        segment_all[None, :] == own_segments[:, None]
-    )
-    scores = masked_scores(query_rotated, key_all, allowed)
-    top_score = jnp.max(scores, axis=-1, keepdims=True)
-    log_total = top_score + jnp.log(jnp.sum(jnp.exp(scores - top_score), axis=-1, keepdims=True))
-    weights_att = jnp.exp(scores - log_total).astype(bf16)
-    attended = jnp.einsum("kgqs,skd->qkgd", weights_att, value_all, preferred_element_type=f32)
-    attended = attended.astype(bf16).reshape(tokens_dev, head_local * HEAD_SIZE)
-    out_partial = jnp.dot(attended, out_weight, preferred_element_type=f32)
-    resid_mid = resid + sum_over_tp(out_partial)
-    scaled_two, normed_two, inverse_two = norm_forward(resid_mid, gain_two)
-    hidden_two = scaled_two.astype(bf16)
-    logits = jnp.dot(hidden_two, router_weight, preferred_element_type=f32)
-    expert_ids = jnp.arange(experts, dtype=jnp.int32)
-    hits = routes[:, :, None] == expert_ids[None, None, :]
-    routed = jnp.any(hits, axis=1)
-    masked_logits = jnp.where(routed, logits, -jnp.inf)
-    raised = jnp.where(
-        routed, jnp.exp(masked_logits - jnp.max(masked_logits, axis=1, keepdims=True)), 0.0
-    )
-    probs = raised / jnp.sum(raised, axis=1, keepdims=True)
-    marks = jnp.where(routed, probs, -1.0).T
-
+    if nf == 8:
+        halves = shard_width // 128
+        turned = w_router.T.reshape(experts, halves, 128).transpose(1, 0, 2).reshape(-1, 128)
+        qk_row = lax.dynamic_update_slice(
+            jnp.zeros((256,), bf16), qk_gains, (f_index * qk_gains.shape[0],)
+        )
+        small = jnp.concatenate(
+            [
+                turned,
+                attn_gain.reshape(-1, 128),
+                ffn_gain.reshape(-1, 128),
+                qk_row.reshape(-1, 128),
+            ]
+        )
+        small = jnp.pad(small, ((0, -small.shape[0] % 16), (0, 0)))
+        own_positions = c_index * tokens_dev + jnp.arange(tokens_dev, dtype=jnp.int32)
+        cosine_table, sine_values = rope_tables(own_positions)
+        cosine_row, sine_row = cosine_table[:, 0], sine_values[:, 0]
+        trig = jnp.stack(
+            [
+                jnp.concatenate([cosine_row, cosine_row], axis=1),
+                jnp.concatenate([sine_row, -sine_row], axis=1),
+            ]
+        )
+        segment_wide = jnp.broadcast_to(segment_ids.astype(bf16)[:, None], (tokens_dev, 128))
+        expert_ids = jnp.arange(experts, dtype=jnp.int32)
+        hits = routes[:, :, None] == expert_ids[None, None, :]
+        routed = jnp.any(hits, axis=1).astype(f32)
+        heads_width, kv_width = w_query.shape[1], key_projection.shape[1]
+        shapes = (tokens_dev, width_dim, heads_width, kv_width, experts)
+        (
+            _,
+            query_weight,
+            key_weight,
+            value_weight,
+            out_weight,
+            grad_all,
+            hidden_two,
+            hidden_slices,
+            marks,
+            probs,
+            resid_mid,
+            attended,
+            query_raw,
+            key_projected,
+            query_rotated,
+            key_all,
+            value_all,
+            bias,
+            log_total,
+            gains,
+            router_rows,
+        ) = forward_pass(
+            nf,
+            (small, w_query, key_projection, value_projection, w_out, grad_out),
+            (hidden_in, segment_wide, routed, trig),
+            shapes,
+        )
+    else:
+        pieces = [w_router.reshape(-1), attn_gain, ffn_gain, qk_gains]
+        flat = jnp.concatenate(pieces)
+        small_rows = -(-flat.shape[0] // 2048) * 16
+        small = jnp.pad(flat, (0, small_rows * 128 - flat.shape[0])).reshape(small_rows, 128)
+        out_form = "row" if shard_width % 128 else "col"
+        small_all, query_weight, key_weight, value_weight, out_weight, grad_all = plane_gather(
+            [
+                Gather(small, nf, chunks=1),
+                Gather(w_query, nf, half=True, chunks=2),
+                Gather(key_projection, nf, half=True, chunks=1),
+                Gather(value_projection, nf, half=True, chunks=1),
+                Gather(w_out, nf, form=out_form, half=True, chunks=2),
+                Gather(grad_out, nf, rep=True, chunks=4),
+            ],
+            1,
+            nf,
+        )
+        if out_form == "row":
+            out_weight = out_weight.reshape(nf, -1, shard_width).transpose(1, 0, 2)
+            out_weight = out_weight.reshape(-1, width_dim)
+        small_all = small_all.reshape(nf, 2, small_rows * 128)[:, 0]
+        ends = [0]
+        for piece in pieces:
+            ends.append(ends[-1] + piece.shape[0])
+        router_weight = small_all[:, ends[0] : ends[1]].reshape(width_dim, experts)
+        gain_one = small_all[:, ends[1] : ends[2]].reshape(-1).astype(f32)
+        gain_two = small_all[:, ends[2] : ends[3]].reshape(-1).astype(f32)
+        gain_qk = small_all[:, ends[3] : ends[4]].reshape(-1).astype(f32)
+        gain_query, gain_key = gain_qk[:HEAD_SIZE], gain_qk[HEAD_SIZE:]
+
+        kv_local = key_weight.shape[1] // HEAD_SIZE
+        head_local = query_weight.shape[1] // HEAD_SIZE
+        resid = hidden_in.astype(f32)
+        scaled_one, normed_one, inverse_one = norm_forward(resid, gain_one)
+        hidden_first = scaled_one.astype(bf16)
+        query_raw = jnp.dot(hidden_first, query_weight, preferred_element_type=f32).reshape(
+            tokens_dev, head_local, HEAD_SIZE
+        )
+        key_projected = jnp.dot(hidden_first, key_weight, preferred_element_type=f32).reshape(
+            tokens_dev, kv_local, HEAD_SIZE
+        )
+        value_rows = jnp.dot(hidden_first, value_weight, preferred_element_type=f32).astype(bf16)
+        query_normed, query_hat, query_inverse = norm_forward(query_raw, gain_query)
+        key_normed, key_unit_rows, key_inverse_norm = norm_forward(key_projected, gain_key)
+        own_positions = c_index * tokens_dev + jnp.arange(tokens_dev, dtype=jnp.int32)
+        cosine_table, sine_values = rope_tables(own_positions)
+        query_rotated = (
+            rotate(query_normed, cosine_table, sine_values)
+            .astype(bf16)
+            .reshape(tokens_dev, kv_local, query_group_width, HEAD_SIZE)
+        )
+        key_rotated = rotate(key_normed, cosine_table, sine_values).astype(bf16)
+        own_segments = segment_ids.astype(bf16)
+        packed_kv = jnp.concatenate(
+            [
+                key_rotated.reshape(tokens_dev, -1),
+                value_rows,
+                jnp.broadcast_to(own_segments[:, None], (tokens_dev, 128)),
+            ],
+            axis=1,
+        )
+        kv_all = lax.all_gather(packed_kv, "ctx", axis=0, tiled=True)
+        kv_width = kv_local * HEAD_SIZE
+        key_all = kv_all[:, :kv_width].reshape(-1, kv_local, HEAD_SIZE)
+        value_all = kv_all[:, kv_width : 2 * kv_width].reshape(-1, kv_local, HEAD_SIZE)
+        segment_all = kv_all[:, 2 * kv_width]
+        key_positions = jnp.arange(key_all.shape[0], dtype=jnp.int32)
+        allowed = (key_positions[None, :] <= own_positions[:, None]) & (
+            segment_all[None, :] == own_segments[:, None]
+        )
+        scores = masked_scores(query_rotated, key_all, allowed)
+        top_score = jnp.max(scores, axis=-1, keepdims=True)
+        log_total = top_score + jnp.log(jnp.sum(jnp.exp(scores - top_score), axis=-1, keepdims=True))
+        weights_att = jnp.exp(scores - log_total).astype(bf16)
+        attended = jnp.einsum("kgqs,skd->qkgd", weights_att, value_all, preferred_element_type=f32)
+        attended = attended.astype(bf16).reshape(tokens_dev, head_local * HEAD_SIZE)
+        out_partial = jnp.dot(attended, out_weight, preferred_element_type=f32)
+        resid_mid = resid + sum_over_tp(out_partial)
+        scaled_two, normed_two, inverse_two = norm_forward(resid_mid, gain_two)
+        hidden_two = scaled_two.astype(bf16)
+        logits = jnp.dot(hidden_two, router_weight, preferred_element_type=f32)
+        expert_ids = jnp.arange(experts, dtype=jnp.int32)
+        hits = routes[:, :, None] == expert_ids[None, None, :]
+        routed = jnp.any(hits, axis=1)
+        masked_logits = jnp.where(routed, logits, -jnp.inf)
+        raised = jnp.where(
+            routed, jnp.exp(masked_logits - jnp.max(masked_logits, axis=1, keepdims=True)), 0.0
+        )
+        probs = raised / jnp.sum(raised, axis=1, keepdims=True)
+        marks = jnp.where(routed, probs, -1.0).T
     if nf == 8:
         (
             hidden_all,
@@ -1721,7 +2136,7 @@
         ) = expert_pass(
             hidden_two,
             marks,
-            by_shard(hidden_first, nf),
+            hidden_slices,
             grad_all,
             w_gate,
             w_up,
@@ -1807,19 +2222,11 @@
     grad_up = jnp.einsum("jrd,jrf->jdf", rows_in, grad_up_pre, preferred_element_type=f32)
 
     if nf == 8:
-        gains = jnp.stack([gain_one, gain_two, jnp.pad(gain_qk, (0, width_dim - gain_qk.shape[0]))])
-        cosine_row, sine_row = cosine_table[:, 0], sine_values[:, 0]
-        trig = jnp.stack(
-            [
-                jnp.concatenate([cosine_row, cosine_row], axis=1),
-                jnp.concatenate([sine_row, -sine_row], axis=1),
-            ]
-        )
         operands = (
             grad_hidden_moe,
             grad_prob,
             probs,
-            router_weight,
+            router_rows,
             hidden_in,
             resid_mid,
             gains,
@@ -1828,17 +2235,17 @@
             query_weight,
             key_weight,
             value_weight,
-            query_raw.reshape(tokens_dev, -1),
-            key_projected.reshape(tokens_dev, -1),
-            query_rotated.reshape(tokens_dev, -1),
-            key_all.reshape(-1, kv_width),
-            value_all.reshape(-1, kv_width),
-            jnp.where(allowed, 0.0, -jnp.inf),
-            log_total.reshape(head_local, tokens_dev, 1),
+            query_raw,
+            key_projected,
+            query_rotated,
+            key_all,
+            value_all,
+            bias,
+            log_total,
             trig,
             moe_partial,
         )
-        shapes = (tokens_dev, width_dim, head_local * HEAD_SIZE, kv_width, key_all.shape[0])
+        shapes = (tokens_dev, width_dim, heads_width, kv_width, key_all.shape[0])
         (
             attended_all,
             dq_all,

time: 580 us -> 539 us (0.929)
  the two profiles are of different devices: /device:TPU:10 before, /device:TPU:0 now
where the time goes in v4:
time: 539 us; the launch traced here: 534 us
  Pallas kernels  482 us (89%)
  matrix products  39.1 us (7%)
  local copies, waits for them, and re-layouts  7.66 us (1%)
    pallas_call x1, Pallas kernels, backward_pass(): pl.pallas_call(functools.partial(backward_kernel, nf, tuple(specs)), out_...  188 us
    pallas_call x1, Pallas kernels, forward_pass(): pl.pallas_call(functools.partial(forward_kernel, nf, tuple(specs)), out_s...  167 us
    pallas_call x1, Pallas kernels, expert_pass(): pl.pallas_call(functools.partial(expert_kernel, nf, capacity, tuple(specs...  127 us

profile of v4, /device:TPU:0, one launch (start us, length us, event | category | flops | bytes accessed | tf_op | source)
XLA Modules:
  0.0 533.7 jit_solution(9296681205060070800)
XLA Ops:
  0.7 0.3 multiply_cosine_fusion
  1.0 0.1 maximum_bitcast_fusion
  1.1 0.7 pad_maximum_fusion.refs_9_.refs_20_
  1.8 0.8 dynamic_update_slice.3
  2.6 0.7 copy_bitcast_fusion
  3.3 1.3 fusion.11.refs_0_
  4.6 0.7 fusion.3
  5.3 0.7 copy.47.refs_8_
  6.1 0.7 convert_element_type.15
  6.7 0.7 broadcast_in_dim.5.refs_7_
  7.4 166.5 %shard_map.246 = (bf16[1280,128]{1,0:T(8,128)(2,1)}, bf16[2048,2048]{1,0:T(8,128)(2,1)}, bf16[2048,256]{1,0:T(8,128)(2,1)}, bf16[2048,256]{1,0:T(8,128)(2,1)}, b...) custom-call(bf16[80,128]{1,0:T(8,128)(2,1)} %fusion.11.refs_0_, ...), custom_call_target="tpu_custom_call" | custom-call | tf_op jit(solution)/shard_map/pallas_call | solution.py:1848
  174.0 127.5 %shard_map.247 = (bf16[2048,2048]{1,0:T(8,128)(2,1)}, f32[512,128]{1,0:T(8,128)}, bf16[2048,256]{1,0:T(8,128)(2,1)}, bf16[2048,2048]{1,0:T(8,128)(2,1)}, bf16[2,...) custom-call(bf16[128,2048]{1,0:T(8,128)(2,1)} %get-tuple-element.53., ...), custom_call_target="tpu_custom_call" | custom-call | tf_op jit(solution)/shard_map/pallas_call | solution.py:965
  301.5 10.2 %fusion.20 = f32[2,384,2048]{2,1,0:T(8,128)} fusion(bf16[2,1024,384]{2,1,0:T(8,128)(2,1)} %get-tuple-element.89, bf16[2,1024,2048]{2,1,0:T(8,128)(2,1)} %get-tuple-element.90), kind=kOutput, calls=%fused_computation.30 | convolution fusion | flops 3221225472 | bytes 16252928 | tf_op jit(solution)/shard_map/jrf,jrd->jfd/dot_general | solution.py:2220
  311.7 6.5 %fusion.19 = f32[2,2048,384]{2,1,0:T(8,128)} fusion(bf16[2,1024,2048]{2,1,0:T(8,128)(2,1)S(1)} %copy-done.6, bf16[2,1024,384]{2,1,0:T(8,128)(2,1)S(1)} %copy-done.8), kind=kOutput, calls=%fused_computation.29 | convolution fusion | flops 3221225472 | bytes 16252928 | tf_op jit(solution)/shard_map/jrd,jrf->jdf/dot_general | solution.py:2222
  318.1 6.4 %fusion.18 = f32[2,2048,384]{2,1,0:T(8,128)} fusion(bf16[2,1024,2048]{2,1,0:T(8,128)(2,1)S(1)} %copy-done.6, bf16[2,1024,384]{2,1,0:T(8,128)(2,1)S(1)} %copy-done.7), kind=kOutput, calls=%fused_computation.28 | convolution fusion | flops 3221225472 | bytes 16252928 | tf_op jit(solution)/shard_map/jrd,jrf->jdf/dot_general | solution.py:2221
  324.6 0.8 slice.6
  325.4 0.7 copy.48
  326.2 188.1 %shard_map.248 = (bf16[2048,2048]{1,0:T(8,128)(2,1)}, bf16[2048,2048]{1,0:T(8,128)(2,1)}, bf16[2048,256]{1,0:T(8,128)(2,1)}, bf16[2048,256]{1,0:T(8,128)(2,1)}, ...) custom-call(bf16[128,2048]{1,0:T(8,128)(2,1)} %get-tuple-element.52., ...), custom_call_target="tpu_custom_call" | custom-call | tf_op jit(solution)/shard_map/pallas_call | solution.py:1510
  514.2 0.0 slice-start
  514.3 2.5 fusion
  516.7 7.6 %fusion.17 = f32[2048,256]{1,0:T(8,128)} fusion(bf16[2048,2048]{1,0:T(8,128)(2,1)} %get-tuple-element.82, bf16[2048,256]{1,0:T(8,128)(2,1)} %get-tuple-element.83), kind=kOutput, calls=%fused_computation.27 | convolution fusion | flops 2147483648 | bytes 11534336 | tf_op jit(solution)/shard_map/td,tq->dq/dot_general | solution.py:2358
  524.3 0.0 copy-done.3
  524.3 1.2 fusion.16
  525.5 0.0 copy-done.2
  525.5 1.2 fusion.15
  526.7 3.7 fusion.14
  530.3 0.1 reshape.67
  530.4 0.1 reduce_sum.9
  530.5 0.6 fusion.13
  531.1 0.6 dynamic_slice.13
  531.7 0.8 copy.60
  532.5 1.0 copy.61
  (24 shorter events, 0.1 us)
Async XLA Ops:
  301.5 10.2 %copy-start.6 = (bf16[2,1024,2048]{2,1,0:T(8,128)(2,1)S(1)}, bf16[2,1024,2048]{2,1,0:T(8,128)(2,1)}, u32[]{:S(2)}) copy-start(bf16[2,1024,2048]{2,1,0:T(8,128)(2,1)} %get-tuple-element.86) | copy-start | bytes 25165828
  301.5 10.2 %copy-start.8 = (bf16[2,1024,384]{2,1,0:T(8,128)(2,1)S(1)}, bf16[2,1024,384]{2,1,0:T(8,128)(2,1)}, u32[]{:S(2)}) copy-start(bf16[2,1024,384]{2,1,0:T(8,128)(2,1)} %get-tuple-element.88) | copy-start | bytes 4718596
  311.7 6.5 %copy-start.7 = (bf16[2,1024,384]{2,1,0:T(8,128)(2,1)S(1)}, bf16[2,1024,384]{2,1,0:T(8,128)(2,1)}, u32[]{:S(2)}) copy-start(bf16[2,1024,384]{2,1,0:T(8,128)(2,1)} %get-tuple-element.87) | copy-start | bytes 4718596
  514.2 12.4 %slice-start = ((s8[8388608]{0:T(1024)(128)(4,1)}), s8[4194304]{0:T(1024)(128)(4,1)S(1)}, s32[]{:S(2)}) async-start(s8[8388608]{0:T(1024)(128)(4,1)} %bitcast.32), calls=%async_computation | async-start | bytes 8388608
  516.7 7.6 %copy-start = (bf16[2048,256]{1,0:T(8,128)(2,1)S(1)}, bf16[2048,256]{1,0:T(8,128)(2,1)}, u32[]{:S(2)}) copy-start(bf16[2048,256]{1,0:T(8,128)(2,1)} %get-tuple-element.78) | copy-start | bytes 3145732
  516.7 7.6 %copy-start.3 = (bf16[2048,256]{1,0:T(8,128)(2,1)S(1)}, bf16[2048,256]{1,0:T(8,128)(2,1)}, u32[]{:S(2)}) copy-start(bf16[2048,256]{1,0:T(8,128)(2,1)} %get-tuple-element.81) | copy-start | bytes 3145732
  516.7 8.7 %copy-start.2 = (bf16[2048,256]{1,0:T(8,128)(2,1)S(1)}, bf16[2048,256]{1,0:T(8,128)(2,1)}, u32[]{:S(2)}) copy-start(bf16[2048,256]{1,0:T(8,128)(2,1)} %get-tuple-element.80) | copy-start | bytes 3145732
  516.7 9.9 %slice-start.1 = ((s8[8388608]{0:T(1024)(128)(4,1)}), s8[4194304]{0:T(1024)(128)(4,1)S(1)}, s32[]{:S(2)}) async-start(s8[8388608]{0:T(1024)(128)(4,1)} %bitcast.32), calls=%async_computation.1 | async-start | bytes 8388608
  526.6 3.7 copy-start.5
  526.6 5.0 copy-start.4
  526.7 5.8 %copy-start.1 = (f32[128,2048]{1,0:T(8,128)S(1)}, f32[128,2048]{1,0:T(8,128)}, u32[]{:S(2)}) copy-start(f32[128,2048]{1,0:T(8,128)} %get-tuple-element.112) | copy-start | bytes 3145732

commit v5 on v4

--- a/solution.py
+++ b/solution.py
@@ -1085,7 +1085,7 @@
         sum_total,
         sum_bufs,
         sum_sems,
-    ) = refs[:28] + (refs[28:32], refs[32:])
+    ) = refs[:28] + (refs[28:33], refs[33:])
     f32, bf16 = jnp.float32, jnp.bfloat16
     f, c, t = lax.axis_index("fsdp"), lax.axis_index("ctx"), lax.axis_index("tp")
     partner, side = (f, 1 - c, t), (f, c, 1 - t)
@@ -1113,7 +1113,7 @@
     early, late = (0,), (1, 2, 3, 4, 5)
     nz = nf // 2
     order = visit_code(nz, f // 2)
-    own_loads, to_partner, to_across, along, finish_sum, drain_sum = token_sum(
+    own_loads, to_partner, to_side, to_across, along, finish_sum, drain_sum = token_sum(
         nf, out_part, sum_own, sum_total, sum_bufs, sum_sems
     )
     for cp in own_loads:
@@ -1159,6 +1159,9 @@
         return carry
 
     lax.fori_loop(0, tokens // part_rows, norm_two, 0)
+    for cp in own_loads:
+        cp.wait()
+    lax.fori_loop(0, nz, lambda i, carry: to_side(visit(order, nz, i), carry), 0)
     shard = width // nf
     for k in range(nf):
         d_out_slices[k * tokens : (k + 1) * tokens, :] = d_out[:, k * shard : (k + 1) * shard]
@@ -1172,11 +1175,8 @@
             d_out[...], w_big[cols, :], NT, preferred_element_type=f32
         ).astype(bf16)
     load(wq_hbm, w_big, 0).start()
-    for cp in own_loads:
-        cp.wait()
-    for i in range(2):
-        to_across(visit(order, nz, i), 0)
     step_of(1, early)
+    to_across(visit(order, nz, 0))
     dk_acc[...] = jnp.zeros_like(dk_acc)
     dv_acc[...] = jnp.zeros_like(dv_acc)
     qk_acc[...] = jnp.zeros_like(qk_acc)
@@ -1213,8 +1213,7 @@
 
     heads = heads_width // HEAD_SIZE
     lax.fori_loop(0, heads // 2, head, 0)
-    for i in range(2, nz):
-        to_across(visit(order, nz, i), 0)
+    to_across(visit(order, nz, 1))
     step_of(2, early)
     lax.fori_loop(heads // 2, heads, head, 0)
 
@@ -1243,6 +1242,8 @@
         d_key[:, cols] = dk.astype(bf16)
     d_value[...] = (dv_acc[mine] + kv_recv[:, kv_width:].astype(f32)).astype(bf16)
     start((2, 3))
+    to_across(visit(order, nz, 2))
+    along(visit(order, nz, 0))
 
     def to_side(src, dst, i):
         return pltpu.make_async_remote_copy(
@@ -1275,8 +1276,9 @@
         dh1[:, rows] = total.astype(bf16)
         if (k + 1) * tile % quarter == 0:
             dh1_copy((k + 1) * tile // quarter - 1).start()
+    to_across(visit(order, nz, 3))
     step_of(3, early)
-    along(visit(order, nz, 0))
+    along(visit(order, nz, 1))
     for i in range(4):
         dh1_copy(i).wait_recv()
     swap_qk.wait_recv()
@@ -1303,18 +1305,17 @@
     tail[2 * lanes : 2 * lanes + 2, :] = qk_acc[0:2, :] + qk_side[0:2, :]
     start((5,))
     step_of(1, late)
+    along(visit(order, nz, 2))
     edge_of(early)
-    along(visit(order, nz, 1))
     step_of(2, late)
-    along(visit(order, nz, 2))
+    along(f // 2)
     step_of(3, late)
     edge_of(late)
-    along(f // 2)
     run_direct()
     land()
 
-    def put_out(rows, value):
-        block_out[rows] = (x_mid[rows] + value).astype(bf16)
+    def put_out(rows, cols, value):
+        block_out[rows, cols] = (x_mid[rows, cols] + value).astype(bf16)
 
     finish_sum(put_out)
     drain()
@@ -1342,17 +1343,31 @@
 
 
 def token_sum(nf, partial, own, total_ref, bufs, sems):
-    from_partner, from_across, from_z, from_side = bufs
-    load_sem, p_send, p_recv, x_send, x_recv, z_send, z_recv, s_send, s_recv = sems
+    from_partner, from_side, from_across, from_z, last_half = bufs
+    (
+        load_sem,
+        p_send,
+        p_recv,
+        y_send,
+        y_recv,
+        x_send,
+        x_recv,
+        z_send,
+        z_recv,
+        s_send,
+        s_recv,
+    ) = sems
     nz = nf // 2
     f, c, t = lax.axis_index("fsdp"), lax.axis_index("ctx"), lax.axis_index("tp")
     z, x = f // 2, lax.rem(f, 2)
     has_up, has_down = z + 1 < nz, z > 0
     up, down = (f + 2, c, t), (f - 2, c, t)
     across_dev, partner, side = (z * 2 + 1 - x, c, t), (f, 1 - c, t), (f, c, 1 - t)
-    tokens = total_ref.shape[0]
+    tokens, half = total_ref.shape
     rows = tokens // SUM_CUT
     bf16 = jnp.bfloat16
+    kept = pl.ds(pl.multiple_of(t * half, half), half)
+    given = pl.ds(pl.multiple_of((1 - t) * half, half), half)
 
     def chunk(q):
         return pl.ds(q * rows, rows)
@@ -1374,8 +1389,7 @@
         for b in range(nf)
     ]
 
-    def p_copy(u, xx, q):
-        b = u * 2 + xx
+    def p_copy(b, q):
         return remote(
             partial.at[pl.ds((2 * b + 1 - c) * tokens + q * rows, rows)],
             from_partner.at[b, chunk(q)],
@@ -1384,9 +1398,18 @@
             partner,
         )
 
+    def y_copy(b, q):
+        return remote(
+            own.at[b, chunk(q), given],
+            from_side.at[b, chunk(q)],
+            y_send.at[b, q],
+            y_recv.at[b, q],
+            side,
+        )
+
     def x_copy(u, q):
         return remote(
-            own.at[u * 2 + 1 - x, chunk(q)],
+            own.at[u * 2 + 1 - x, chunk(q), kept],
             from_across.at[u, chunk(q)],
             x_send.at[u, q],
             x_recv.at[u, q],
@@ -1395,7 +1418,7 @@
 
     def z_copy(u, q, way, dev):
         return remote(
-            own.at[u * 2 + x, chunk(q)],
+            own.at[u * 2 + x, chunk(q), kept],
             from_z.at[way, u, chunk(q)],
             z_send.at[u, q],
             z_recv.at[way, u, q],
@@ -1404,7 +1427,7 @@
 
     def s_copy(q):
         return remote(
-            own.at[f, chunk(q)], from_side.at[chunk(q)], s_send.at[q], s_recv.at[q], side
+            own.at[f, chunk(q), kept], last_half.at[chunk(q)], s_send.at[q], s_recv.at[q], side
         )
 
     def wide(value):
@@ -1413,27 +1436,37 @@
     def to_partner(u, carry):
         for xx in range(2):
             for q in range(SUM_CUT):
-                p_copy(u, xx, q).start()
+                p_copy(u * 2 + xx, q).start()
         return carry
 
-    def to_across(u, carry):
+    def to_side(u, carry):
+        for xx in range(2):
+            b = u * 2 + xx
+            for q in range(SUM_CUT):
+                p_copy(b, q).wait_recv()
+                own[b, chunk(q)] = (
+                    wide(own[b, chunk(q)]) + wide(from_partner[b, chunk(q)])
+                ).astype(bf16)
+                y_copy(b, q).start()
+        return carry
+
+    def to_across(u):
         b = u * 2 + 1 - x
         for q in range(SUM_CUT):
-            for xx in range(2):
-                p_copy(u, xx, q).wait_recv()
-            own[b, chunk(q)] = (wide(own[b, chunk(q)]) + wide(from_partner[b, chunk(q)])).astype(
-                bf16
-            )
+            y_copy(b, q).wait_recv()
+            own[b, chunk(q), kept] = (
+                wide(own[b, chunk(q), kept]) + wide(from_side[b, chunk(q)])
+            ).astype(bf16)
             x_copy(u, q).start()
-        return carry
 
     def along(u):
         b = u * 2 + x
         for q in range(SUM_CUT):
+            y_copy(b, q).wait_recv()
             x_copy(u, q).wait_recv()
             total_ref[chunk(q)] = (
-                wide(own[b, chunk(q)])
-                + wide(from_partner[b, chunk(q)])
+                wide(own[b, chunk(q), kept])
+                + wide(from_side[b, chunk(q)])
                 + wide(from_across[u, chunk(q)])
             )
 
@@ -1447,7 +1480,7 @@
                 z_copy(u, q, 1, partner).wait_recv()
                 total_ref[chunk(q)] += wide(from_z[1, u, chunk(q)])
 
-            own[b, chunk(q)] = total_ref[chunk(q)].astype(bf16)
+            own[b, chunk(q), kept] = total_ref[chunk(q)].astype(bf16)
 
             @pl.when(u > z)
             def _():
@@ -1463,14 +1496,16 @@
 
     def finish_sum(put):
         for q in range(SUM_CUT):
+            put(chunk(q), kept, wide(own[f, chunk(q), kept]))
             s_copy(q).wait_recv()
-            put(chunk(q), wide(own[f, chunk(q)]) + wide(from_side[chunk(q)]))
+            put(chunk(q), given, wide(last_half[chunk(q)]))
 
     def drain_sum():
         def ends(u, carry):
             for q in range(SUM_CUT):
                 for xx in range(2):
-                    p_copy(u, xx, q).wait_send()
+                    p_copy(u * 2 + xx, q).wait_send()
+                    y_copy(u * 2 + xx, q).wait_send()
                 x_copy(u, q).wait_send()
 
                 @pl.when(u != z)
@@ -1483,7 +1518,7 @@
         for q in range(SUM_CUT):
             s_copy(q).wait_send()
 
-    return own_loads, to_partner, to_across, along, finish_sum, drain_sum
+    return own_loads, to_partner, to_side, to_across, along, finish_sum, drain_sum
 
 
 def backward_pass(nf, arrays, attended, shapes):
@@ -1543,12 +1578,15 @@
             dma((5,)),
             dma((5,)),
             pltpu.VMEM((nf, tokens, width), bf16),
-            pltpu.VMEM((tokens, width), f32),
+            pltpu.VMEM((tokens, width // 2), f32),
             pltpu.VMEM((nf, tokens, width), bf16),
-            pltpu.VMEM((nz, tokens, width), bf16),
-            pltpu.VMEM((2, nz, tokens, width), bf16),
-            pltpu.VMEM((tokens, width), bf16),
+            pltpu.VMEM((nf, tokens, width // 2), bf16),
+            pltpu.VMEM((nz, tokens, width // 2), bf16),
+            pltpu.VMEM((2, nz, tokens, width // 2), bf16),
+            pltpu.VMEM((tokens, width // 2), bf16),
             dma((nf,)),
+            dma((nf, SUM_CUT)),
+            dma((nf, SUM_CUT)),
             dma((nf, SUM_CUT)),
             dma((nf, SUM_CUT)),
             dma((nz, SUM_CUT)),

time: 539 us -> 507 us (0.941)
  Pallas kernels: 482 us -> 450 us
    pallas_call x1, Pallas kernels: 188 us -> 156 us  [backward_pass(): pl.pallas_call(functools.partial(backward_kernel, nf, tuple(specs)), out_...]
where the time goes in v5:
time: 507 us; the launch traced here: 502 us
  Pallas kernels  450 us (89%)
  matrix products  39.1 us (8%)
  local copies, waits for them, and re-layouts  7.66 us (2%)
    pallas_call x1, Pallas kernels, forward_pass(): pl.pallas_call(functools.partial(forward_kernel, nf, tuple(specs)), out_s...  167 us
    pallas_call x1, Pallas kernels, backward_pass(): pl.pallas_call(functools.partial(backward_kernel, nf, tuple(specs)), out_...  156 us
    pallas_call x1, Pallas kernels, expert_pass(): pl.pallas_call(functools.partial(expert_kernel, nf, capacity, tuple(specs...  127 us
    dot_general x1, matrix products, on_device(): jnp.einsum('jrf,jrd->jfd', activated, grad_prod, preferred_element_type=f32)  10.2 us

profile of v5, /device:TPU:0, one launch (start us, length us, event | category | flops | bytes accessed | tf_op | source)
XLA Modules:
  0.0 502.0 jit_solution(14175499148578296658)
XLA Ops:
  0.7 0.3 multiply_cosine_fusion
  1.0 0.1 maximum_bitcast_fusion
  1.1 0.7 pad_maximum_fusion.refs_9_.refs_20_
  1.8 0.8 dynamic_update_slice.3
  2.6 0.7 copy_bitcast_fusion
  3.3 1.3 fusion.11.refs_0_
  4.6 0.7 fusion.3
  5.3 0.7 copy.47.refs_8_
  6.1 0.7 convert_element_type.15
  6.7 0.7 broadcast_in_dim.5.refs_7_
  7.4 166.5 %shard_map.246 = (bf16[1280,128]{1,0:T(8,128)(2,1)}, bf16[2048,2048]{1,0:T(8,128)(2,1)}, bf16[2048,256]{1,0:T(8,128)(2,1)}, bf16[2048,256]{1,0:T(8,128)(2,1)}, b...) custom-call(bf16[80,128]{1,0:T(8,128)(2,1)} %fusion.11.refs_0_, ...), custom_call_target="tpu_custom_call" | custom-call | tf_op jit(solution)/shard_map/pallas_call | solution.py:1886
  174.0 127.5 %shard_map.247 = (bf16[2048,2048]{1,0:T(8,128)(2,1)}, f32[512,128]{1,0:T(8,128)}, bf16[2048,256]{1,0:T(8,128)(2,1)}, bf16[2048,2048]{1,0:T(8,128)(2,1)}, bf16[2,...) custom-call(bf16[128,2048]{1,0:T(8,128)(2,1)} %get-tuple-element.53., ...), custom_call_target="tpu_custom_call" | custom-call | tf_op jit(solution)/shard_map/pallas_call | solution.py:965
  301.5 10.2 %fusion.20 = f32[2,384,2048]{2,1,0:T(8,128)} fusion(bf16[2,1024,384]{2,1,0:T(8,128)(2,1)} %get-tuple-element.89, bf16[2,1024,2048]{2,1,0:T(8,128)(2,1)} %get-tuple-element.90), kind=kOutput, calls=%fused_computation.30 | convolution fusion | flops 3221225472 | bytes 16252928 | tf_op jit(solution)/shard_map/jrf,jrd->jfd/dot_general | solution.py:2258
  311.7 6.5 %fusion.19 = f32[2,2048,384]{2,1,0:T(8,128)} fusion(bf16[2,1024,2048]{2,1,0:T(8,128)(2,1)S(1)} %copy-done.6, bf16[2,1024,384]{2,1,0:T(8,128)(2,1)S(1)} %copy-done.8), kind=kOutput, calls=%fused_computation.29 | convolution fusion | flops 3221225472 | bytes 16252928 | tf_op jit(solution)/shard_map/jrd,jrf->jdf/dot_general | solution.py:2260
  318.1 0.0 copy-done.7
  318.1 6.4 %fusion.18 = f32[2,2048,384]{2,1,0:T(8,128)} fusion(bf16[2,1024,2048]{2,1,0:T(8,128)(2,1)S(1)} %copy-done.6, bf16[2,1024,384]{2,1,0:T(8,128)(2,1)S(1)} %copy-done.7), kind=kOutput, calls=%fused_computation.28 | convolution fusion | flops 3221225472 | bytes 16252928 | tf_op jit(solution)/shard_map/jrd,jrf->jdf/dot_general | solution.py:2259
  324.6 0.8 slice.6
  325.4 0.7 copy.48
  326.2 156.4 %shard_map.248 = (bf16[2048,2048]{1,0:T(8,128)(2,1)}, bf16[2048,2048]{1,0:T(8,128)(2,1)}, bf16[2048,256]{1,0:T(8,128)(2,1)}, bf16[2048,256]{1,0:T(8,128)(2,1)}, ...) custom-call(bf16[128,2048]{1,0:T(8,128)(2,1)} %get-tuple-element.52., ...), custom_call_target="tpu_custom_call" | custom-call | tf_op jit(solution)/shard_map/pallas_call | solution.py:1545
  482.5 0.0 slice-start
  482.5 2.5 fusion
  485.0 7.6 %fusion.17 = f32[2048,256]{1,0:T(8,128)} fusion(bf16[2048,2048]{1,0:T(8,128)(2,1)} %get-tuple-element.82, bf16[2048,256]{1,0:T(8,128)(2,1)} %get-tuple-element.83), kind=kOutput, calls=%fused_computation.27 | convolution fusion | flops 2147483648 | bytes 11534336 | tf_op jit(solution)/shard_map/td,tq->dq/dot_general | solution.py:2396
  492.6 1.2 fusion.16
  493.8 1.2 fusion.15
  495.0 3.7 fusion.14
  498.6 0.0 copy-done.5
  498.6 0.1 reshape.67
  498.7 0.1 reduce_sum.9
  498.7 0.6 fusion.13
  499.4 0.6 dynamic_slice.13
  500.0 0.8 copy.60
  500.8 1.0 copy.61
  (24 shorter events, 0.1 us)
Async XLA Ops:
  301.5 10.2 %copy-start.6 = (bf16[2,1024,2048]{2,1,0:T(8,128)(2,1)S(1)}, bf16[2,1024,2048]{2,1,0:T(8,128)(2,1)}, u32[]{:S(2)}) copy-start(bf16[2,1024,2048]{2,1,0:T(8,128)(2,1)} %get-tuple-element.86) | copy-start | bytes 25165828
  301.5 10.2 %copy-start.8 = (bf16[2,1024,384]{2,1,0:T(8,128)(2,1)S(1)}, bf16[2,1024,384]{2,1,0:T(8,128)(2,1)}, u32[]{:S(2)}) copy-start(bf16[2,1024,384]{2,1,0:T(8,128)(2,1)} %get-tuple-element.88) | copy-start | bytes 4718596
  311.7 6.5 %copy-start.7 = (bf16[2,1024,384]{2,1,0:T(8,128)(2,1)S(1)}, bf16[2,1024,384]{2,1,0:T(8,128)(2,1)}, u32[]{:S(2)}) copy-start(bf16[2,1024,384]{2,1,0:T(8,128)(2,1)} %get-tuple-element.87) | copy-start | bytes 4718596
  482.5 12.4 %slice-start = ((s8[8388608]{0:T(1024)(128)(4,1)}), s8[4194304]{0:T(1024)(128)(4,1)S(1)}, s32[]{:S(2)}) async-start(s8[8388608]{0:T(1024)(128)(4,1)} %bitcast.32), calls=%async_computation | async-start | bytes 8388608
  485.0 7.6 %copy-start = (bf16[2048,256]{1,0:T(8,128)(2,1)S(1)}, bf16[2048,256]{1,0:T(8,128)(2,1)}, u32[]{:S(2)}) copy-start(bf16[2048,256]{1,0:T(8,128)(2,1)} %get-tuple-element.78) | copy-start | bytes 3145732
  485.0 7.6 %copy-start.3 = (bf16[2048,256]{1,0:T(8,128)(2,1)S(1)}, bf16[2048,256]{1,0:T(8,128)(2,1)}, u32[]{:S(2)}) copy-start(bf16[2048,256]{1,0:T(8,128)(2,1)} %get-tuple-element.81) | copy-start | bytes 3145732
  485.0 8.8 %copy-start.2 = (bf16[2048,256]{1,0:T(8,128)(2,1)S(1)}, bf16[2048,256]{1,0:T(8,128)(2,1)}, u32[]{:S(2)}) copy-start(bf16[2048,256]{1,0:T(8,128)(2,1)} %get-tuple-element.80) | copy-start | bytes 3145732
  485.0 9.9 %slice-start.1 = ((s8[8388608]{0:T(1024)(128)(4,1)}), s8[4194304]{0:T(1024)(128)(4,1)S(1)}, s32[]{:S(2)}) async-start(s8[8388608]{0:T(1024)(128)(4,1)} %bitcast.32), calls=%async_computation.1 | async-start | bytes 8388608
  494.9 3.7 copy-start.5
  494.9 5.0 %copy-start.4 = (bf16[128,2048]{1,0:T(8,128)(2,1)S(1)}, bf16[128,2048]{1,0:T(8,128)(2,1)}, u32[]{:S(2)}) copy-start(bf16[128,2048]{1,0:T(8,128)(2,1)} %get-tuple-element.111) | copy-start | bytes 1572868
  494.9 5.8 %copy-start.1 = (f32[128,2048]{1,0:T(8,128)S(1)}, f32[128,2048]{1,0:T(8,128)}, u32[]{:S(2)}) copy-start(f32[128,2048]{1,0:T(8,128)} %get-tuple-element.112) | copy-start | bytes 3145732

commit v6 on v5

--- a/solution.py
+++ b/solution.py
@@ -20,11 +20,12 @@
 
 
 class Gather:
-    def __init__(self, array, nf, form="row", half=False, rep=False, chunks=2):
+    def __init__(self, array, nf, form="row", half=False, rep=False, chunks=2, split=None):
         if nf > 8:
             chunks = 2 if rep else 1
         self.array, self.form, self.half, self.rep, self.chunks = array, form, half, rep, chunks
         self.shape = array.shape
+        self.split = nf // 2 - 1 if split is None else split
         self.rows = array.shape[0] // 2 if half else array.shape[0]
         self.step = (self.rows // nf if form == "a2a" else self.rows) // chunks
 
@@ -107,11 +108,11 @@
             pl.when(cond)(fn)
 
     def go_up(a, q, dist):
-        far = dist + 1 < nz - 1 if specs[a].rep and not in_half(a, q) else None
+        far = dist + 1 < specs[a].split if specs[a].rep and not in_half(a, q) else None
         return both(has_up, far)
 
     def go_down(a, q, dist):
-        far = dist + 1 < nz - 1 if specs[a].rep and not in_half(a, q) else None
+        far = dist + 1 < specs[a].split if specs[a].rep and not in_half(a, q) else None
         return both(has_down, far)
 
     def go_across(a, q):
@@ -187,8 +188,8 @@
 
     def column(k, a, q):
         rep = specs[a].rep
-        came = k < nz - 1 if rep and not in_half(a, q) else None
-        far = (k == nz - 1) if rep and in_half(a, q) else False
+        came = k < specs[a].split if rep and not in_half(a, q) else None
+        far = (k >= specs[a].split) if rep and in_half(a, q) else False
 
         def take(zz, kind, onward):
             bf = zz * 2 + x
@@ -230,10 +231,11 @@
             arrived(a, q, bf, c)
             pass_on(a, q, bf, PARTNER)
 
-        when((z - k >= 0), lambda: take((z - k) * 2 + 1 - x))
-        when((z + k < nz) & (k > 0), lambda: take((z + k) * 2 + 1 - x))
-        when((z - k >= 0) & (k == nz - 1), lambda: take((z - k) * 2 + x))
-        when((z + k < nz) & (k == nz - 1), lambda: take((z + k) * 2 + x))
+        when(z - k >= 0, lambda: take((z - k) * 2 + 1 - x))
+        when(both(z + k < nz, k > 0), lambda: take((z + k) * 2 + 1 - x))
+        far = k >= specs[a].split
+        when(both(z - k >= 0, far), lambda: take((z - k) * 2 + x))
+        when(both(z + k < nz, far), lambda: take((z + k) * 2 + x))
 
     count = len(relays)
     lag = 2
@@ -297,7 +299,7 @@
         for a, q in some:
             across(k - 1, a, q)
 
-        if k > 1:
+        if any(specs[a].rep for a, _ in some) and k > 1:
             for a, q in some:
                 aside(k - 2, a, q)
 
@@ -355,7 +357,7 @@
                 when(cond, lambda: copy(a, q, bf, c, view, kind).wait_send())
 
             half = in_half(a, q) if rep else None
-            by_z = dist < nz - 1 if rep and not half else None
+            by_z = dist < specs[a].split if rep and not half else None
             sent(PARTNER, None)
             sent(UP, both(here, zz <= z, by_z, go_up(a, q, dist)))
             sent(DOWN, both(here, zz >= z, by_z, go_down(a, q, dist)))
@@ -366,7 +368,7 @@
                 sent(UP, there & even)
                 sent(DOWN, there & jnp.logical_not(even))
             if rep and half:
-                sent(SIDE, jnp.logical_not(here) | (dist == nz - 1))
+                sent(SIDE, jnp.logical_not(here) | (dist >= specs[a].split))
         for a, q in direct:
             arrived(a, q, bf, 1 - c)
             view = dst(a, q, bf, c)
@@ -620,7 +622,7 @@
         return copies
 
     def chunk(q):
-        return pl.ds(q * step_rows, step_rows)
+        return pl.ds(pl.multiple_of(q * step_rows, step_rows), step_rows)
 
     def p_copy(u, xx, q):
         return pltpu.make_async_remote_copy(
@@ -799,7 +801,8 @@
         return ref.astype(f32)
 
     def to_across(u):
-        for q in range(CUT):
+        @pl.loop(0, CUT)
+        def _(q):
             for xx in range(2):
                 p_copy(u, xx, q).wait_recv()
             blk = u * 4 + (1 - x) * 2 + c
@@ -810,7 +813,9 @@
 
     def along(u):
         blk = u * 4 + x * 2 + c
-        for q in range(CUT):
+
+        @pl.loop(0, CUT)
+        def _(q):
             x_copy(u, q).wait_recv()
 
             def total():
@@ -1039,8 +1044,7 @@
         grad_out,
         wo_hbm,
         wq_hbm,
-        wk_hbm,
-        wv_hbm,
+        wkv_hbm,
         q_raw,
         k_raw,
         q_rot,
@@ -1050,23 +1054,26 @@
         lse,
         trig,
         out_part,
-    ), refs = refs[:22], refs[22:]
+        xs_hbm,
+        de_hbm,
+        act_hbm,
+        dg_hbm,
+        du_hbm,
+    ), refs = refs[:26], refs[26:]
     gathered, grad_in, block_out, refs = refs[:n], refs[n], refs[n + 1], refs[n + 2 :]
+    (gate_out, up_out, down_out), refs = refs[:3], refs[3:]
     stage, refs = refs[:n], refs[n:]
     (recv, send, local), refs = refs[:3], refs[3:]
     (
         w_big,
-        w_key,
-        w_value,
+        w_kv,
         dx1,
         dh2,
         d_out,
         d_out_slices,
         d_attn,
         d_query,
-        d_key,
-        d_value,
-        logit,
+        d_rest,
         tail,
         dk_acc,
         dv_acc,
@@ -1085,7 +1092,8 @@
         sum_total,
         sum_bufs,
         sum_sems,
-    ) = refs[:28] + (refs[28:33], refs[33:])
+    ) = refs[:25] + (refs[25:30], refs[30:41])
+    act, dg, du, x_tile, d_tile, gate_tile, up_tile, down_tile, e_sem, t_sem, o_sem = refs[41:]
     f32, bf16 = jnp.float32, jnp.bfloat16
     f, c, t = lax.axis_index("fsdp"), lax.axis_index("ctx"), lax.axis_index("tp")
     partner, side = (f, 1 - c, t), (f, c, 1 - t)
@@ -1106,11 +1114,12 @@
         pl.semaphore_signal(barrier, 1, device_id=dev, device_id_type=MESH)
     pl.semaphore_wait(barrier, nf + 1)
 
-    ins = (attended, d_query, d_key, d_value, logit, tail, d_out_slices)
+    ins = (attended, d_query, d_rest, tail, d_out_slices)
     start, run, land, start_direct, run_direct, drain, step_of, edge_of, _ = gather_engine(
         nf, specs, ins, gathered, stage, recv, send, local
     )
-    early, late = (0,), (1, 2, 3, 4, 5)
+    early, late = (0,), (1, 2, 3)
+    kv_width = dk_acc.shape[1]
     nz = nf // 2
     order = visit_code(nz, f // 2)
     own_loads, to_partner, to_side, to_across, along, finish_sum, drain_sum = token_sum(
@@ -1124,15 +1133,72 @@
     def load(src, dst, i):
         return pltpu.make_async_copy(src, dst, w_sem.at[i])
 
+    kept_loads = [
+        pltpu.make_async_copy(src, dst, e_sem.at[i])
+        for i, (src, dst) in enumerate(((act_hbm, act), (dg_hbm, dg), (du_hbm, du)))
+    ]
+    span = x_tile.shape[2]
+    tiles = width // span
+    pieces = act.shape[0] * tiles
+
+    def tile_at(p):
+        return p // tiles, pl.ds(pl.multiple_of(lax.rem(p, tiles) * span, span), span)
+
+    def tile_loads(p):
+        j, cols = tile_at(p)
+        slot = lax.rem(p, 2)
+        return (
+            pltpu.make_async_copy(xs_hbm.at[j, :, cols], x_tile.at[slot], t_sem.at[0, slot]),
+            pltpu.make_async_copy(de_hbm.at[j, :, cols], d_tile.at[slot], t_sem.at[1, slot]),
+        )
+
+    def tile_stores(p):
+        j, cols = tile_at(p)
+        slot = lax.rem(p, 2)
+        return (
+            pltpu.make_async_copy(gate_tile.at[slot], gate_out.at[j, cols], o_sem.at[0, slot]),
+            pltpu.make_async_copy(up_tile.at[slot], up_out.at[j, cols], o_sem.at[1, slot]),
+            pltpu.make_async_copy(down_tile.at[slot], down_out.at[j, :, cols], o_sem.at[2, slot]),
+        )
+
+    def piece(p, carry):
+        j, _ = tile_at(p)
+        slot = lax.rem(p, 2)
+        for cp in tile_loads(p):
+            cp.wait()
+
+        @pl.when(p + 1 < pieces)
+        def _():
+            for cp in tile_loads(p + 1):
+                cp.start()
+
+        @pl.when(p >= 2)
+        def _():
+            for cp in tile_stores(p - 2):
+                cp.wait()
+
+        rows = x_tile[slot]
+        gate_tile[slot] = lax.dot_general(rows, dg[j], TN, preferred_element_type=f32).astype(bf16)
+        up_tile[slot] = lax.dot_general(rows, du[j], TN, preferred_element_type=f32).astype(bf16)
+        down_tile[slot] = lax.dot_general(
+            act[j], d_tile[slot], TN, preferred_element_type=f32
+        ).astype(bf16)
+        for cp in tile_stores(p):
+            cp.start()
+        return carry
+
     load(wo_hbm, w_big, 0).start()
-    load(wk_hbm, w_key, 1).start()
-    load(wv_hbm, w_value, 2).start()
-
-    logit[...] = jnp.zeros_like(logit)
+    for cp in kept_loads:
+        cp.start()
+    for cp in tile_loads(0):
+        cp.start()
+    load(wkv_hbm, w_kv, 1).start()
+
+    d_rest[...] = jnp.zeros_like(d_rest)
     pr = probs[...]
     gp = grad_prob[...]
     dl = (pr * (gp - jnp.sum(pr * gp, axis=1, keepdims=True))).astype(bf16)
-    logit[:, :experts] = dl
+    d_rest[:, 2 * kv_width : 2 * kv_width + experts] = dl
     tile = 512
     for k in range(width // tile):
         cols = slice(k * tile, (k + 1) * tile)
@@ -1217,7 +1283,6 @@
     step_of(2, early)
     lax.fori_loop(heads // 2, heads, head, 0)
 
-    kv_width = dk_acc.shape[1]
     theirs = pl.ds(pl.multiple_of((1 - c) * tokens, tokens), tokens)
     mine = pl.ds(pl.multiple_of(c * tokens, tokens), tokens)
     kv_send[:, :kv_width] = dk_acc[theirs].astype(bf16)
@@ -1231,7 +1296,7 @@
         device_id_type=MESH,
     )
     swap_kv.start()
-    start((1, 4))
+    start((1,))
     start_direct()
     swap_kv.wait()
     for kv in range(kv_width // HEAD_SIZE):
@@ -1239,9 +1304,9 @@
         g = dk_acc[mine, cols] + kv_recv[:, cols].astype(f32)
         gain_grad, dk = norm_back(unrope(g), k_raw[:, cols], gain_key)
         qk_acc[1:2, :] += gain_grad
-        d_key[:, cols] = dk.astype(bf16)
-    d_value[...] = (dv_acc[mine] + kv_recv[:, kv_width:].astype(f32)).astype(bf16)
-    start((2, 3))
+        d_rest[:, cols] = dk.astype(bf16)
+    d_rest[:, kv_width : 2 * kv_width] = (dv_acc[mine] + kv_recv[:, kv_width:].astype(f32)).astype(bf16)
+    start((2,))
     to_across(visit(order, nz, 2))
     along(visit(order, nz, 0))
 
@@ -1258,8 +1323,7 @@
     swap_qk = to_side(qk_acc, qk_side, 4)
     swap_qk.start()
     load(wq_hbm, w_big, 0).wait()
-    load(wk_hbm, w_key, 1).wait()
-    load(wv_hbm, w_value, 2).wait()
+    load(wkv_hbm, w_kv, 1).wait()
     quarter = width // 4
 
     def dh1_copy(i):
@@ -1269,9 +1333,8 @@
     for k in range(width // tile):
         rows = slice(k * tile, (k + 1) * tile)
         total = lax.dot_general(d_query[...], w_big[rows, :], NT, preferred_element_type=f32)
-        total = total + lax.dot_general(d_key[...], w_key[rows, :], NT, preferred_element_type=f32)
         total = total + lax.dot_general(
-            d_value[...], w_value[rows, :], NT, preferred_element_type=f32
+            d_rest[:, : 2 * kv_width], w_kv[rows, :], NT, preferred_element_type=f32
         )
         dh1[:, rows] = total.astype(bf16)
         if (k + 1) * tile % quarter == 0:
@@ -1303,13 +1366,29 @@
             row = which * lanes + k
             tail[row : row + 1, :] = row_sum[which : which + 1, k * 128 : (k + 1) * 128]
     tail[2 * lanes : 2 * lanes + 2, :] = qk_acc[0:2, :] + qk_side[0:2, :]
-    start((5,))
-    step_of(1, late)
-    along(visit(order, nz, 2))
-    edge_of(early)
-    step_of(2, late)
-    along(f // 2)
-    step_of(3, late)
+    start((3,))
+    for cp in kept_loads:
+        cp.wait()
+
+    def stage_at(s, carry):
+        lax.fori_loop(s * (pieces // nz), (s + 1) * (pieces // nz), piece, 0)
+
+        @pl.when(s + 1 < nz)
+        def _():
+            step_of(s + 1, late)
+
+        @pl.when(s == 0)
+        def _():
+            along(visit(order, nz, 2))
+            edge_of(early)
+
+        @pl.when(s == 1)
+        def _():
+            along(f // 2)
+
+        return carry
+
+    lax.fori_loop(0, nz, stage_at, 0)
     edge_of(late)
     run_direct()
     land()
@@ -1318,6 +1397,9 @@
         block_out[rows, cols] = (x_mid[rows, cols] + value).astype(bf16)
 
     finish_sum(put_out)
+    for p in (pieces - 2, pieces - 1):
+        for cp in tile_stores(p):
+            cp.wait()
     drain()
     drain_sum()
     for i in range(4):
@@ -1370,7 +1452,7 @@
     given = pl.ds(pl.multiple_of((1 - t) * half, half), half)
 
     def chunk(q):
-        return pl.ds(q * rows, rows)
+        return pl.ds(pl.multiple_of(q * rows, rows), rows)
 
     def remote(src, dst, send, recv, dev):
         return pltpu.make_async_remote_copy(
@@ -1442,7 +1524,9 @@
     def to_side(u, carry):
         for xx in range(2):
             b = u * 2 + xx
-            for q in range(SUM_CUT):
+
+            @pl.loop(0, SUM_CUT)
+            def _(q, b=b):
                 p_copy(b, q).wait_recv()
                 own[b, chunk(q)] = (
                     wide(own[b, chunk(q)]) + wide(from_partner[b, chunk(q)])
@@ -1452,7 +1536,9 @@
 
     def to_across(u):
         b = u * 2 + 1 - x
-        for q in range(SUM_CUT):
+
+        @pl.loop(0, SUM_CUT)
+        def _(q):
             y_copy(b, q).wait_recv()
             own[b, chunk(q), kept] = (
                 wide(own[b, chunk(q), kept]) + wide(from_side[b, chunk(q)])
@@ -1461,7 +1547,9 @@
 
     def along(u):
         b = u * 2 + x
-        for q in range(SUM_CUT):
+
+        @pl.loop(0, SUM_CUT)
+        def _(q):
             y_copy(b, q).wait_recv()
             x_copy(u, q).wait_recv()
             total_ref[chunk(q)] = (
@@ -1529,40 +1617,39 @@
     specs = [
         Gather(attended, nf, chunks=2),
         Gather(shape((tokens, heads_width), bf16), nf, chunks=2),
-        Gather(shape((tokens, kv_width), bf16), nf, chunks=1),
-        Gather(shape((tokens, kv_width), bf16), nf, chunks=1),
-        Gather(shape((tokens, 128), bf16), nf, chunks=1),
+        Gather(shape((tokens, 2 * kv_width + 128), bf16), nf, chunks=1),
         Gather(shape((tail_rows, 128), f32), nf, chunks=1),
         Gather(shape((nf * tokens, width // nf), bf16), nf, form="a2a", chunks=1),
     ]
     n = len(specs)
+    experts, rows, hidden = arrays[-3].shape
+    gate_shape, down_shape = (experts, width, hidden), (experts, hidden, width)
+    span = 256
     total = sum(s.chunks for s in specs)
     any_spec = pl.BlockSpec(memory_space=pl.ANY)
     vmem = pl.BlockSpec(memory_space=pltpu.VMEM)
     dma = pltpu.SemaphoreType.DMA
-    in_any = {0, 9, 10, 11, 12, 21}
+    in_any = {0, 9, 10, 11, 20, 21, 22, 23, 24, 25}
     nz = nf // 2
     return pl.pallas_call(
         functools.partial(backward_kernel, nf, tuple(specs)),
         out_shape=tuple(shape(s.out_shape(nf), s.array.dtype) for s in specs)
-        + (shape((tokens, width), f32), shape((tokens, width), bf16)),
-        in_specs=[any_spec if i in in_any else vmem for i in range(22)],
-        out_specs=tuple([any_spec] * n + [vmem, vmem]),
+        + (shape((tokens, width), f32), shape((tokens, width), bf16))
+        + tuple(shape(s, bf16) for s in (gate_shape, gate_shape, down_shape)),
+        in_specs=[any_spec if i in in_any else vmem for i in range(26)],
+        out_specs=tuple([any_spec] * n + [vmem, vmem] + [any_spec] * 3),
         scratch_shapes=[stage_of(s, nf) for s in specs]
         + [dma((2 * nf, total)), dma((5, 2 * nf, total)), dma((2, n))]
         + [
             pltpu.VMEM((width, max(width, heads_width)), bf16),
-            pltpu.VMEM((width, kv_width), bf16),
-            pltpu.VMEM((width, kv_width), bf16),
+            pltpu.VMEM((width, 2 * kv_width), bf16),
             pltpu.VMEM((tokens, width), f32),
             pltpu.VMEM((tokens, width), f32),
             pltpu.VMEM((tokens, width), bf16),
             pltpu.VMEM((nf * tokens, width // nf), bf16),
             pltpu.VMEM((tokens, heads_width), bf16),
             pltpu.VMEM((tokens, heads_width), bf16),
-            pltpu.VMEM((tokens, kv_width), bf16),
-            pltpu.VMEM((tokens, kv_width), bf16),
-            pltpu.VMEM((tokens, 128), bf16),
+            pltpu.VMEM((tokens, 2 * kv_width + 128), bf16),
             pltpu.VMEM((tail_rows, 128), f32),
             pltpu.VMEM((keys, kv_width), f32),
             pltpu.VMEM((keys, kv_width), f32),
@@ -1573,7 +1660,7 @@
             pltpu.VMEM((tokens, width), bf16),
             pltpu.VMEM((8, 128), f32),
             pltpu.VMEM((2, width), f32),
-            dma((3,)),
+            dma((2,)),
             dma((2,)),
             dma((5,)),
             dma((5,)),
@@ -1595,6 +1682,17 @@
             dma((2, nz, SUM_CUT)),
             dma((SUM_CUT,)),
             dma((SUM_CUT,)),
+            pltpu.VMEM((experts, rows, hidden), bf16),
+            pltpu.VMEM((experts, rows, hidden), bf16),
+            pltpu.VMEM((experts, rows, hidden), bf16),
+            pltpu.VMEM((2, rows, span), bf16),
+            pltpu.VMEM((2, rows, span), bf16),
+            pltpu.VMEM((2, span, hidden), bf16),
+            pltpu.VMEM((2, span, hidden), bf16),
+            pltpu.VMEM((2, hidden, span), bf16),
+            dma((3,)),
+            dma((2, 2)),
+            dma((3, 2)),
         ],
         compiler_params=pltpu.CompilerParams(
             collective_id=8, has_side_effects=True, vmem_limit_bytes=67043328
@@ -1628,8 +1726,7 @@
     (recv, send, local), refs = refs[:3], refs[3:]
     (
         w_big,
-        w_key,
-        w_value,
+        w_kv,
         small,
         hidden_one,
         kv_all,
@@ -1672,10 +1769,14 @@
     start, _, _, _, _, drain, step_of, edge_of, land_of = gather_engine(
         nf, specs, ins, gathered, stage, recv, send, local
     )
-    first, second, third = (0, 1, 2, 3), (4,), (5,)
+    first, second, third = (0, 1, 2), (3,), (4,)
     start(first)
-    for k in range(1, nz):
+
+    def first_step(k, carry):
         step_of(k, first)
+        return carry
+
+    lax.fori_loop(1, nz, first_step, 0)
     start(second)
     edge_of(first)
     land_of(first)
@@ -1683,10 +1784,9 @@
     def load(src, dst, i):
         return pltpu.make_async_copy(src, dst, w_sem.at[i])
 
-    small_load = load(gathered[0], small, 3)
+    small_load = load(gathered[0], small, 2)
     small_load.start()
-    load(gathered[2], w_key, 1).start()
-    load(gathered[3], w_value, 2).start()
+    load(gathered[2], w_kv, 1).start()
     load(gathered[1], w_big, 0).start()
     small_load.wait()
 
@@ -1730,12 +1830,13 @@
         turned = normed * trig[0] - pltpu.roll(normed, HEAD_SIZE // 2, 1) * trig[1]
         return turned.astype(bf16)
 
-    load(gathered[2], w_key, 1).wait()
-    load(gathered[3], w_value, 2).wait()
+    load(gathered[2], w_kv, 1).wait()
     mine = pl.ds(pl.multiple_of(c * tokens, tokens), tokens)
-    k_raw[...] = jnp.dot(hidden_one[...], w_key[...], preferred_element_type=f32)
+    k_raw[...] = jnp.dot(
+        hidden_one[...], w_kv[:, :kv_width], preferred_element_type=f32
+    )
     kv_all[mine, kv_width : 2 * kv_width] = jnp.dot(
-        hidden_one[...], w_value[...], preferred_element_type=f32
+        hidden_one[...], w_kv[:, kv_width:], preferred_element_type=f32
     ).astype(bf16)
     for kv in range(kv_width // HEAD_SIZE):
         cols = slice(kv * HEAD_SIZE, (kv + 1) * HEAD_SIZE)
@@ -1794,9 +1895,9 @@
     lax.fori_loop(heads // 2, heads, head, 0)
     edge_of(second)
     land_of(second)
-    load(gathered[4], w_big, 0).start()
+    load(gathered[3], w_big, 0).start()
     step_of(1, third)
-    load(gathered[4], w_big, 0).wait()
+    load(gathered[3], w_big, 0).wait()
     quarter = width // 4
 
     def side_copy(i):
@@ -1849,15 +1950,14 @@
 
 def forward_pass(nf, arrays, operands, shapes):
     f32, bf16 = jnp.float32, jnp.bfloat16
-    small, w_query, key_projection, value_projection, w_out, grad_out = arrays
+    small, w_query, kv_projection, w_out, grad_out = arrays
     tokens, width, heads_width, kv_width, experts = shapes
     specs = [
         Gather(small, nf, chunks=1),
         Gather(w_query, nf, half=True, chunks=2),
-        Gather(key_projection, nf, half=True, chunks=1),
-        Gather(value_projection, nf, half=True, chunks=1),
+        Gather(kv_projection, nf, half=True, chunks=1),
         Gather(w_out, nf, form="col", half=True, chunks=2),
-        Gather(grad_out, nf, rep=True, chunks=4),
+        Gather(grad_out, nf, chunks=2),
     ]
     n = len(specs)
     total = sum(s.chunks for s in specs)
@@ -1892,15 +1992,14 @@
         + [dma((2 * nf, total)), dma((5, 2 * nf, total)), dma((2, n))]
         + [
             pltpu.VMEM((width, max(width, heads_width)), bf16),
-            pltpu.VMEM((width, kv_width), bf16),
-            pltpu.VMEM((width, kv_width), bf16),
+            pltpu.VMEM((width, 2 * kv_width), bf16),
             pltpu.VMEM(specs[0].out_shape(nf), bf16),
             pltpu.VMEM((tokens, width), bf16),
             pltpu.VMEM((span, 2 * kv_width + 128), bf16),
             pltpu.VMEM((tokens, width), bf16),
             pltpu.VMEM((tokens, width), bf16),
             pltpu.VMEM((tokens, 128), f32),
-            dma((4,)),
+            dma((3,)),
             dma((2,)),
             dma((4,)),
             dma((4,)),
@@ -2039,12 +2138,12 @@
         hits = routes[:, :, None] == expert_ids[None, None, :]
         routed = jnp.any(hits, axis=1).astype(f32)
         heads_width, kv_width = w_query.shape[1], key_projection.shape[1]
+        kv_projection = jnp.concatenate([key_projection, value_projection], axis=1)
         shapes = (tokens_dev, width_dim, heads_width, kv_width, experts)
         (
             _,
             query_weight,
-            key_weight,
-            value_weight,
+            kv_weight,
             out_weight,
             grad_all,
             hidden_two,
@@ -2064,7 +2163,7 @@
             router_rows,
         ) = forward_pass(
             nf,
-            (small, w_query, key_projection, value_projection, w_out, grad_out),
+            (small, w_query, kv_projection, w_out, grad_out),
             (hidden_in, segment_wide, routed, trig),
             shapes,
         )
@@ -2255,9 +2354,6 @@
         ).reshape(experts, tokens_dev)
         grad_prob = grad_prob + swap(grad_prob, "tp")
         grad_prob = grad_prob.T
-    grad_down = jnp.einsum("jrf,jrd->jfd", activated, grad_prod, preferred_element_type=f32)
-    grad_gate = jnp.einsum("jrd,jrf->jdf", rows_in, grad_gate_pre, preferred_element_type=f32)
-    grad_up = jnp.einsum("jrd,jrf->jdf", rows_in, grad_up_pre, preferred_element_type=f32)
 
     if nf == 8:
         operands = (
@@ -2271,8 +2367,7 @@
             grad_out,
             out_weight,
             query_weight,
-            key_weight,
-            value_weight,
+            kv_weight,
             query_raw,
             key_projected,
             query_rotated,
@@ -2282,21 +2377,37 @@
             log_total,
             trig,
             moe_partial,
+            rows_in,
+            grad_prod,
+            activated,
+            grad_gate_pre,
+            grad_up_pre,
         )
         shapes = (tokens_dev, width_dim, heads_width, kv_width, key_all.shape[0])
         (
             attended_all,
             dq_all,
-            dk_all,
-            dv_all,
-            logits_all,
+            rest_all,
             tail_all,
             proj_slice,
             grad_in,
             block_out,
+            grad_gate,
+            grad_up,
+            grad_down,
         ) = backward_pass(nf, operands, attended, shapes)
+        grad_gate, grad_up, grad_down = (
+            grad_gate.astype(f32),
+            grad_up.astype(f32),
+            grad_down.astype(f32),
+        )
         tail_rows = tail_all.shape[0] // devices
+        dk_all, dv_all = rest_all[:, :kv_width], rest_all[:, kv_width : 2 * kv_width]
+        logits_all = rest_all[:, 2 * kv_width :]
     else:
+        grad_down = jnp.einsum("jrf,jrd->jfd", activated, grad_prod, preferred_element_type=f32)
+        grad_gate = jnp.einsum("jrd,jrf->jdf", rows_in, grad_gate_pre, preferred_element_type=f32)
+        grad_up = jnp.einsum("jrd,jrf->jdf", rows_in, grad_up_pre, preferred_element_type=f32)
         block_out = (resid_mid + sum_over_tp(block_sum(moe_partial, nf))).astype(bf16)
 
         grad_rows = grad_out.astype(f32)

time: 507 us -> 492 us (0.970)
  matrix products: 39.1 us -> 15.9 us
  other arithmetic: 3.8 us -> 16.3 us
    dot_general x3 -> x0, matrix products: 23.1 us -> none  [the longest x1 10.2 us: on_device(): jnp.einsum('jrf,jrd->jfd', activated, grad_prod, preferred_element_type=f32)]
    convert_element_type x0 -> x3, other arithmetic: none -> 10.8 us  [the longest x1 4.04 us: on_device(): grad_down.astype(f32)]
    pallas_call x1, Pallas kernels: 167 us -> 159 us  [forward_pass(): pl.pallas_call(functools.partial(forward_kernel, nf, tuple(specs)), out_s...]
where the time goes in v6:
time: 492 us; the launch traced here: 488 us
  Pallas kernels  446 us (91%)
  other arithmetic  16.3 us (3%)
  matrix products  15.9 us (3%)
  local copies, waits for them, and re-layouts  8.74 us (2%)
    pallas_call x1, Pallas kernels, backward_pass(): pl.pallas_call(functools.partial(backward_kernel, nf, tuple(specs)), out_...  160 us
    pallas_call x1, Pallas kernels, forward_pass(): pl.pallas_call(functools.partial(forward_kernel, nf, tuple(specs)), out_s...  159 us
    pallas_call x1, Pallas kernels, expert_pass(): pl.pallas_call(functools.partial(expert_kernel, nf, capacity, tuple(specs...  127 us

profile of v6, /device:TPU:0, one launch (start us, length us, event | category | flops | bytes accessed | tf_op | source)
XLA Modules:
  0.0 487.6 jit_solution(5179257352590343065)
XLA Ops:
  0.7 0.3 multiply_cosine_fusion
  1.0 0.1 maximum_bitcast_fusion
  1.1 0.7 pad_maximum_fusion.1.refs_8_.refs_19_
  1.8 0.8 dynamic_update_slice.3
  2.6 0.7 copy_bitcast_fusion
  3.3 1.3 fusion.15.refs_0_
  4.6 1.7 pad_maximum_fusion.refs_2_
  6.3 0.7 fusion.7
  7.0 0.7 copy.38.refs_7_
  7.8 0.7 convert_element_type.24
  8.4 0.7 broadcast_in_dim.5.refs_6_
  9.1 158.9 %shard_map.246 = (bf16[1280,128]{1,0:T(8,128)(2,1)}, bf16[2048,2048]{1,0:T(8,128)(2,1)}, bf16[2048,512]{1,0:T(8,128)(2,1)}, bf16[2048,2048]{1,0:T(8,128)(2,1)}, ...) custom-call(bf16[80,128]{1,0:T(8,128)(2,1)} %fusion.15.refs_0_, ...), custom_call_target="tpu_custom_call" | custom-call | tf_op jit(solution)/shard_map/pallas_call | solution.py:1986
  168.0 127.0 %shard_map.247 = (bf16[2048,2048]{1,0:T(8,128)(2,1)}, f32[512,128]{1,0:T(8,128)}, bf16[2048,256]{1,0:T(8,128)(2,1)}, bf16[2048,2048]{1,0:T(8,128)(2,1)}, bf16[2,...) custom-call(bf16[128,2048]{1,0:T(8,128)(2,1)} %get-tuple-element.53., ...), custom_call_target="tpu_custom_call" | custom-call | tf_op jit(solution)/shard_map/pallas_call | solution.py:970
  295.0 0.8 slice.15
  295.8 0.7 copy.39
  296.6 159.6 %shard_map.248 = (bf16[2048,2048]{1,0:T(8,128)(2,1)}, bf16[2048,2048]{1,0:T(8,128)(2,1)}, bf16[2048,640]{1,0:T(8,128)(2,1)}, f32[640,128]{1,0:T(8,128)}, bf16[20...) custom-call(bf16[128,2048]{1,0:T(8,128)(2,1)} %get-tuple-element.52., ...), custom_call_target="tpu_custom_call" | custom-call | tf_op jit(solution)/shard_map/pallas_call | solution.py:1634
  456.2 2.3 fusion
  458.5 7.6 %fusion.19 = f32[2048,256]{1,0:T(8,128)} fusion(bf16[2048,2048]{1,0:T(8,128)(2,1)} %get-tuple-element.85, bf16[2048,256]{1,0:T(8,128)(2,1)} %get-tuple-element.86), kind=kOutput, calls=%fused_computation.30 | convolution fusion | flops 2147483648 | bytes 11534336 | tf_op jit(solution)/shard_map/td,tq->dq/dot_general | solution.py:2507
  466.1 3.1 convert_element_type.27
  469.2 0.1 copy-done.2
  469.3 3.6 convert_element_type.28
  472.9 4.0 convert_element_type.29
  477.0 1.0 copy-done.4
  478.0 1.2 fusion.2
  479.2 1.2 fusion.4
  480.4 3.7 fusion.18
  484.0 0.1 reshape.67
  484.1 0.1 reduce_sum.9
  484.2 0.6 fusion.17
  484.8 0.6 dynamic_slice.13
  485.4 0.8 copy.45
  486.2 1.0 copy.46
  (23 shorter events, 0.1 us)
Async XLA Ops:
  458.5 7.6 %copy-start.3 = (bf16[2,2048,384]{2,1,0:T(8,128)(2,1)S(1)}, bf16[2,2048,384]{2,1,0:T(8,128)(2,1)}, u32[]{:S(2)}) copy-start(bf16[2,2048,384]{2,1,0:T(8,128)(2,1)} %get-tuple-element.88) | copy-start | bytes 9437188
  466.1 3.2 copy-start.2
  469.3 3.6 copy-start.1
  469.3 11.0 %slice-start = ((s8[8388608]{0:T(1024)(128)(4,1)}), s8[4194304]{0:T(1024)(128)(4,1)S(1)}, s32[]{:S(2)}) async-start(s8[8388608]{0:T(1024)(128)(4,1)} %bitcast.24), calls=%async_computation | async-start | bytes 8388608
  472.9 4.1 copy-start
  472.9 5.1 %copy-start.4 = (bf16[2048,640]{1,0:T(8,128)(2,1)S(1)}, bf16[2048,640]{1,0:T(8,128)(2,1)}, u32[]{:S(2)}) copy-start(bf16[2048,640]{1,0:T(8,128)(2,1)} %get-tuple-element.84) | copy-start | bytes 7864324
  472.9 7.4 %slice-start.1 = ((s8[8388608]{0:T(1024)(128)(4,1)}), s8[4194304]{0:T(1024)(128)(4,1)S(1)}, s32[]{:S(2)}) async-start(s8[8388608]{0:T(1024)(128)(4,1)} %bitcast.24), calls=%async_computation.1 | async-start | bytes 8388608
  480.3 3.7 copy-start.7
  480.3 5.0 %copy-start.6 = (bf16[128,2048]{1,0:T(8,128)(2,1)S(1)}, bf16[128,2048]{1,0:T(8,128)(2,1)}, u32[]{:S(2)}) copy-start(bf16[128,2048]{1,0:T(8,128)(2,1)} %get-tuple-element.111) | copy-start | bytes 1572868
  480.4 5.8 %copy-start.5 = (f32[128,2048]{1,0:T(8,128)S(1)}, f32[128,2048]{1,0:T(8,128)}, u32[]{:S(2)}) copy-start(f32[128,2048]{1,0:T(8,128)} %get-tuple-element.112) | copy-start | bytes 3145732

commit v7 on v6

--- a/solution.py
+++ b/solution.py
@@ -774,8 +774,11 @@
         for b in range(4):
             spread(b)
         for xx in range(2):
-            for q in range(CUT):
+
+            @pl.loop(0, CUT)
+            def _(q, xx=xx):
                 p_copy(u, xx, q).start()
+
         for b in range(4):
             back = jnp.transpose(pick[b]).astype(bf16)
             for k in range(width // tile):
@@ -893,7 +896,8 @@
     )
     swap_prob.start()
     run_direct()
-    for q in range(CUT):
+    @pl.loop(0, CUT)
+    def _(q):
         s_copy(q).wait_recv()
         grad_tok[chunk(q)] = wide(part[me, chunk(q)]) + wide(from_side[chunk(q)])
     swap_prob.wait_recv()
@@ -904,7 +908,8 @@
     swap_prob.wait_send()
 
     def ends(u, carry):
-        for q in range(CUT):
+        @pl.loop(0, CUT)
+        def _(q):
             for xx in range(2):
                 p_copy(u, xx, q).wait_send()
             x_copy(u, q).wait_send()
@@ -1583,14 +1588,16 @@
                 s_copy(q).start()
 
     def finish_sum(put):
-        for q in range(SUM_CUT):
+        @pl.loop(0, SUM_CUT)
+        def _(q):
             put(chunk(q), kept, wide(own[f, chunk(q), kept]))
             s_copy(q).wait_recv()
             put(chunk(q), given, wide(last_half[chunk(q)]))
 
     def drain_sum():
         def ends(u, carry):
-            for q in range(SUM_CUT):
+            @pl.loop(0, SUM_CUT)
+            def _(q):
                 for xx in range(2):
                     p_copy(u * 2 + xx, q).wait_send()
                     y_copy(u * 2 + xx, q).wait_send()
@@ -1870,6 +1877,7 @@
         allowed = (key_at <= query_at) & (theirs[:, cols] == own)
         bias[:, cols] = jnp.where(allowed, 0.0, -jnp.inf)
     step_of(2, second)
+    start(third)
     group = QUERY_HEADS // KEY_VALUE_HEADS
 
     def head(h, carry):
@@ -1891,7 +1899,6 @@
     heads = heads_width // HEAD_SIZE
     lax.fori_loop(0, heads // 2, head, 0)
     step_of(3, second)
-    start(third)
     lax.fori_loop(heads // 2, heads, head, 0)
     edge_of(second)
     land_of(second)

time: 492 us -> 492 us (level)
  no operation moved by 1% of the time
where the time goes in v7:
time: 492 us; the launch traced here: 487 us
  Pallas kernels  445 us (90%)
  other arithmetic  16.3 us (3%)
  matrix products  15.9 us (3%)
  local copies, waits for them, and re-layouts  8.74 us (2%)
    pallas_call x1, Pallas kernels, backward_pass(): pl.pallas_call(functools.partial(backward_kernel, nf, tuple(specs)), out_...  160 us
    pallas_call x1, Pallas kernels, forward_pass(): pl.pallas_call(functools.partial(forward_kernel, nf, tuple(specs)), out_s...  158 us
    pallas_call x1, Pallas kernels, expert_pass(): pl.pallas_call(functools.partial(expert_kernel, nf, capacity, tuple(specs...  127 us

profile of v7, /device:TPU:0, one launch (start us, length us, event | category | flops | bytes accessed | tf_op | source)
XLA Modules:
  0.0 486.8 jit_solution(17945001099906376441)
XLA Ops:
  0.7 0.3 multiply_cosine_fusion
  1.0 0.1 maximum_bitcast_fusion
  1.1 0.7 pad_maximum_fusion.1.refs_8_.refs_19_
  1.8 0.8 dynamic_update_slice.3
  2.6 0.7 copy_bitcast_fusion
  3.3 1.3 fusion.15.refs_0_
  4.6 1.7 pad_maximum_fusion.refs_2_
  6.3 0.7 fusion.7
  7.0 0.7 copy.38.refs_7_
  7.8 0.7 convert_element_type.24
  8.4 0.7 broadcast_in_dim.5.refs_6_
  9.1 157.9 %shard_map.246 = (bf16[1280,128]{1,0:T(8,128)(2,1)}, bf16[2048,2048]{1,0:T(8,128)(2,1)}, bf16[2048,512]{1,0:T(8,128)(2,1)}, bf16[2048,2048]{1,0:T(8,128)(2,1)}, ...) custom-call(bf16[80,128]{1,0:T(8,128)(2,1)} %fusion.15.refs_0_, ...), custom_call_target="tpu_custom_call" | custom-call | tf_op jit(solution)/shard_map/pallas_call | solution.py:1993
  167.0 126.8 %shard_map.247 = (bf16[2048,2048]{1,0:T(8,128)(2,1)}, f32[512,128]{1,0:T(8,128)}, bf16[2048,256]{1,0:T(8,128)(2,1)}, bf16[2048,2048]{1,0:T(8,128)(2,1)}, bf16[2,...) custom-call(bf16[128,2048]{1,0:T(8,128)(2,1)} %get-tuple-element.53., ...), custom_call_target="tpu_custom_call" | custom-call | tf_op jit(solution)/shard_map/pallas_call | solution.py:975
  293.8 0.8 slice.15
  294.6 0.7 copy.39
  295.3 160.1 %shard_map.248 = (bf16[2048,2048]{1,0:T(8,128)(2,1)}, bf16[2048,2048]{1,0:T(8,128)(2,1)}, bf16[2048,640]{1,0:T(8,128)(2,1)}, f32[640,128]{1,0:T(8,128)}, bf16[20...) custom-call(bf16[128,2048]{1,0:T(8,128)(2,1)} %get-tuple-element.52., ...), custom_call_target="tpu_custom_call" | custom-call | tf_op jit(solution)/shard_map/pallas_call | solution.py:1641
  455.4 2.3 fusion
  457.7 7.6 %fusion.19 = f32[2048,256]{1,0:T(8,128)} fusion(bf16[2048,2048]{1,0:T(8,128)(2,1)} %get-tuple-element.85, bf16[2048,256]{1,0:T(8,128)(2,1)} %get-tuple-element.86), kind=kOutput, calls=%fused_computation.30 | convolution fusion | flops 2147483648 | bytes 11534336 | tf_op jit(solution)/shard_map/td,tq->dq/dot_general | solution.py:2514
  465.3 3.1 convert_element_type.27
  468.4 0.1 copy-done.2
  468.5 3.6 convert_element_type.28
  472.1 4.0 convert_element_type.29
  476.1 1.0 copy-done.4
  477.2 1.2 fusion.2
  478.4 1.2 fusion.4
  479.6 3.7 fusion.18
  483.2 0.1 reshape.67
  483.3 0.1 reduce_sum.9
  483.3 0.6 fusion.17
  484.0 0.6 dynamic_slice.13
  484.6 0.8 copy.45
  485.4 1.0 copy.46
  (23 shorter events, 0.1 us)
Async XLA Ops:
  457.7 7.6 %copy-start.3 = (bf16[2,2048,384]{2,1,0:T(8,128)(2,1)S(1)}, bf16[2,2048,384]{2,1,0:T(8,128)(2,1)}, u32[]{:S(2)}) copy-start(bf16[2,2048,384]{2,1,0:T(8,128)(2,1)} %get-tuple-element.88) | copy-start | bytes 9437188
  465.3 3.2 copy-start.2
  468.5 3.6 copy-start.1
  468.5 11.0 %slice-start = ((s8[8388608]{0:T(1024)(128)(4,1)}), s8[4194304]{0:T(1024)(128)(4,1)S(1)}, s32[]{:S(2)}) async-start(s8[8388608]{0:T(1024)(128)(4,1)} %bitcast.24), calls=%async_computation | async-start | bytes 8388608
  472.1 4.1 copy-start
  472.1 5.1 %copy-start.4 = (bf16[2048,640]{1,0:T(8,128)(2,1)S(1)}, bf16[2048,640]{1,0:T(8,128)(2,1)}, u32[]{:S(2)}) copy-start(bf16[2048,640]{1,0:T(8,128)(2,1)} %get-tuple-element.84) | copy-start | bytes 7864324
  472.1 7.4 %slice-start.1 = ((s8[8388608]{0:T(1024)(128)(4,1)}), s8[4194304]{0:T(1024)(128)(4,1)S(1)}, s32[]{:S(2)}) async-start(s8[8388608]{0:T(1024)(128)(4,1)} %bitcast.24), calls=%async_computation.1 | async-start | bytes 8388608
  479.5 3.7 copy-start.7
  479.5 5.0 %copy-start.6 = (bf16[128,2048]{1,0:T(8,128)(2,1)S(1)}, bf16[128,2048]{1,0:T(8,128)(2,1)}, u32[]{:S(2)}) copy-start(bf16[128,2048]{1,0:T(8,128)(2,1)} %get-tuple-element.111) | copy-start | bytes 1572868
  479.6 5.8 %copy-start.5 = (f32[128,2048]{1,0:T(8,128)S(1)}, f32[128,2048]{1,0:T(8,128)}, u32[]{:S(2)}) copy-start(f32[128,2048]{1,0:T(8,128)} %get-tuple-element.112) | copy-start | bytes 3145732
